TPU v7x, 128 devices: a whole 4x4x4 slice. The times are simulated.
128 devices in a mesh: tm: 8 (over y, z_hi), sky: 16 (over x, z_lo, core).
Axes of the slice: x: 4, y: 4, z: 4 (z_hi: 2, z_lo: 2; z = z_hi * 2 + z_lo), core: 2. Of those that a mesh axis runs over, the one named last changes fastest.
Arguments:
- residual: float32 [65536, 128], P(('tm', 'sky')), may hold values from -110 to 110
- obs_weight: float32 [65536, 128], P(('tm', 'sky')), may hold values from 0.5 to 2
- source_partials: float32 [5, 65536, 128], P(None, ('tm', 'sky')), may hold values from -1 to 1
- attitude_partials: float32 [16, 65536, 128], P(None, ('tm', 'sky')), may hold values from -1.5 to 1.5
- source_index: int32 [65536, 128], P(('tm', 'sky')), may hold values from 0 to 127
- tile_pixel: int32 [65536], P(('tm', 'sky')), may hold values from 0 to 2047, as said below
- tile_knot: int32 [65536], P(('tm', 'sky')), may hold values from 0 to 4095, as said below
- pixel_slot: int32 [2048], replicated, may hold values from 0 to 2047, as said below
Outputs:
- final_residual: float32 [65536, 128], P(('tm', 'sky'))
- source_update: float32 [5, 262144], P(None, 'sky')
- attitude_update: float32 [4, 4096], P(None, 'tm')
Inputs may be any that keep to these rules, and one draw needn't show every extreme that they name: Tiles come in aligned blocks of 512; with owner = pixel_slot[tile_pixel[t]] // 128, no block holds more than 96 tiles of one owner, and every block holds exactly 96 tiles of some owner. `pixel_slot`: every slot number appears once. `tile_knot`: the tiles of aligned block q of 512 tiles have first knots in [q * 32, (q + 1) * 32).
All inputs are finite; a program needn't handle non-finite values.
Results may differ from a plain program's by a relative error of at most 0.0003.
Values sent between devices are 32-bit elements; how exact they have to be, the bound alone decides.
A program may use at most 128 MiB of HBM per device.

v0:
```python
import jax
import jax.numpy as jnp
from jax import lax
from jax.sharding import PartitionSpec as P

PIX_DEV = 128
SRC_PIX = 128
KNOTS_DEV = 512


SOURCE_PAIRS = tuple(((first, second) for first in range(5) for second in range(first, 5)))
KNOT_PAIRS = tuple(((first, second) for first in range(4) for second in range(first, 4)))


def in_blocks(array, dim, peers):
    shape = array.shape
    blocks = array.reshape(*shape[:dim], peers, shape[dim] // peers, *shape[dim + 1 :])
    return jnp.moveaxis(blocks, dim, 0)


def edges_of(length, count):
    lap = length // count
    if lap >= 8:
        lap -= lap % 8
    return [lap * k for k in range(1, count)]


def joined_along(blocks, dim):
    shape = list(blocks.shape[1:])
    shape[dim] *= blocks.shape[0]
    return jnp.moveaxis(blocks, 0, dim).reshape(shape)


def cut_exchange(array, axis, pieces, split_dim, concat_dim):
    blocks = in_blocks(array, split_dim, lax.axis_size(axis))
    split_at = max(range(1, max(2, blocks.ndim - 1)), key=lambda d: blocks.shape[d])
    done = []
    for piece in jnp.split(blocks, edges_of(blocks.shape[split_at], pieces), axis=split_at):
        if piece.size:
            done.append(lax.all_to_all(piece, axis, split_axis=0, concat_axis=0, tiled=True))
    return joined_along(jnp.concatenate(done, axis=split_at), concat_dim)


def summed_on_arrival(array, axis, dim):
    peers = lax.axis_size(axis)
    blocks = lax.all_to_all(in_blocks(array, dim, peers), axis, 0, 0, tiled=True)
    return jnp.sum(blocks, axis=0)


def from_everyone(array, axis):
    copies = jnp.broadcast_to(array, (lax.axis_size(axis), *array.shape))
    return lax.all_to_all(copies, axis, split_axis=0, concat_axis=0, tiled=True)


def gather_directly(array, axis, dim):
    return joined_along(from_everyone(array, axis), dim)


def passed_along(value, axis, steps):
    count = lax.axis_size(axis)
    first, last = (max(0, -steps), min(count, count - steps))
    return lax.ppermute(value, axis, [(source, source + steps) for source in range(first, last)])


def of_everyone(array, axis):
    return from_everyone(array, axis).sum(axis=0)


def damped_solve(normal, target, order, pairs):
    entries = {}
    for number, couple in enumerate(pairs):
        entries[couple] = normal[number]
    factor = {}
    for column in range(order):
        pivot_value = entries[column, column] + 1.0
        for earlier in range(column):
            pivot_value = pivot_value - factor[column, earlier] * factor[column, earlier]
        pivot_value = jnp.sqrt(pivot_value)
        factor[column, column] = pivot_value
        for below in range(column + 1, order):
            current = entries[column, below]
            for earlier in range(column):
                current = current - factor[below, earlier] * factor[column, earlier]
            factor[below, column] = current / pivot_value
    forward = []
    for column in range(order):
        current = target[column]
        for earlier in range(column):
            current = current - factor[column, earlier] * forward[earlier]
        forward.append(current / factor[column, column])
    answer = [None] * order
    for column in reversed(range(order)):
        current = forward[column]
        for later in range(column + 1, order):
            current = current - factor[later, column] * answer[later]
        answer[column] = current / factor[column, column]
    return jnp.stack(answer)


def source_terms(weights, partials, baseline):
    products = [weights * partials[first] * partials[second] for first, second in SOURCE_PAIRS]
    products = products + [weights * partials[first] * baseline for first in range(5)]
    return products


def knot_terms(weights, partials, baseline):
    result = []
    for segment in range(4):
        portion = partials[4 * segment : 4 * segment + 4]
        sums_rows = [
            jnp.sum(weights * portion[first] * portion[second], axis=-1)
            for first, second in KNOT_PAIRS
        ]
        sums_rows = sums_rows + [
            jnp.sum(weights * portion[first] * baseline, axis=-1) for first in range(4)
        ]
        result.append(jnp.stack(sums_rows))
    return result


def correct(baseline, partials, picked):
    accumulated = partials[0] * picked[0]
    for component in range(1, partials.shape[0]):
        accumulated = accumulated + partials[component] * picked[component]
    return baseline - accumulated


def pixel_sums(products, indices, owners, capacity):

    def add_sender(sender, running):
        offset = sender * capacity
        portion = lax.dynamic_slice_in_dim(products, offset, capacity, 1)
        chosen = lax.dynamic_slice_in_dim(indices, offset, capacity, 0)
        within = ((chosen % SRC_PIX)[:, :, None] == jnp.arange(SRC_PIX, dtype=jnp.int32)).astype(
            jnp.float32
        )
        pixel_hits = (
            (chosen[:, 0] // SRC_PIX)[:, None] == jnp.arange(PIX_DEV, dtype=jnp.int32)
        ).astype(jnp.float32)
        spread = jnp.einsum("ctk,tks->cts", portion, within, precision=lax.Precision.HIGHEST)
        return running + jnp.einsum(
            "cts,tp->cps", spread, pixel_hits, precision=lax.Precision.HIGHEST
        )

    running = lax.fori_loop(0, owners, add_sender, jnp.zeros((20, PIX_DEV, SRC_PIX), jnp.float32))
    return running.reshape(20, PIX_DEV * SRC_PIX)


def pick_sources(update, indices, rows):
    pixels = update.shape[1] // SRC_PIX
    table = update.reshape(update.shape[0], pixels, SRC_PIX)
    blocks = indices.shape[0] // rows

    def fill(number, output):
        offset = number * rows
        chosen = lax.dynamic_slice_in_dim(indices, offset, rows, 0)
        pixel_hits = (
            (chosen[:, 0] // SRC_PIX)[:, None] == jnp.arange(pixels, dtype=jnp.int32)
        ).astype(jnp.float32)
        within = ((chosen % SRC_PIX)[:, :, None] == jnp.arange(SRC_PIX, dtype=jnp.int32)).astype(
            jnp.float32
        )
        row_values = jnp.einsum("tp,cps->cts", pixel_hits, table, precision=lax.Precision.HIGHEST)
        picked = jnp.einsum("cts,tks->ctk", row_values, within, precision=lax.Precision.HIGHEST)
        return lax.dynamic_update_slice_in_dim(output, picked, offset, 1)

    empty = jnp.zeros((update.shape[0], indices.shape[0], indices.shape[1]), jnp.float32)
    return lax.fori_loop(0, blocks, fill, empty)


def body(
    residual,
    obs_weight,
    source_partials,
    attitude_partials,
    source_index,
    tile_pixel,
    tile_knot,
    pixel_slot,
):
    owners = lax.axis_size("sky")
    tiles = residual.shape[0]
    capacity = 3 * tiles // owners
    pixels = pixel_slot.shape[0]
    pixel_match = (tile_pixel[:, None] == jnp.arange(pixels, dtype=jnp.int32)[None, :]).astype(
        jnp.float32
    )
    seats_float = jnp.dot(
        pixel_match, pixel_slot.astype(jnp.float32), precision=lax.Precision.HIGHEST
    )
    seats = seats_float.astype(jnp.int32)
    owner_ids = seats // PIX_DEV
    local_pixel = seats % PIX_DEV
    member = (owner_ids[:, None] == jnp.arange(owners, dtype=jnp.int32)[None, :]).astype(
        jnp.float32
    )
    tile_numbers = jnp.arange(tiles, dtype=jnp.int32)
    lower = (tile_numbers[:, None] > tile_numbers[None, :]).astype(jnp.float32)
    before = jnp.dot(lower, member, precision=lax.Precision.HIGHEST)
    position = jnp.sum(before * member, axis=1).astype(jnp.int32)
    slot_index = owner_ids * capacity + position
    place = (jnp.arange(owners * capacity, dtype=jnp.int32)[:, None] == slot_index[None, :]).astype(
        jnp.float32
    )
    local_source = (local_pixel[:, None] * SRC_PIX + source_index).astype(jnp.float32)
    sent_index = jnp.dot(place, local_source, precision=lax.Precision.HIGHEST).astype(jnp.int32)[
        None
    ]
    fields = jnp.concatenate([residual[None], obs_weight[None], source_partials], axis=0)
    packed = jnp.einsum("st,ctk->csk", place, fields, precision=lax.Precision.HIGHEST)
    arrived, arrived_index = (
        cut_exchange(packed, "sky", 2, 1, 1),
        cut_exchange(sent_index, "sky", 2, 1, 1),
    )
    products = jnp.stack(source_terms(arrived[1], arrived[2:], arrived[0]))
    normals = pixel_sums(products, arrived_index[0], owners, capacity)
    shares = summed_on_arrival(normals, "tm", 1)
    solved = damped_solve(shares[:15], shares[15:], 5, SOURCE_PAIRS)
    source_update = gather_directly(solved, "tm", 1)
    picked = pick_sources(source_update, arrived_index[0], capacity)
    corrected = correct(arrived[0], arrived[2:], picked)
    returned = lax.all_to_all(corrected, "sky", split_axis=0, concat_axis=0, tiled=True)
    settled = jnp.dot(place.T, returned, precision=lax.Precision.HIGHEST)
    knot_start = tile_knot - lax.axis_index("tm") * KNOTS_DEV
    knot_hits = (knot_start[:, None] == jnp.arange(KNOTS_DEV, dtype=jnp.int32)[None, :]).astype(
        jnp.float32
    )
    accumulated = jnp.zeros((14, KNOTS_DEV + 3), jnp.float32)
    for segment, tile_sums in enumerate(knot_terms(obs_weight, attitude_partials, settled)):
        placed = jnp.dot(tile_sums, knot_hits, precision=lax.Precision.HIGHEST)
        accumulated = accumulated + jnp.pad(placed, ((0, 0), (segment, 3 - segment)))
    arriving = passed_along(accumulated[:, KNOTS_DEV:], "tm", 1)
    own_rows = accumulated[:, :KNOTS_DEV] + jnp.pad(arriving, ((0, 0), (0, KNOTS_DEV - 3)))
    whole = of_everyone(own_rows, "sky")
    attitude_update = damped_solve(whole[:10], whole[10:], 4, KNOT_PAIRS)
    following = passed_along(attitude_update[:, :3], "tm", -1)
    extended = jnp.concatenate([attitude_update, following], axis=1)
    accumulated_fix = None
    for segment in range(4):
        window = extended[:, segment : segment + KNOTS_DEV]
        values = jnp.dot(window, knot_hits.T, precision=lax.Precision.HIGHEST)
        for component in range(4):
            addend = attitude_partials[4 * segment + component] * values[component][:, None]
            accumulated_fix = addend if accumulated_fix is None else accumulated_fix + addend
    final_residual = settled - accumulated_fix
    return (final_residual, source_update, attitude_update)


def solution(mesh):
    in_specs = (
        P(("tm", "sky"), None),
        P(("tm", "sky"), None),
        P(None, ("tm", "sky"), None),
        P(None, ("tm", "sky"), None),
        P(("tm", "sky"), None),
        P(("tm", "sky")),
        P(("tm", "sky")),
        P(),
    )
    out_specs = (P(("tm", "sky"), None), P(None, "sky"), P(None, "tm"))
    return jax.shard_map(body, mesh=mesh, in_specs=in_specs, out_specs=out_specs, check_vma=False)
```

profile of v0, /device:TPU:8, one launch (start us, length us, event | category | flops | bytes accessed | tf_op | source)
XLA Modules:
  0.0 544.9 jit_solution(12708216598552357669)
XLA Ops:
  7.9 5.8 %all-to-all-start.2 = ((s32[16,1,48,128]{3,2,1,0:T(8,128)}), s32[16,1,48,128]{3,2,1,0:T(8,128)S(1)}, u32[]{:S(2)}, u32[]{:S(2)}) async-start(s32[16,1,48,128]{3,2,1,0:T(8,128)} %get-tuple-element.475), calls=%async_computation.2 | async-start | bytes 786432 | tf_op jit(solution)/shard_map/all_to_all | solution.py:40
  16.3 6.8 %convolution_bitcast_fusion.2 = f32[7,1536,128]{1,2,0:T(8,128)} fusion(f32[5,512,128]{1,2,0:T(8,128)S(1)} %copy.440, f32[1,512,128]{1,2,0:T(8,128)S(1)} %bitcast.573, f32[1,512,128]{1,2,0:T(8,128)S(1)} %bitcast.575, s32[512]{0:T(512)S(1)} %convert_add_fusion), kind=kOutput, calls=%fused_computation.46 | convolution fusion | flops 8457420800 | bytes 7342080 | tf_op jit(solution)/shard_map/st,ctk->csk/dot_general | solution.py:210
  23.1 6.1 %copy.441 = f32[7,1536,128]{2,1,0:T(8,128)} copy(f32[7,1536,128]{1,2,0:T(8,128)} %convolution_bitcast_fusion.2) | data formatting | bytes 11010048 | tf_op jit(solution)/shard_map/st,ctk->csk/transpose | solution.py:210
  29.2 5.7 %all-to-all-start.3 = ((s32[16,1,48,128]{3,2,1,0:T(8,128)}), s32[16,1,48,128]{3,2,1,0:T(8,128)S(1)}, u32[]{:S(2)}, u32[]{:S(2)}) async-start(s32[16,1,48,128]{3,2,1,0:T(8,128)} %get-tuple-element.476), calls=%async_computation.3 | async-start | bytes 786432 | tf_op jit(solution)/shard_map/all_to_all | solution.py:40
  51.3 31.2 %all-to-all-done = f32[16,7,48,128]{3,2,1,0:T(8,128)S(1)} async-done(((f32[16,7,48,128]{3,2,1,0:T(8,128)}), f32[16,7,48,128]{3,2,1,0:T(8,128)S(1)}, u32[]{:S(2)}, u32[]{:S(2)}) %all-to-all-start) | async-done | bytes 2752544 | tf_op jit(solution)/shard_map/all_to_all | solution.py:40
  84.0 6.8 %all-to-all-start.1 = ((f32[16,7,48,128]{3,2,1,0:T(8,128)}), f32[16,7,48,128]{3,2,1,0:T(8,128)}, u32[]{:S(2)}, u32[]{:S(2)}) async-start(f32[16,7,48,128]{3,2,1,0:T(8,128)} %copy.443), calls=%async_computation.1 | async-start | bytes 5505024 | tf_op jit(solution)/shard_map/all_to_all | solution.py:40
  91.2 34.4 %all-to-all-done.1 = f32[16,7,48,128]{3,2,1,0:T(8,128)} async-done(((f32[16,7,48,128]{3,2,1,0:T(8,128)}), f32[16,7,48,128]{3,2,1,0:T(8,128)}, u32[]{:S(2)}, u32[]{:S(2)}) %all-to-all-start.1) | async-done | bytes 2752544 | tf_op jit(solution)/shard_map/all_to_all | solution.py:40
  134.4 5.5 %copy-done.2 = f32[20,1536,128]{2,1,0:T(8,128)} copy-done((f32[20,1536,128]{2,1,0:T(8,128)}, f32[20,1536,128]{2,1,0:T(8,128)S(1)}, u32[]{:S(2)}) %copy-start.2) | copy-done | bytes 15728664
  139.9 134.8 %while.32 = (s32[]{:T(128)}, f32[20,128,128]{2,1,0:T(8,128)S(1)}, s32[1536,128]{0,1:T(8,128)S(1)}, f32[20,1536,128]{2,1,0:T(8,128)}, s32[]{:T(128)}, /*index=5*/s32[]{:T(128)}, s32[]{:T(128)}, s32[]{:T(128)}) while((s32[]{:T(128)}, f32[20,128,128]{2,1,0:T(8,128)S(1)}, s32[1536,128]{0,1:T(8,128)S(1)}, f32[20,1536,128]{2,1,0:T(8,128)}, ...), condition=%wide.region_2.3_spmd.clone, body=%wide.region_1.2_spmd.clone.sunk | while | flops 757351808 | bytes 7783705 | solution.py:145
  141.4 5.6 %fusion.215 = f32[20,96,128]{2,0,1:T(8,128)S(1)} fusion(s32[96,128]{1,0:T(8,128)S(1)} %copy.538, f32[20,96,128]{2,1,0:T(8,128)S(1)} %constant_dynamic-slice_fusion.4), kind=kOutput, calls=%fused_computation.25.clone.1 | convolution fusion | flops 379060224 | bytes 2015232 | tf_op jit(solution)/shard_map/while/body/eval_jaxpr/ctk,tks->cts/dot_general | solution.py:140
  149.8 5.6 %fusion.215 = f32[20,96,128]{2,0,1:T(8,128)S(1)} fusion(s32[96,128]{1,0:T(8,128)S(1)} %copy.538, f32[20,96,128]{2,1,0:T(8,128)S(1)} %constant_dynamic-slice_fusion.4), kind=kOutput, calls=%fused_computation.25.clone.1 | convolution fusion | flops 379060224 | bytes 2015232 | tf_op jit(solution)/shard_map/while/body/eval_jaxpr/ctk,tks->cts/dot_general | solution.py:140
  158.2 5.6 %fusion.215 = f32[20,96,128]{2,0,1:T(8,128)S(1)} fusion(s32[96,128]{1,0:T(8,128)S(1)} %copy.538, f32[20,96,128]{2,1,0:T(8,128)S(1)} %constant_dynamic-slice_fusion.4), kind=kOutput, calls=%fused_computation.25.clone.1 | convolution fusion | flops 379060224 | bytes 2015232 | tf_op jit(solution)/shard_map/while/body/eval_jaxpr/ctk,tks->cts/dot_general | solution.py:140
  166.7 5.6 %fusion.215 = f32[20,96,128]{2,0,1:T(8,128)S(1)} fusion(s32[96,128]{1,0:T(8,128)S(1)} %copy.538, f32[20,96,128]{2,1,0:T(8,128)S(1)} %constant_dynamic-slice_fusion.4), kind=kOutput, calls=%fused_computation.25.clone.1 | convolution fusion | flops 379060224 | bytes 2015232 | tf_op jit(solution)/shard_map/while/body/eval_jaxpr/ctk,tks->cts/dot_general | solution.py:140
  175.1 5.6 %fusion.215 = f32[20,96,128]{2,0,1:T(8,128)S(1)} fusion(s32[96,128]{1,0:T(8,128)S(1)} %copy.538, f32[20,96,128]{2,1,0:T(8,128)S(1)} %constant_dynamic-slice_fusion.4), kind=kOutput, calls=%fused_computation.25.clone.1 | convolution fusion | flops 379060224 | bytes 2015232 | tf_op jit(solution)/shard_map/while/body/eval_jaxpr/ctk,tks->cts/dot_general | solution.py:140
  183.5 5.6 %fusion.215 = f32[20,96,128]{2,0,1:T(8,128)S(1)} fusion(s32[96,128]{1,0:T(8,128)S(1)} %copy.538, f32[20,96,128]{2,1,0:T(8,128)S(1)} %constant_dynamic-slice_fusion.4), kind=kOutput, calls=%fused_computation.25.clone.1 | convolution fusion | flops 379060224 | bytes 2015232 | tf_op jit(solution)/shard_map/while/body/eval_jaxpr/ctk,tks->cts/dot_general | solution.py:140
  191.9 5.6 %fusion.215 = f32[20,96,128]{2,0,1:T(8,128)S(1)} fusion(s32[96,128]{1,0:T(8,128)S(1)} %copy.538, f32[20,96,128]{2,1,0:T(8,128)S(1)} %constant_dynamic-slice_fusion.4), kind=kOutput, calls=%fused_computation.25.clone.1 | convolution fusion | flops 379060224 | bytes 2015232 | tf_op jit(solution)/shard_map/while/body/eval_jaxpr/ctk,tks->cts/dot_general | solution.py:140
  200.4 5.6 %fusion.215 = f32[20,96,128]{2,0,1:T(8,128)S(1)} fusion(s32[96,128]{1,0:T(8,128)S(1)} %copy.538, f32[20,96,128]{2,1,0:T(8,128)S(1)} %constant_dynamic-slice_fusion.4), kind=kOutput, calls=%fused_computation.25.clone.1 | convolution fusion | flops 379060224 | bytes 2015232 | tf_op jit(solution)/shard_map/while/body/eval_jaxpr/ctk,tks->cts/dot_general | solution.py:140
  208.8 5.6 %fusion.215 = f32[20,96,128]{2,0,1:T(8,128)S(1)} fusion(s32[96,128]{1,0:T(8,128)S(1)} %copy.538, f32[20,96,128]{2,1,0:T(8,128)S(1)} %constant_dynamic-slice_fusion.4), kind=kOutput, calls=%fused_computation.25.clone.1 | convolution fusion | flops 379060224 | bytes 2015232 | tf_op jit(solution)/shard_map/while/body/eval_jaxpr/ctk,tks->cts/dot_general | solution.py:140
  217.2 5.6 %fusion.215 = f32[20,96,128]{2,0,1:T(8,128)S(1)} fusion(s32[96,128]{1,0:T(8,128)S(1)} %copy.538, f32[20,96,128]{2,1,0:T(8,128)S(1)} %constant_dynamic-slice_fusion.4), kind=kOutput, calls=%fused_computation.25.clone.1 | convolution fusion | flops 379060224 | bytes 2015232 | tf_op jit(solution)/shard_map/while/body/eval_jaxpr/ctk,tks->cts/dot_general | solution.py:140
  225.6 5.6 %fusion.215 = f32[20,96,128]{2,0,1:T(8,128)S(1)} fusion(s32[96,128]{1,0:T(8,128)S(1)} %copy.538, f32[20,96,128]{2,1,0:T(8,128)S(1)} %constant_dynamic-slice_fusion.4), kind=kOutput, calls=%fused_computation.25.clone.1 | convolution fusion | flops 379060224 | bytes 2015232 | tf_op jit(solution)/shard_map/while/body/eval_jaxpr/ctk,tks->cts/dot_general | solution.py:140
  234.1 5.6 %fusion.215 = f32[20,96,128]{2,0,1:T(8,128)S(1)} fusion(s32[96,128]{1,0:T(8,128)S(1)} %copy.538, f32[20,96,128]{2,1,0:T(8,128)S(1)} %constant_dynamic-slice_fusion.4), kind=kOutput, calls=%fused_computation.25.clone.1 | convolution fusion | flops 379060224 | bytes 2015232 | tf_op jit(solution)/shard_map/while/body/eval_jaxpr/ctk,tks->cts/dot_general | solution.py:140
  242.5 5.6 %fusion.215 = f32[20,96,128]{2,0,1:T(8,128)S(1)} fusion(s32[96,128]{1,0:T(8,128)S(1)} %copy.538, f32[20,96,128]{2,1,0:T(8,128)S(1)} %constant_dynamic-slice_fusion.4), kind=kOutput, calls=%fused_computation.25.clone.1 | convolution fusion | flops 379060224 | bytes 2015232 | tf_op jit(solution)/shard_map/while/body/eval_jaxpr/ctk,tks->cts/dot_general | solution.py:140
  250.9 5.6 %fusion.215 = f32[20,96,128]{2,0,1:T(8,128)S(1)} fusion(s32[96,128]{1,0:T(8,128)S(1)} %copy.538, f32[20,96,128]{2,1,0:T(8,128)S(1)} %constant_dynamic-slice_fusion.4), kind=kOutput, calls=%fused_computation.25.clone.1 | convolution fusion | flops 379060224 | bytes 2015232 | tf_op jit(solution)/shard_map/while/body/eval_jaxpr/ctk,tks->cts/dot_general | solution.py:140
  259.4 5.6 %fusion.215 = f32[20,96,128]{2,0,1:T(8,128)S(1)} fusion(s32[96,128]{1,0:T(8,128)S(1)} %copy.538, f32[20,96,128]{2,1,0:T(8,128)S(1)} %constant_dynamic-slice_fusion.4), kind=kOutput, calls=%fused_computation.25.clone.1 | convolution fusion | flops 379060224 | bytes 2015232 | tf_op jit(solution)/shard_map/while/body/eval_jaxpr/ctk,tks->cts/dot_general | solution.py:140
  267.8 5.6 %fusion.215 = f32[20,96,128]{2,0,1:T(8,128)S(1)} fusion(s32[96,128]{1,0:T(8,128)S(1)} %copy.538, f32[20,96,128]{2,1,0:T(8,128)S(1)} %constant_dynamic-slice_fusion.4), kind=kOutput, calls=%fused_computation.25.clone.1 | convolution fusion | flops 379060224 | bytes 2015232 | tf_op jit(solution)/shard_map/while/body/eval_jaxpr/ctk,tks->cts/dot_general | solution.py:140
  275.7 28.9 %all_to_all.44 = f32[8,20,2048]{2,1,0:T(8,128)S(1)} all-to-all(f32[8,20,2048]{2,1,0:T(8,128)S(1)} %copy.452), channel_id=1, replica_groups=mesh['tm'=8,'sky'=16] {'tm'}, dimensions={0} | all-to-all | bytes 2621440 | tf_op jit(solution)/shard_map/all_to_all | solution.py:46
  311.6 9.3 %all-to-all-done.5 = f32[8,5,2048]{2,1,0:T(8,128)S(1)} async-done(((f32[8,5,2048]{2,1,0:T(8,128)}), f32[8,5,2048]{2,1,0:T(8,128)S(1)}, u32[]{:S(2)}, u32[]{:S(2)}) %all-to-all-start.5) | async-done | bytes 327712 | tf_op jit(solution)/shard_map/all_to_all | solution.py:52
  324.1 122.2 %while.31 = (s32[]{:T(128)}, f32[5,1536,128]{2,0,1:T(8,128)}, s32[1536,128]{0,1:T(8,128)S(1)}, f32[5,128,128]{2,1,0:T(8,128)S(1)}, s32[]{:T(128)}, /*index=5*/s32[]{:T(128)}, s32[]{:T(128)}, s32[]{:T(128)}) while((s32[]{:T(128)}, f32[5,1536,128]{2,0,1:T(8,128)}, s32[1536,128]{0,1:T(8,128)S(1)}, f32[5,128,128]{2,1,0:T(8,128)S(1)}, s32[]{:T(128)}, ...), condition=%wide.region_5.6_spmd, body=%wide.region_4.5_spmd.sunk | while | flops 190465440 | bytes 1459471 | solution.py:168
  324.7 7.0 %fusion.211 = f32[5,1536,128]{2,0,1:T(8,128)} fusion(f32[5,1536,128]{2,0,1:T(8,128)} %get-tuple-element.583, s32[]{:T(128)S(6)} %select_n.119, s32[96,128]{1,0:T(8,128)S(1)} %copy.535, f32[5,96,128]{2,1,0:T(8,128)S(1)} %convolution_bitcast_fusion.4), kind=kOutput, calls=%fused_computation.4.clone.1 | convolution fusion | flops 95944704 | bytes 688132 | tf_op jit(solution)/shard_map/while/body/eval_jaxpr/cts,tks->ctk/dot_general | solution.py:164
  332.3 7.0 %fusion.211 = f32[5,1536,128]{2,0,1:T(8,128)} fusion(f32[5,1536,128]{2,0,1:T(8,128)} %get-tuple-element.583, s32[]{:T(128)S(6)} %select_n.119, s32[96,128]{1,0:T(8,128)S(1)} %copy.535, f32[5,96,128]{2,1,0:T(8,128)S(1)} %convolution_bitcast_fusion.4), kind=kOutput, calls=%fused_computation.4.clone.1 | convolution fusion | flops 95944704 | bytes 688132 | tf_op jit(solution)/shard_map/while/body/eval_jaxpr/cts,tks->ctk/dot_general | solution.py:164
  339.9 7.0 %fusion.211 = f32[5,1536,128]{2,0,1:T(8,128)} fusion(f32[5,1536,128]{2,0,1:T(8,128)} %get-tuple-element.583, s32[]{:T(128)S(6)} %select_n.119, s32[96,128]{1,0:T(8,128)S(1)} %copy.535, f32[5,96,128]{2,1,0:T(8,128)S(1)} %convolution_bitcast_fusion.4), kind=kOutput, calls=%fused_computation.4.clone.1 | convolution fusion | flops 95944704 | bytes 688132 | tf_op jit(solution)/shard_map/while/body/eval_jaxpr/cts,tks->ctk/dot_general | solution.py:164
  347.6 7.0 %fusion.211 = f32[5,1536,128]{2,0,1:T(8,128)} fusion(f32[5,1536,128]{2,0,1:T(8,128)} %get-tuple-element.583, s32[]{:T(128)S(6)} %select_n.119, s32[96,128]{1,0:T(8,128)S(1)} %copy.535, f32[5,96,128]{2,1,0:T(8,128)S(1)} %convolution_bitcast_fusion.4), kind=kOutput, calls=%fused_computation.4.clone.1 | convolution fusion | flops 95944704 | bytes 688132 | tf_op jit(solution)/shard_map/while/body/eval_jaxpr/cts,tks->ctk/dot_general | solution.py:164
  355.2 7.0 %fusion.211 = f32[5,1536,128]{2,0,1:T(8,128)} fusion(f32[5,1536,128]{2,0,1:T(8,128)} %get-tuple-element.583, s32[]{:T(128)S(6)} %select_n.119, s32[96,128]{1,0:T(8,128)S(1)} %copy.535, f32[5,96,128]{2,1,0:T(8,128)S(1)} %convolution_bitcast_fusion.4), kind=kOutput, calls=%fused_computation.4.clone.1 | convolution fusion | flops 95944704 | bytes 688132 | tf_op jit(solution)/shard_map/while/body/eval_jaxpr/cts,tks->ctk/dot_general | solution.py:164
  362.8 7.0 %fusion.211 = f32[5,1536,128]{2,0,1:T(8,128)} fusion(f32[5,1536,128]{2,0,1:T(8,128)} %get-tuple-element.583, s32[]{:T(128)S(6)} %select_n.119, s32[96,128]{1,0:T(8,128)S(1)} %copy.535, f32[5,96,128]{2,1,0:T(8,128)S(1)} %convolution_bitcast_fusion.4), kind=kOutput, calls=%fused_computation.4.clone.1 | convolution fusion | flops 95944704 | bytes 688132 | tf_op jit(solution)/shard_map/while/body/eval_jaxpr/cts,tks->ctk/dot_general | solution.py:164
  370.5 7.0 %fusion.211 = f32[5,1536,128]{2,0,1:T(8,128)} fusion(f32[5,1536,128]{2,0,1:T(8,128)} %get-tuple-element.583, s32[]{:T(128)S(6)} %select_n.119, s32[96,128]{1,0:T(8,128)S(1)} %copy.535, f32[5,96,128]{2,1,0:T(8,128)S(1)} %convolution_bitcast_fusion.4), kind=kOutput, calls=%fused_computation.4.clone.1 | convolution fusion | flops 95944704 | bytes 688132 | tf_op jit(solution)/shard_map/while/body/eval_jaxpr/cts,tks->ctk/dot_general | solution.py:164
  378.1 7.0 %fusion.211 = f32[5,1536,128]{2,0,1:T(8,128)} fusion(f32[5,1536,128]{2,0,1:T(8,128)} %get-tuple-element.583, s32[]{:T(128)S(6)} %select_n.119, s32[96,128]{1,0:T(8,128)S(1)} %copy.535, f32[5,96,128]{2,1,0:T(8,128)S(1)} %convolution_bitcast_fusion.4), kind=kOutput, calls=%fused_computation.4.clone.1 | convolution fusion | flops 95944704 | bytes 688132 | tf_op jit(solution)/shard_map/while/body/eval_jaxpr/cts,tks->ctk/dot_general | solution.py:164
  385.8 7.0 %fusion.211 = f32[5,1536,128]{2,0,1:T(8,128)} fusion(f32[5,1536,128]{2,0,1:T(8,128)} %get-tuple-element.583, s32[]{:T(128)S(6)} %select_n.119, s32[96,128]{1,0:T(8,128)S(1)} %copy.535, f32[5,96,128]{2,1,0:T(8,128)S(1)} %convolution_bitcast_fusion.4), kind=kOutput, calls=%fused_computation.4.clone.1 | convolution fusion | flops 95944704 | bytes 688132 | tf_op jit(solution)/shard_map/while/body/eval_jaxpr/cts,tks->ctk/dot_general | solution.py:164
  393.4 7.0 %fusion.211 = f32[5,1536,128]{2,0,1:T(8,128)} fusion(f32[5,1536,128]{2,0,1:T(8,128)} %get-tuple-element.583, s32[]{:T(128)S(6)} %select_n.119, s32[96,128]{1,0:T(8,128)S(1)} %copy.535, f32[5,96,128]{2,1,0:T(8,128)S(1)} %convolution_bitcast_fusion.4), kind=kOutput, calls=%fused_computation.4.clone.1 | convolution fusion | flops 95944704 | bytes 688132 | tf_op jit(solution)/shard_map/while/body/eval_jaxpr/cts,tks->ctk/dot_general | solution.py:164
  401.0 7.0 %fusion.211 = f32[5,1536,128]{2,0,1:T(8,128)} fusion(f32[5,1536,128]{2,0,1:T(8,128)} %get-tuple-element.583, s32[]{:T(128)S(6)} %select_n.119, s32[96,128]{1,0:T(8,128)S(1)} %copy.535, f32[5,96,128]{2,1,0:T(8,128)S(1)} %convolution_bitcast_fusion.4), kind=kOutput, calls=%fused_computation.4.clone.1 | convolution fusion | flops 95944704 | bytes 688132 | tf_op jit(solution)/shard_map/while/body/eval_jaxpr/cts,tks->ctk/dot_general | solution.py:164
  408.7 7.0 %fusion.211 = f32[5,1536,128]{2,0,1:T(8,128)} fusion(f32[5,1536,128]{2,0,1:T(8,128)} %get-tuple-element.583, s32[]{:T(128)S(6)} %select_n.119, s32[96,128]{1,0:T(8,128)S(1)} %copy.535, f32[5,96,128]{2,1,0:T(8,128)S(1)} %convolution_bitcast_fusion.4), kind=kOutput, calls=%fused_computation.4.clone.1 | convolution fusion | flops 95944704 | bytes 688132 | tf_op jit(solution)/shard_map/while/body/eval_jaxpr/cts,tks->ctk/dot_general | solution.py:164
  416.3 7.0 %fusion.211 = f32[5,1536,128]{2,0,1:T(8,128)} fusion(f32[5,1536,128]{2,0,1:T(8,128)} %get-tuple-element.583, s32[]{:T(128)S(6)} %select_n.119, s32[96,128]{1,0:T(8,128)S(1)} %copy.535, f32[5,96,128]{2,1,0:T(8,128)S(1)} %convolution_bitcast_fusion.4), kind=kOutput, calls=%fused_computation.4.clone.1 | convolution fusion | flops 95944704 | bytes 688132 | tf_op jit(solution)/shard_map/while/body/eval_jaxpr/cts,tks->ctk/dot_general | solution.py:164
  423.9 7.0 %fusion.211 = f32[5,1536,128]{2,0,1:T(8,128)} fusion(f32[5,1536,128]{2,0,1:T(8,128)} %get-tuple-element.583, s32[]{:T(128)S(6)} %select_n.119, s32[96,128]{1,0:T(8,128)S(1)} %copy.535, f32[5,96,128]{2,1,0:T(8,128)S(1)} %convolution_bitcast_fusion.4), kind=kOutput, calls=%fused_computation.4.clone.1 | convolution fusion | flops 95944704 | bytes 688132 | tf_op jit(solution)/shard_map/while/body/eval_jaxpr/cts,tks->ctk/dot_general | solution.py:164
  431.6 7.0 %fusion.211 = f32[5,1536,128]{2,0,1:T(8,128)} fusion(f32[5,1536,128]{2,0,1:T(8,128)} %get-tuple-element.583, s32[]{:T(128)S(6)} %select_n.119, s32[96,128]{1,0:T(8,128)S(1)} %copy.535, f32[5,96,128]{2,1,0:T(8,128)S(1)} %convolution_bitcast_fusion.4), kind=kOutput, calls=%fused_computation.4.clone.1 | convolution fusion | flops 95944704 | bytes 688132 | tf_op jit(solution)/shard_map/while/body/eval_jaxpr/cts,tks->ctk/dot_general | solution.py:164
  439.2 7.0 %fusion.211 = f32[5,1536,128]{2,0,1:T(8,128)} fusion(f32[5,1536,128]{2,0,1:T(8,128)} %get-tuple-element.583, s32[]{:T(128)S(6)} %select_n.119, s32[96,128]{1,0:T(8,128)S(1)} %copy.535, f32[5,96,128]{2,1,0:T(8,128)S(1)} %convolution_bitcast_fusion.4), kind=kOutput, calls=%fused_computation.4.clone.1 | convolution fusion | flops 95944704 | bytes 688132 | tf_op jit(solution)/shard_map/while/body/eval_jaxpr/cts,tks->ctk/dot_general | solution.py:164
  446.3 14.1 %fusion.179 = (f32[1,1536,128]{2,0,1:T(1,128)S(1)}, f32[1,1536,128]{2,0,1:T(1,128)S(1)}, f32[1,1536,128]{2,0,1:T(1,128)S(1)}, f32[1,1536,128]{2,0,1:T(1,128)S(1)}, f32[1,1536,128]{2,0,1:T(1,128)S(1)}) fusion(f32[5,1536,128]{2,0,1:T(8,128)} %get-tuple-element.230), kind=kLoop, calls=%fused_computation.396 | loop fusion | bytes 7864320 | tf_op jit(solution)/shard_map/slice | solution.py:122
  464.6 6.5 %all-to-all-start.6 = ((f32[16,96,128]{2,1,0:T(8,128)}), f32[16,96,128]{2,1,0:T(8,128)}, u32[]{:S(2)}, u32[]{:S(2)}) async-start(f32[16,96,128]{2,1,0:T(8,128)} %fusion.46), calls=%async_computation.6 | async-start | bytes 1572864 | tf_op jit(solution)/shard_map/all_to_all | solution.py:222
  514.7 5.7 %all-to-all-start.7 = ((f32[16,14,512]{2,1,0:T(8,128)}), f32[16,14,512]{2,1,0:T(8,128)S(1)}, u32[]{:S(2)}, u32[]{:S(2)}) async-start(f32[16,14,512]{2,1,0:T(8,128)} %broadcast_in_dim.58), calls=%async_computation.7 | async-start | bytes 1048576 | tf_op jit(solution)/shard_map/all_to_all | solution.py:52
  520.4 10.8 %all-to-all-done.7 = f32[16,14,512]{2,1,0:T(8,128)S(1)} async-done(((f32[16,14,512]{2,1,0:T(8,128)}), f32[16,14,512]{2,1,0:T(8,128)S(1)}, u32[]{:S(2)}, u32[]{:S(2)}) %all-to-all-start.7) | async-done | bytes 458784 | tf_op jit(solution)/shard_map/all_to_all | solution.py:52
  (279 shorter events, 162.7 us)
Async XLA Ops:
  0.6 14.2 %copy-start.3 = (f32[5,512,128]{2,1,0:T(8,128)S(1)}, f32[5,512,128]{2,1,0:T(8,128)}, u32[]{:S(2)}) copy-start(f32[5,512,128]{2,1,0:T(8,128)} %param.14) | copy-start | bytes 3932164
  7.9 21.3 %all-to-all-start.2 = ((s32[16,1,48,128]{3,2,1,0:T(8,128)}), s32[16,1,48,128]{3,2,1,0:T(8,128)S(1)}, u32[]{:S(2)}, u32[]{:S(2)}) async-start(s32[16,1,48,128]{3,2,1,0:T(8,128)} %get-tuple-element.475), calls=%async_computation.2 | async-start | bytes 786432 | tf_op jit(solution)/shard_map/all_to_all | solution.py:40
  14.8 14.4 %copy-start.4 = (f32[512,128]{0,1:T(8,128)}, f32[512,128]{0,1:T(8,128)S(1)}, u32[]{:S(2)}) copy-start(f32[512,128]{0,1:T(8,128)S(1)} %copy.439) | copy-start | bytes 786436
  29.2 14.8 %all-to-all-start.3 = ((s32[16,1,48,128]{3,2,1,0:T(8,128)}), s32[16,1,48,128]{3,2,1,0:T(8,128)S(1)}, u32[]{:S(2)}, u32[]{:S(2)}) async-start(s32[16,1,48,128]{3,2,1,0:T(8,128)} %get-tuple-element.476), calls=%async_computation.3 | async-start | bytes 786432 | tf_op jit(solution)/shard_map/all_to_all | solution.py:40
  44.0 38.5 %all-to-all-start = ((f32[16,7,48,128]{3,2,1,0:T(8,128)}), f32[16,7,48,128]{3,2,1,0:T(8,128)S(1)}, u32[]{:S(2)}, u32[]{:S(2)}) async-start(f32[16,7,48,128]{3,2,1,0:T(8,128)} %copy.442), calls=%async_computation | async-start | bytes 5505024 | tf_op jit(solution)/shard_map/all_to_all | solution.py:40
  82.5 1.5 copy-start.1
  84.0 41.6 %all-to-all-start.1 = ((f32[16,7,48,128]{3,2,1,0:T(8,128)}), f32[16,7,48,128]{3,2,1,0:T(8,128)}, u32[]{:S(2)}, u32[]{:S(2)}) async-start(f32[16,7,48,128]{3,2,1,0:T(8,128)} %copy.443), calls=%async_computation.1 | async-start | bytes 5505024 | tf_op jit(solution)/shard_map/all_to_all | solution.py:40
  128.8 2.3 copy-start
  134.4 5.5 %copy-start.2 = (f32[20,1536,128]{2,1,0:T(8,128)}, f32[20,1536,128]{2,1,0:T(8,128)S(1)}, u32[]{:S(2)}) copy-start(f32[20,1536,128]{2,1,0:T(8,128)S(1)} %constant_dynamic-update-slice_fusion) | copy-start | bytes 47185924
  306.3 14.7 %all-to-all-start.5 = ((f32[8,5,2048]{2,1,0:T(8,128)}), f32[8,5,2048]{2,1,0:T(8,128)S(1)}, u32[]{:S(2)}, u32[]{:S(2)}) async-start(f32[8,5,2048]{2,1,0:T(8,128)} %broadcast_in_dim.57), calls=%async_computation.5 | async-start | bytes 1048576 | tf_op jit(solution)/shard_map/all_to_all | solution.py:52
  464.6 24.7 %all-to-all-start.6 = ((f32[16,96,128]{2,1,0:T(8,128)}), f32[16,96,128]{2,1,0:T(8,128)}, u32[]{:S(2)}, u32[]{:S(2)}) async-start(f32[16,96,128]{2,1,0:T(8,128)} %fusion.46), calls=%async_computation.6 | async-start | bytes 1572864 | tf_op jit(solution)/shard_map/all_to_all | solution.py:222
  474.5 13.2 %copy-start.10 = (s32[512]{0:T(512)S(1)}, s32[512]{0:T(512)}, u32[]{:S(2)}) copy-start(s32[512]{0:T(512)} %param.18) | copy-start | bytes 6148
  474.5 13.8 %copy-start.5 = (f32[512,128]{0,1:T(8,128)S(1)}, f32[512,128]{0,1:T(8,128)}, u32[]{:S(2)}) copy-start(f32[512,128]{0,1:T(8,128)} %copy-done.4) | copy-start | bytes 786436
  476.9 17.6 %copy-start.6 = (f32[1,512,128]{1,2,0:T(8,128)}, f32[1,512,128]{1,2,0:T(8,128)S(1)}, u32[]{:S(2)}) copy-start(f32[1,512,128]{1,2,0:T(8,128)S(1)} %copy.499) | copy-start | bytes 786436
  489.3 5.9 %copy-start.8 = (f32[512,128]{0,1:T(8,128)S(1)}, f32[512,128]{0,1:T(8,128)}, u32[]{:S(2)}) copy-start(f32[512,128]{0,1:T(8,128)} %get-tuple-element.477) | copy-start | bytes 786436
  494.5 0.7 copy-start.7
  494.5 37.0 %copy-start.11 = (s32[512]{0:T(512)S(1)}, s32[512]{0:T(512)}, u32[]{:S(2)}) copy-start(s32[512]{0:T(512)} %broadcast_subtract_fusion) | copy-start | bytes 6148
  505.9 7.9 %collective-permute-start = (f32[14,3]{1,0:T(8,128)S(1)}, f32[14,3]{1,0:T(8,128)S(1)}, u32[]{:S(2)}, u32[]{:S(2)}) collective-permute-start(f32[14,3]{1,0:T(8,128)S(1)} %pad_add_fusion.2), channel_id=1, source_target_pairs={{0,16},{16,32},{32,48},{48,64},{64,80},{80,96},{96,112},{1,17},{17... | collective-permute-start | bytes 512 | tf_op jit(solution)/shard_map/ppermute | solution.py:62
  514.7 16.5 %all-to-all-start.7 = ((f32[16,14,512]{2,1,0:T(8,128)}), f32[16,14,512]{2,1,0:T(8,128)S(1)}, u32[]{:S(2)}, u32[]{:S(2)}) async-start(f32[16,14,512]{2,1,0:T(8,128)} %broadcast_in_dim.58), calls=%async_computation.7 | async-start | bytes 1048576 | tf_op jit(solution)/shard_map/all_to_all | solution.py:52
  531.5 13.4 %copy-start.9 = (f32[4,512]{1,0:T(4,128)}, f32[4,512]{1,0:T(4,128)S(1)}, u32[]{:S(2)}) copy-start(f32[4,512]{1,0:T(4,128)S(1)} %pad_maximum_fusion.2) | copy-start | bytes 24580
  532.1 7.0 %collective-permute-start.1 = (f32[4,3]{1,0:T(4,128)S(1)}, f32[4,3]{1,0:T(4,128)S(1)}, u32[]{:S(2)}, u32[]{:S(2)}) collective-permute-start(f32[4,3]{1,0:T(4,128)S(1)} %slice.608), channel_id=1, source_target_pairs={{16,0},{32,16},{48,32},{64,48},{80,64},{96,80},{112,96},{17,1},{33... | collective-permute-start | bytes 152 | tf_op jit(solution)/shard_map/ppermute | solution.py:62
where the time goes:
time: 547 us; the launch traced here: 545 us
  matrix products  251 us (46%)
  local copies, waits for them, and re-layouts  98.3 us (18%)
  waiting for transfers between devices  95.4 us (17%)
  starting transfers between devices  47.5 us (9%)
  blocking collectives  28.9 us (5%)
  other arithmetic  20.7 us (4%)
    dot_general x16, matrix products, fill(): jnp.einsum('cts,tks->ctk', row_values, within, precision=lax.Precision.HI...  113 us
    dot_general x16, matrix products, add_sender(): jnp.einsum('ctk,tks->cts', portion, within, precision=lax.Precision.HIGHEST)  89.3 us
    all_to_all x4, waiting for transfers between devices, cut_exchange(): lax.all_to_all(piece, axis, split_axis=0, concat_axis=0, tiled=True)  68.4 us
    all_to_all x1, blocking collectives, summed_on_arrival(): lax.all_to_all(in_blocks(array, dim, peers), axis, 0, 0, tiled=True)  28.9 us
    unnamed x64, local copies, waits for them, and re-layouts  28.4 us
    all_to_all x4, starting transfers between devices, cut_exchange(): lax.all_to_all(piece, axis, split_axis=0, concat_axis=0, tiled=True)  22 us
    dynamic_slice x16, local copies, waits for them, and re-layouts, add_sender(): portion = lax.dynamic_slice_in_dim(products, offset, capacity, 1)  20.5 us
    all_to_all x2, waiting for transfers between devices, from_everyone(): return lax.all_to_all(copies, axis, split_axis=0, concat_axis=0, tiled=True)  20.1 us
  transfers between devices with their start and end apart: 9, of which 7 were waited for; matrix products, arithmetic and copies ran while one was open for 8% of the time, Pallas kernels for 0%

commit v1 on v0

v1 whole, which is shorter than its diff:
```python
import jax
import jax.numpy as jnp
from jax import lax
from jax.experimental import pallas as pl
from jax.experimental.pallas import tpu as pltpu
from jax.sharding import PartitionSpec as P

TILES = 512
OWNERS = 16
TIMES = 8
CAP = 96
PIX = 128
SRC = 128
FIELDS = 7
BLOCK_ROWS = CAP * FIELDS + 8
SPAN = 32
TERMS = 20
PART_ROWS = (PIX // TIMES) * TERMS
KNOT_PAIRS = tuple((c, e) for c in range(4) for e in range(c, 4))
TERM_ROW = {
    (0, 0): 0, (1, 1): 1, (2, 2): 2, (3, 3): 3, (4, 4): 4, (0, 5): 5,
    (0, 1): 6, (1, 2): 7, (2, 3): 8, (3, 4): 9, (4, 5): 10, (0, 4): 11, (1, 5): 12,
    (0, 2): 13, (1, 3): 14, (2, 4): 15, (3, 5): 16, (0, 3): 17, (1, 4): 18, (2, 5): 19,
}
VMEM = pl.BlockSpec(memory_space=pltpu.VMEM)
SMEM = pl.BlockSpec(memory_space=pltpu.SMEM)
F32 = jnp.float32
BF16 = jnp.bfloat16


def params(**kw):
    return pltpu.CompilerParams(vmem_limit_bytes=60 * 1024 * 1024, **kw)


def pack_kernel(pixel_ref, slot_ref, res_ref, w_ref, part_ref, idx_ref,
                out_ref, where_ref, pix_ref, count_ref, stage_ref):
    def clear(i, _):
        for o in range(OWNERS):
            pix_ref[o, i] = PIX
        return 0

    lax.fori_loop(0, 128, clear, 0)
    for o in range(OWNERS):
        count_ref[o] = 0

    def scale(g, _):
        rows = pl.ds(pl.multiple_of(g * 8, 8), 8)
        root = jnp.sqrt(w_ref[rows, :])
        for a in range(5):
            stage_ref[a, rows, :] = part_ref[a, rows, :] * root
        stage_ref[5, rows, :] = res_ref[rows, :] * root
        stage_ref[6, rows, :] = idx_ref[rows, :].astype(F32)
        return 0

    lax.fori_loop(0, TILES // 8, scale, 0, unroll=4)

    def place(g, _):
        for j in range(8):
            t = g * 8 + j
            seat = slot_ref[pixel_ref[t]]
            owner = lax.shift_right_logical(seat, 7)
            position = count_ref[owner]
            count_ref[owner] = position + 1
            where_ref[t] = owner * CAP + position
            pix_ref[owner, position] = lax.bitwise_and(seat, 127)
            base = owner * BLOCK_ROWS + position * FIELDS
            for f in range(FIELDS):
                out_ref[pl.ds(base + f, 1), :] = stage_ref[f, pl.ds(t, 1), :]
        return 0

    lax.fori_loop(0, TILES // 8, place, 0)
    for o in range(OWNERS):
        pix_ref[o, 127] = count_ref[o]


def pack(tile_pixel, pixel_slot, residual, weight, partials, index):
    return pl.pallas_call(
        pack_kernel,
        out_shape=(
            jax.ShapeDtypeStruct((OWNERS * BLOCK_ROWS, 128), F32),
            jax.ShapeDtypeStruct((TILES,), jnp.int32),
            jax.ShapeDtypeStruct((OWNERS, 128), jnp.int32),
        ),
        in_specs=[SMEM, SMEM, VMEM, VMEM, VMEM, VMEM],
        out_specs=(VMEM, SMEM, SMEM),
        scratch_shapes=[pltpu.SMEM((OWNERS,), jnp.int32), pltpu.VMEM((FIELDS, TILES, 128), F32)],
        compiler_params=params(),
        name="pack",
    )(tile_pixel, pixel_slot, residual, weight, partials, index)


def pair_products(v, row):
    low5, low4 = row < 5, row < 4
    one = pltpu.roll(v, 1, 0)
    first = jnp.where(low5, v, pltpu.roll(v, 5, 0))
    second = jnp.where(low5, pltpu.roll(v, 7, 0), one)
    third = jnp.where(low4, v, pltpu.roll(v, 4, 0))
    fourth = jnp.where(low4, pltpu.roll(v, 6, 0), one)
    return jnp.concatenate([first * v, first * second, third * fourth], axis=0)


def tile_sums(v, row, sources):
    products = pair_products(v, row)
    high = products.astype(BF16).astype(F32)
    left = jnp.concatenate([high, products - high], axis=0).astype(BF16)
    hits = (v[6:7, :].astype(BF16) == sources).astype(BF16)
    out = lax.dot_general(left, hits, (((1,), (1,)), ((), ())), preferred_element_type=F32)
    return out[:24] + out[24:]


def normals_kernel(pix_ref, in_ref, out_ref, acc_ref):
    zero = jnp.zeros((24, 128), F32)

    def clear(p, _):
        acc_ref[p] = zero
        return 0

    lax.fori_loop(0, PIX + 1, clear, 0, unroll=8)
    row = lax.broadcasted_iota(jnp.int32, (8, 128), 0)
    sources = lax.broadcasted_iota(jnp.int32, (128, 128), 0).astype(F32).astype(BF16)

    def sender(b, _):
        count = pix_ref[b, 127]

        def group(g, _):
            sums = []
            for j in range(8):
                start = b * BLOCK_ROWS + (g * 8 + j) * FIELDS
                sums.append(tile_sums(in_ref[pl.ds(start, 8), :], row, sources))
            for j in range(8):
                p = pix_ref[b, g * 8 + j]
                acc_ref[p] = acc_ref[p] + sums[j]
            return 0

        lax.fori_loop(0, lax.shift_right_logical(count + 7, 3), group, 0)
        return 0

    lax.fori_loop(0, OWNERS, sender, 0)

    def write(p, _):
        base = p * TERMS
        out_ref[pl.ds(base, 8), :] = acc_ref[p, 0:8]
        out_ref[pl.ds(base + 6, 8), :] = acc_ref[p, 8:16]
        out_ref[pl.ds(base + 13, 7), :] = acc_ref[p, 16:23]
        return 0

    lax.fori_loop(0, PIX, write, 0, unroll=4)


def normals_of(pix, arrived):
    return pl.pallas_call(
        normals_kernel,
        out_shape=jax.ShapeDtypeStruct((PIX * TERMS, 128), F32),
        in_specs=[SMEM, VMEM],
        out_specs=VMEM,
        scratch_shapes=[pltpu.VMEM((PIX + 1, 24, 128), F32)],
        compiler_params=params(),
        name="normals",
    )(pix, arrived)


def damped_solve(entries, target, order):
    factor = {}
    for column in range(order):
        pivot = entries[column, column] + 1.0
        for earlier in range(column):
            pivot = pivot - factor[column, earlier] * factor[column, earlier]
        pivot = jnp.sqrt(pivot)
        factor[column, column] = pivot
        for below in range(column + 1, order):
            current = entries[column, below]
            for earlier in range(column):
                current = current - factor[below, earlier] * factor[column, earlier]
            factor[below, column] = current / pivot
    forward = []
    for column in range(order):
        current = target[column]
        for earlier in range(column):
            current = current - factor[column, earlier] * forward[earlier]
        forward.append(current / factor[column, column])
    answer = [None] * order
    for column in reversed(range(order)):
        current = forward[column]
        for later in range(column + 1, order):
            current = current - factor[later, column] * answer[later]
        answer[column] = current / factor[column, column]
    return answer


def solve_kernel(in_ref, out_ref):
    count = PIX // TIMES
    sums = []
    for term in range(TERMS):
        total = in_ref[0, pl.ds(term, count, stride=TERMS), :]
        for part in range(1, TIMES):
            total = total + in_ref[part, pl.ds(term, count, stride=TERMS), :]
        sums.append(total)
    entries = {key: sums[at] for key, at in TERM_ROW.items() if key[1] < 5}
    target = [sums[TERM_ROW[a, 5]] for a in range(5)]
    for a, value in enumerate(damped_solve(entries, target, 5)):
        out_ref[pl.ds(a, count, stride=5), :] = value


def solve(parts):
    return pl.pallas_call(
        solve_kernel,
        out_shape=jax.ShapeDtypeStruct((5 * PIX // TIMES, 128), F32),
        in_specs=[VMEM],
        out_specs=VMEM,
        compiler_params=params(),
        name="solve",
    )(parts)


def pick_kernel(pix_ref, in_ref, table_ref, out_ref, update_ref, rows_ref):
    row = lax.broadcasted_iota(jnp.int32, (8, 128), 0)

    def spread(p, _):
        rows_ref[p] = jnp.where(row < 5, table_ref[pl.ds(p * 5, 8), :], -1.0)
        return 0

    lax.fori_loop(0, PIX - 1, spread, 0, unroll=4)
    rows_ref[PIX - 1] = jnp.where(
        row < 5, pltpu.roll(table_ref[pl.ds(PIX * 5 - 8, 8), :], 5, 0), -1.0)
    for p in range(PIX):
        update_ref[:, p * 128:(p + 1) * 128] = rows_ref[p, 0:5]

    def sender(b, _):
        count = pix_ref[b, 127]

        def group(g, _):
            for j in range(8):
                start = b * BLOCK_ROWS + (g * 8 + j) * FIELDS
                v = in_ref[pl.ds(start, 8), :]
                table = rows_ref[jnp.minimum(pix_ref[b, g * 8 + j], PIX - 1)]
                at = jnp.broadcast_to(jnp.clip(v[6:7, :].astype(jnp.int32), 0, 127), (8, 128))
                picked = jnp.take_along_axis(table, at, axis=1)
                terms = jnp.where(row < 6, v * picked, 0.0)
                out_ref[b, pl.ds(g * 8 + j, 1), :] = -jnp.sum(terms, axis=0, keepdims=True)
            return 0

        lax.fori_loop(0, lax.shift_right_logical(count + 7, 3), group, 0)
        return 0

    lax.fori_loop(0, OWNERS, sender, 0)


def pick(pix, arrived, table):
    return pl.pallas_call(
        pick_kernel,
        out_shape=(
            jax.ShapeDtypeStruct((OWNERS, CAP, 128), F32),
            jax.ShapeDtypeStruct((5, PIX * SRC), F32),
        ),
        in_specs=[SMEM, VMEM, VMEM],
        out_specs=(VMEM, VMEM),
        scratch_shapes=[pltpu.VMEM((PIX, 8, 128), F32)],
        compiler_params=params(),
        name="pick",
    )(pix, arrived, table)


def knot_hits(knot_row, first):
    lane = lax.broadcasted_iota(jnp.int32, (SPAN, TILES), 0)
    return (lane == knot_row - first).astype(F32)


def split_dot(hits, value):
    high = value.astype(BF16)
    low = (value - high.astype(F32)).astype(BF16)
    return (jnp.dot(hits, high, preferred_element_type=F32)
            + jnp.dot(hits, low, preferred_element_type=F32))


def quad_kernel(knot_ref, first_ref, w_ref, att_ref, out_ref, hits_ref):
    hits = knot_hits(knot_ref[...], first_ref[0])
    flipped = hits.T
    hits_ref[...] = jnp.concatenate([flipped] * 3 + [jnp.zeros_like(flipped)], axis=1).astype(BF16)
    hits = hits.astype(BF16)
    lane = lax.broadcasted_iota(jnp.int32, (SPAN, 128), 1)
    total = jnp.zeros((SPAN, 128), F32)
    weight = w_ref[...]
    for m in range(4):
        for c in range(4):
            scaled = weight * att_ref[4 * m + c]
            for e in range(c, 4):
                sums = split_dot(hits, scaled * att_ref[4 * m + e])
                at = 14 * m + KNOT_PAIRS.index((c, e))
                total = total + jnp.where(lane == at, jnp.sum(sums, axis=1, keepdims=True), 0.0)
    out_ref[...] = total


def quads(knots, first, weight, attitude):
    return pl.pallas_call(
        quad_kernel,
        out_shape=(jax.ShapeDtypeStruct((SPAN, 128), F32), jax.ShapeDtypeStruct((TILES, 128), BF16)),
        in_specs=[VMEM, SMEM, VMEM, VMEM],
        out_specs=(VMEM, VMEM),
        compiler_params=params(),
        name="quads",
    )(knots, first, weight, attitude)


def linear_kernel(where_ref, knot_ref, first_ref, back_ref, w_ref, att_ref, quad_ref,
                  settled_ref, sums_ref, halo_ref):
    def fetch(g, _):
        for j in range(8):
            t = g * 8 + j
            settled_ref[pl.ds(t, 1), :] = back_ref[pl.ds(where_ref[t], 1), :]
        return 0

    lax.fori_loop(0, TILES // 8, fetch, 0)
    weight = w_ref[...]
    root = jnp.sqrt(weight)
    settled = settled_ref[...] / root
    settled_ref[...] = settled
    hits = knot_hits(knot_ref[...], first_ref[0]).astype(BF16)
    lane = lax.broadcasted_iota(jnp.int32, (SPAN, 128), 1)
    total = quad_ref[...]
    scaled = weight * settled
    for m in range(4):
        for c in range(4):
            sums = split_dot(hits, scaled * att_ref[4 * m + c])
            at = 14 * m + 10 + c
            total = total + jnp.where(lane == at, jnp.sum(sums, axis=1, keepdims=True), 0.0)
    lane40 = lax.broadcasted_iota(jnp.int32, (SPAN + 8, 128), 1)
    padded = jnp.concatenate([total, jnp.zeros((8, 128), F32)], axis=0)
    moved = jnp.where(lane40 < 14, padded, 0.0)
    for m in range(1, 4):
        shifted = pltpu.roll(pltpu.roll(padded, m, 0), 128 - 14 * m, 1)
        moved = moved + jnp.where(lane40 < 14, shifted, 0.0)
    sums_ref[...] = moved[:SPAN]
    halo_ref[...] = moved[SPAN:]


def linear(where, knots, first, back, weight, attitude, quad):
    return pl.pallas_call(
        linear_kernel,
        out_shape=(
            jax.ShapeDtypeStruct((TILES, 128), F32),
            jax.ShapeDtypeStruct((SPAN, 128), F32),
            jax.ShapeDtypeStruct((8, 128), F32),
        ),
        in_specs=[SMEM, VMEM, SMEM, VMEM, VMEM, VMEM, VMEM],
        out_specs=(VMEM, VMEM, VMEM),
        compiler_params=params(),
        name="linear",
    )(where, knots, first, back, weight, attitude, quad)


def knot_solve_kernel(sums_ref, halo_ref, out_ref, head_ref):
    sums = sums_ref[...]
    sums = jnp.concatenate([sums[:8] + halo_ref[...], sums[8:]], axis=0)

    def column(at):
        return jnp.broadcast_to(sums[:, at:at + 1], (SPAN, 128))

    entries = {pair: column(n) for n, pair in enumerate(KNOT_PAIRS)}
    answer = damped_solve(entries, [column(10 + c) for c in range(4)], 4)
    for c in range(4):
        out_ref[c] = answer[c]
        head_ref[c] = answer[c][:8]


def knot_solve(sums, halo):
    return pl.pallas_call(
        knot_solve_kernel,
        out_shape=(jax.ShapeDtypeStruct((4, SPAN, 128), F32), jax.ShapeDtypeStruct((4, 8, 128), F32)),
        in_specs=[VMEM, VMEM],
        out_specs=(VMEM, VMEM),
        compiler_params=params(),
        name="knot_solve",
    )(sums, halo)


def final_kernel(hits_ref, settled_ref, att_ref, own_ref, next_ref, out_ref):
    hits = hits_ref[...]
    total = None
    for m in range(4):
        for c in range(4):
            both = jnp.concatenate([own_ref[c], next_ref[c]], axis=0)
            value = both[m:m + SPAN]
            high = value.astype(BF16)
            rest = value - high.astype(F32)
            middle = rest.astype(BF16)
            low = (rest - middle.astype(F32)).astype(BF16)
            table = jnp.concatenate([high, middle, low, jnp.zeros_like(high)], axis=0)
            term = att_ref[4 * m + c] * jnp.dot(hits, table, preferred_element_type=F32)
            total = term if total is None else total + term
    out_ref[...] = settled_ref[...] - total


def finish(hits, settled, attitude, own, following):
    return pl.pallas_call(
        final_kernel,
        out_shape=jax.ShapeDtypeStruct((TILES, 128), F32),
        in_specs=[VMEM] * 5,
        out_specs=VMEM,
        compiler_params=params(),
        name="finish",
    )(hits, settled, attitude, own, following)


def body(residual, obs_weight, source_partials, attitude_partials, source_index,
         tile_pixel, tile_knot, pixel_slot):
    both = ("tm", "sky")
    block = lax.axis_index("tm") * OWNERS + lax.axis_index("sky")
    first = (block * SPAN).reshape(1)
    knots = tile_knot.reshape(1, TILES)
    packed, where, pix = pack(tile_pixel, pixel_slot, residual, obs_weight, source_partials, source_index)
    arrived = lax.all_to_all(packed.reshape(OWNERS, BLOCK_ROWS, 128), "sky", 0, 0, tiled=True)
    pix = lax.all_to_all(pix, "sky", 0, 0, tiled=True)
    arrived = arrived.reshape(OWNERS * BLOCK_ROWS, 128)
    quad, hits = quads(knots, first, obs_weight, attitude_partials)
    normals = normals_of(pix, arrived)
    parts = lax.all_to_all(normals.reshape(TIMES, PART_ROWS, 128), "tm", 0, 0, tiled=True)
    solved = solve(parts)
    table = lax.all_gather(solved, "tm", axis=0, tiled=True)
    corrected, source_update = pick(pix, arrived, table)
    back = lax.all_to_all(corrected, "sky", 0, 0, tiled=True).reshape(OWNERS * CAP, 128)
    settled, sums, halo = linear(where, knots, first, back, obs_weight, attitude_partials, quad)
    last = TIMES * OWNERS - 1
    halo = lax.ppermute(halo, both, [(q, q + 1) for q in range(last)])
    own, head = knot_solve(sums, halo)
    following = lax.ppermute(head, both, [(q + 1, q) for q in range(last)])
    final = finish(hits, settled, attitude_partials, own, following)
    attitude_update = lax.all_gather(own[:, :, 0], "sky", axis=1, tiled=True)
    return final, source_update, attitude_update


def solution(mesh):
    in_specs = (
        P(("tm", "sky"), None),
        P(("tm", "sky"), None),
        P(None, ("tm", "sky"), None),
        P(None, ("tm", "sky"), None),
        P(("tm", "sky"), None),
        P(("tm", "sky")),
        P(("tm", "sky")),
        P(),
    )
    out_specs = (P(("tm", "sky"), None), P(None, "sky"), P(None, "tm"))
    return jax.shard_map(body, mesh=mesh, in_specs=in_specs, out_specs=out_specs, check_vma=False)
```

time: 547 us -> 298 us (0.54)
  matrix products: 251 us -> 0 us
  blocking collectives: 28.9 us -> 163 us
  local copies, waits for them, and re-layouts: 98.3 us -> 2.08 us
  waiting for transfers between devices: 95.4 us -> 15.4 us
  Pallas kernels: 0 us -> 62.2 us
  other arithmetic: 20.7 us -> 0.95 us
  starting transfers between devices: 47.5 us -> 53.2 us
    dot_general x77 -> x0, matrix products: 251 us -> none  [the longest x16 113 us: fill(): jnp.einsum('cts,tks->ctk', row_values, within, precision=lax.Precision.HI...]
    all_to_all x7 -> x1, waiting for transfers between devices: 88.5 us -> 7.99 us  [body(): lax.all_to_all(corrected, 'sky', 0, 0, tiled=True)]
    all_to_all x1 -> x3, blocking collectives: 28.9 us -> 107 us  [the longest x1 69.1 us: body(): lax.all_to_all(packed.reshape(OWNERS, BLOCK_ROWS, 128), 'sky', 0, 0, tile...]
    pallas_call x0 -> x8, Pallas kernels: none -> 62.2 us  [the longest x1 23.9 us: normals_of(): pl.pallas_call(normals_kernel, out_shape=jax.ShapeDtypeStruct((PIX * TERM...]
    all_gather x0 -> x2, blocking collectives: none -> 55.9 us  [the longest x1 36 us: body(): table = lax.all_gather(solved, 'tm', axis=0, tiled=True)]
    unnamed x64 -> x6, local copies, waits for them, and re-layouts: 28.4 us -> 2.08 us
    dynamic_slice x16 -> x0, local copies, waits for them, and re-layouts: 20.5 us -> none  [add_sender(): portion = lax.dynamic_slice_in_dim(products, offset, capacity, 1)]
    slice x8 -> x0, local copies, waits for them, and re-layouts: 18.1 us -> none  [the longest x1 14.1 us: correct(): accumulated = partials[0] * picked[0]]
  transfers between devices with their start and end apart: 9 -> 3, of which waited for: 7 -> 2; matrix products, arithmetic and copies ran while one was open for 8% -> 0% of each run, Pallas kernels for 0% -> 2%
where the time goes in v1:
time: 298 us
  blocking collectives  163 us (55%)
  Pallas kernels  62.2 us (21%)
  starting transfers between devices  53.2 us (18%)
  waiting for transfers between devices  15.4 us (5%)
    all_to_all x1, blocking collectives, body(): lax.all_to_all(packed.reshape(OWNERS, BLOCK_ROWS, 128), 'sky', 0, 0, tile...  69.1 us
    all_to_all x1, starting transfers between devices, body(): lax.all_to_all(corrected, 'sky', 0, 0, tiled=True)  49.4 us
    all_gather x1, blocking collectives, body(): table = lax.all_gather(solved, 'tm', axis=0, tiled=True)  36 us
    all_to_all x1, blocking collectives, body(): lax.all_to_all(normals.reshape(TIMES, PART_ROWS, 128), 'tm', 0, 0, tiled=...  26.2 us
    pallas_call x1, Pallas kernels, normals_of(): pl.pallas_call(normals_kernel, out_shape=jax.ShapeDtypeStruct((PIX * TERM...  23.9 us
    all_gather x1, blocking collectives, body(): attitude_update = lax.all_gather(own[:, :, 0], 'sky', axis=1, tiled=True)  19.9 us
    all_to_all x1, blocking collectives, body(): pix = lax.all_to_all(pix, 'sky', 0, 0, tiled=True)  11.9 us
    pallas_call x1, Pallas kernels, pick(): pl.pallas_call(pick_kernel, out_shape=(jax.ShapeDtypeStruct((OWNERS, CAP,...  10.7 us
  transfers between devices with their start and end apart: 3, of which 2 were waited for; matrix products, arithmetic and copies ran while one was open for 0% of the time, Pallas kernels for 2%

profile of v1, /device:TPU:8, one launch (start us, length us, event | category | flops | bytes accessed | tf_op | source)
XLA Modules:
  0.0 297.6 jit_solution(5106764343788830674)
XLA Ops:
  0.6 9.8 %pack.1 = (f32[10880,128]{1,0:T(8,128)}, s32[512]{0:T(512)}, s32[16,128]{1,0:T(8,128)}) custom-call(s32[512]{0:T(512)} %pixel_ref.1, s32[2048]{0:T(1024)} %slot_ref.1, f32[512,128]{1,0:T(8,128)} %res_ref.1, f32[512,128]{1,0:T(8,128)} %w_ref.5, f32[5,512,128]{2,1,0:T(8,128)} %part_ref.1, s32[512,128]{1,0:T(8,128)} %idx_ref.1), custom_call_target="tpu_custom_call" | custom-call | tf_op jit(solution)/shard_map/pack/pallas_call | solution.py:77
  10.5 11.9 %all_to_all.26 = s32[16,1,128]{2,1,0:T(1,128)} all-to-all(s32[16,1,128]{2,1,0:T(1,128)} %bitcast.21), channel_id=1, replica_groups=mesh['tm'=8,'sky'=16] {'sky'}, dimensions={0} | all-to-all | bytes 16384 | tf_op jit(solution)/shard_map/all_to_all | solution.py:412
  22.4 69.1 %all_to_all.27 = f32[16,680,128]{2,1,0:T(8,128)} all-to-all(f32[16,680,128]{2,1,0:T(8,128)} %bitcast.13), channel_id=1, replica_groups=mesh['tm'=8,'sky'=16] {'sky'}, dimensions={0} | all-to-all | bytes 11141120 | tf_op jit(solution)/shard_map/all_to_all | solution.py:411
  91.5 23.9 %normals.1 = f32[2560,128]{1,0:T(8,128)} custom-call(s32[16,128]{1,0:T(8,128)} %bitcast.17, f32[10880,128]{1,0:T(8,128)} %bitcast.11), custom_call_target="tpu_custom_call" | custom-call | tf_op jit(solution)/shard_map/normals/pallas_call | solution.py:151
  115.3 26.2 %all_to_all.28.in_ref = f32[8,320,128]{2,1,0:T(8,128)} all-to-all(f32[8,320,128]{2,1,0:T(8,128)} %bitcast.14), channel_id=1, replica_groups=mesh['tm'=8,'sky'=16] {'tm'}, dimensions={0} | all-to-all | bytes 2621440 | tf_op jit(solution)/shard_map/all_to_all | solution.py:416
  141.5 2.1 solve.1
  143.6 36.0 %all_gather.6.table_ref = f32[640,128]{1,0:T(8,128)} all-gather(f32[80,128]{1,0:T(8,128)} %solve.1), channel_id=1, replica_groups=mesh['tm'=8,'sky'=16] {'tm'}, dimensions={0}, use_global_device_ids=true | all-gather | bytes 368640 | tf_op jit(solution)/shard_map/all_gather | solution.py:418
  179.6 10.7 %pick.1 = (f32[16,96,128]{2,1,0:T(8,128)}, f32[5,16384]{1,0:T(8,128)}) custom-call(s32[16,128]{1,0:T(8,128)} %bitcast.18, f32[10880,128]{1,0:T(8,128)} %bitcast.12, f32[640,128]{1,0:T(8,128)} %all_gather.6.table_ref), custom_call_target="tpu_custom_call" | custom-call | tf_op jit(solution)/shard_map/pick/pallas_call | solution.py:249
  190.2 49.4 %all-to-all-start.3 = ((f32[16,96,128]{2,1,0:T(8,128)}), f32[16,96,128]{2,1,0:T(8,128)S(1)}, u32[]{:S(2)}, u32[]{:S(2)}) async-start(f32[16,96,128]{2,1,0:T(8,128)} %get-tuple-element.19), calls=%async_computation.3 | async-start | bytes 1572864 | tf_op jit(solution)/shard_map/all_to_all | solution.py:420
  239.7 5.6 %quads.1 = (f32[32,128]{1,0:T(8,128)}, bf16[512,128]{1,0:T(8,128)(2,1)}) custom-call(s32[1,512]{1,0:T(1,128)} %bitcast.19, s32[1]{0:T(128)} %bitcast.1.first_ref, f32[512,128]{1,0:T(8,128)} %w_ref.5, f32[16,512,128]{2,1,0:T(8,128)} %att_ref.5), custom_call_target="tpu_custom_call" | custom-call | tf_op jit(solution)/shard_map/quads/pallas_call | solution.py:294
  245.3 8.0 %all-to-all-done.3 = f32[16,96,128]{2,1,0:T(8,128)S(1)} async-done(((f32[16,96,128]{2,1,0:T(8,128)}), f32[16,96,128]{2,1,0:T(8,128)S(1)}, u32[]{:S(2)}, u32[]{:S(2)}) %all-to-all-start.3) | async-done | bytes 786464 | tf_op jit(solution)/shard_map/all_to_all | solution.py:420
  253.3 0.0 copy-start
  253.3 0.9 copy-done
  254.2 4.8 %linear.1 = (f32[512,128]{1,0:T(8,128)}, f32[32,128]{1,0:T(8,128)}, f32[8,128]{1,0:T(8,128)}) custom-call(s32[512]{0:T(512)} %get-tuple-element.16.where_ref, s32[1,512]{1,0:T(1,128)} %bitcast.20, s32[1]{0:T(128)} %bitcast.1.first_ref, f32[1536,128]{1,0:T(8,128)} %bitcast.15, f32[512,128]{1,0:T(8,128)} %w_ref.5, f32[16,512,128]{2,1,0:T(8,128)} %att_ref.5, ...), custom_call_target="tpu_custom_call" | custom-call | tf_op jit(solution)/shard_map/linear/pallas_call | solution.py:337
  259.0 1.9 collective-permute-start
  260.9 7.4 %collective-permute-done.halo_ref = f32[8,128]{1,0:T(8,128)S(1)} collective-permute-done((f32[8,128]{1,0:T(8,128)}, f32[8,128]{1,0:T(8,128)S(1)}, u32[]{:S(2)}, u32[]{:S(2)}) %collective-permute-start) | collective-permute-done | bytes 4128 | tf_op jit(solution)/shard_map/ppermute | solution.py:423
  268.3 0.0 copy-start.2
  268.4 0.6 copy-done.2
  268.9 1.5 knot_solve.1
  270.4 1.9 collective-permute-start.1
  272.4 19.9 %all-gather = f32[4,512,1]{2,1,0:T(8,128)S(1)} all-gather(f32[4,32,1]{2,1,0:T(8,128)} %bitcast.16), channel_id=2, replica_groups=mesh['tm'=8,'sky'=16] {'sky'}, dimensions={1}, use_global_device_ids=true | all-gather | bytes 8704 | tf_op jit(solution)/shard_map/all_gather | solution.py:427
  292.3 1.0 reduce
  293.2 0.0 collective-permute-done.1.next_ref
  293.2 0.0 copy-start.1
  293.2 0.6 copy-done.1
  293.8 3.8 %finish.1 = f32[512,128]{1,0:T(8,128)} custom-call(bf16[512,128]{1,0:T(8,128)(2,1)} %get-tuple-element.15.hits_ref, f32[512,128]{1,0:T(8,128)} %get-tuple-element.21.settled_ref, f32[16,512,128]{2,1,0:T(8,128)} %att_ref.5, f32[4,32,128]{2,1,0:T(8,128)} %get-tuple-element.24.own_ref, f32[4,8,128]{2,1,0:T(8,128)} %copy-done.1), custom_call_target="tpu_custom_call" | custom-call | tf_op jit(solution)/shard_map/finish/pallas_call | solution.py:394
Async XLA Ops:
  190.2 63.1 %all-to-all-start.3 = ((f32[16,96,128]{2,1,0:T(8,128)}), f32[16,96,128]{2,1,0:T(8,128)S(1)}, u32[]{:S(2)}, u32[]{:S(2)}) async-start(f32[16,96,128]{2,1,0:T(8,128)} %get-tuple-element.19), calls=%async_computation.3 | async-start | bytes 1572864 | tf_op jit(solution)/shard_map/all_to_all | solution.py:420
  253.3 0.9 copy-start
  259.0 9.3 %collective-permute-start = (f32[8,128]{1,0:T(8,128)}, f32[8,128]{1,0:T(8,128)S(1)}, u32[]{:S(2)}, u32[]{:S(2)}) collective-permute-start(f32[8,128]{1,0:T(8,128)} %get-tuple-element.23), channel_id=1, source_target_pairs={{0,1},{1,2},{2,3},{3,4},{4,5},{5,6},{6,7},{7,8},{8,9},{9,10},{10,1... | collective-permute-start | bytes 12296 | tf_op jit(solution)/shard_map/ppermute | solution.py:423
  268.3 0.6 copy-start.2
  270.4 22.8 %collective-permute-start.1 = (f32[4,8,128]{2,1,0:T(8,128)}, f32[4,8,128]{2,1,0:T(8,128)S(1)}, u32[]{:S(2)}, u32[]{:S(2)}) collective-permute-start(f32[4,8,128]{2,1,0:T(8,128)} %get-tuple-element.25), channel_id=1, source_target_pairs={{1,0},{2,1},{3,2},{4,3},{5,4},{6,5},{7,6},{8,7},{9,8},{10,9},{11,1... | collective-permute-start | bytes 49160 | tf_op jit(solution)/shard_map/ppermute | solution.py:425
  293.2 0.6 copy-start.1

commit v2 on v1

v2 whole, which is shorter than its diff:
```python
import jax
import jax.numpy as jnp
from jax import lax
from jax.experimental import pallas as pl
from jax.experimental.pallas import tpu as pltpu
from jax.sharding import PartitionSpec as P

TILES = 512
OWNERS = 16
TIMES = 8
CAP = 96
PIX = 128
SRC = 128
FIELDS = 7
CLASSES = 4
SEATS = CAP // CLASSES
SLOTS = OWNERS * CLASSES
BLOCK_ROWS = SEATS * FIELDS
ROWS_IN = SLOTS * BLOCK_ROWS + 8
SPAN = 32
TERMS = 20
QUARTER = PIX // 4
HALF = PIX // TIMES
QROWS = QUARTER * TERMS
HROWS = HALF * TERMS
KNOT_PAIRS = tuple((c, e) for c in range(4) for e in range(c, 4))
TERM_ROW = {
    (0, 0): 0, (1, 1): 1, (2, 2): 2, (3, 3): 3, (4, 4): 4, (0, 5): 5,
    (0, 1): 6, (1, 2): 7, (2, 3): 8, (3, 4): 9, (4, 5): 10, (0, 4): 11, (1, 5): 12,
    (0, 2): 13, (1, 3): 14, (2, 4): 15, (3, 5): 16, (0, 3): 17, (1, 4): 18, (2, 5): 19,
}
VMEM = pl.BlockSpec(memory_space=pltpu.VMEM)
SMEM = pl.BlockSpec(memory_space=pltpu.SMEM)
F32 = jnp.float32
BF16 = jnp.bfloat16


def params(**kw):
    return pltpu.CompilerParams(vmem_limit_bytes=60 * 1024 * 1024, **kw)


def pack_kernel(pixel_ref, slot_ref, res_ref, w_ref, part_ref, idx_ref,
                out_ref, where_ref, pix_ref, count_ref, stage_ref):
    def clear(i, _):
        for b in range(SLOTS):
            pix_ref[b, i] = PIX
        return 0

    lax.fori_loop(0, SEATS, clear, 0)
    for o in range(OWNERS):
        count_ref[o] = 0

    def scale(g, _):
        rows = pl.ds(pl.multiple_of(g * 8, 8), 8)
        root = jnp.sqrt(w_ref[rows, :])
        for a in range(5):
            stage_ref[a, rows, :] = part_ref[a, rows, :] * root
        stage_ref[5, rows, :] = res_ref[rows, :] * root
        stage_ref[6, rows, :] = idx_ref[rows, :].astype(F32)
        return 0

    lax.fori_loop(0, TILES // 8, scale, 0, unroll=4)

    def place(g, _):
        for j in range(8):
            t = g * 8 + j
            seat = slot_ref[pixel_ref[t]]
            owner = lax.shift_right_logical(seat, 7)
            rank = count_ref[owner]
            count_ref[owner] = rank + 1
            plan = lax.bitwise_and(rank, 1)
            half = lax.bitwise_and(lax.shift_right_logical(rank, 1), 1)
            position = lax.shift_right_logical(rank, 2)
            block = plan * (2 * OWNERS) + owner * 2 + half
            where_ref[t] = block * SEATS + position
            pix_ref[block, position] = lax.bitwise_and(seat, 127)
            base = block * BLOCK_ROWS + position * FIELDS
            for f in range(FIELDS):
                out_ref[pl.ds(base + f, 1), :] = stage_ref[f, pl.ds(t, 1), :]
        return 0

    lax.fori_loop(0, TILES // 8, place, 0)
    for o in range(OWNERS):
        for plan in range(2):
            for half in range(2):
                left = count_ref[o] + (3 - plan - 2 * half)
                pix_ref[plan * 2 * OWNERS + o * 2 + half, 127] = lax.shift_right_logical(left, 2)


def pack(tile_pixel, pixel_slot, residual, weight, partials, index):
    return pl.pallas_call(
        pack_kernel,
        out_shape=(
            jax.ShapeDtypeStruct((ROWS_IN, 128), F32),
            jax.ShapeDtypeStruct((TILES,), jnp.int32),
            jax.ShapeDtypeStruct((SLOTS, 128), jnp.int32),
        ),
        in_specs=[SMEM, SMEM, VMEM, VMEM, VMEM, VMEM],
        out_specs=(VMEM, SMEM, SMEM),
        scratch_shapes=[pltpu.SMEM((OWNERS,), jnp.int32), pltpu.VMEM((FIELDS, TILES, 128), F32)],
        compiler_params=params(),
        name="pack",
    )(tile_pixel, pixel_slot, residual, weight, partials, index)


def place_of():
    tm, sky = lax.axis_index("tm"), lax.axis_index("sky")
    return tm // 2, tm % 2, sky // 4, (sky // 2) % 2, sky % 2


def device_of(y, zh, x, zl, c):
    return (y * 2 + zh, x * 4 + zl * 2 + c)


def send(src, dst, sent, landed, device):
    copy = pltpu.make_async_remote_copy(
        src_ref=src, dst_ref=dst, send_sem=sent, recv_sem=landed,
        device_id=device, device_id_type=pl.DeviceIdType.MESH)
    copy.start()
    return copy


def greet(devices):
    barrier = pltpu.get_barrier_semaphore()
    for device in devices:
        pl.semaphore_signal(barrier, inc=1, device_id=device, device_id_type=pl.DeviceIdType.MESH)
    pl.semaphore_wait(barrier, len(devices))


MOVES = [(plan, d, dz, dc, h) for d in (2, 1, 3, 0) for dz in (1, 0) for plan in range(2)
         for dc in (1, 0) for h in range(2)]


def exchange_kernel(sizes, *refs):
    n = len(sizes)
    srcs, dsts = refs[:n], refs[n:2 * n]
    bounces = refs[2 * n:3 * n]
    sent, landed, local = refs[3 * n:]
    y, zh, x, zl, c = place_of()
    mine = (x * 4 + zl * 2 + c, y * 4 + zl * 2 + c)
    routes = []
    for plan, d, dz, dc, h in MOVES:
        far = ((y if plan else x) + d) % 4
        zl_to, c_to, zh_to = (zl + dz) % 2, (c + dc) % 2, (zh + dz * h) % 2
        owner = far * 4 + zl_to * 2 + c_to
        to = device_of(far, zh_to, x, zl_to, c_to) if plan else device_of(y, zh_to, far, zl_to, c_to)
        routes.append((plan * 32 + owner * 2 + h, plan * 32 + mine[plan] * 2 + h, to,
                       d == 0 and dz == 0 and dc == 0))
    greet([to for _, _, to, own in routes if not own])
    copies = []
    for k, (block, slot, to, own) in enumerate(routes):
        if not own:
            for i, size in enumerate(sizes):
                copies.append(send(srcs[i].at[pl.ds(block * size, size)], dsts[i].at[pl.ds(slot * size, size)],
                                   sent.at[i, k], landed.at[i, k], to))
    kept = [(block, at) for at, (block, slot, to, own) in enumerate(r for r in routes if r[3])]
    for way in range(2):
        moves = []
        for block, at in kept:
            for i, size in enumerate(sizes):
                ends = (srcs[i].at[pl.ds(block * size, size)], bounces[i].at[pl.ds(at * size, size)])
                if way:
                    ends = (ends[1], dsts[i].at[pl.ds(block * size, size)])
                move = pltpu.make_async_copy(ends[0], ends[1], local.at[i, at])
                move.start()
                moves.append(move)
        for move in moves:
            move.wait()
    for copy in copies:
        copy.wait()


def exchange(arrays, sizes, number):
    n = len(arrays)
    return pl.pallas_call(
        lambda *refs: exchange_kernel(sizes, *refs),
        out_shape=tuple(jax.ShapeDtypeStruct(a.shape, a.dtype) for a in arrays),
        in_specs=[pl.BlockSpec(memory_space=pltpu.HBM)] * n,
        out_specs=tuple(pl.BlockSpec(memory_space=pltpu.HBM) for _ in arrays),
        scratch_shapes=[pltpu.VMEM((4 * size, 128), a.dtype) for a, size in zip(arrays, sizes)] + [
            pltpu.SemaphoreType.DMA((n, len(MOVES))),
            pltpu.SemaphoreType.DMA((n, len(MOVES))),
            pltpu.SemaphoreType.DMA((n, 4)),
        ],
        compiler_params=params(collective_id=number, has_side_effects=True),
        name="exchange" + str(number),
    )(*arrays)


def pair_products(v, row):
    low5, low4 = row < 5, row < 4
    one = pltpu.roll(v, 1, 0)
    first = jnp.where(low5, v, pltpu.roll(v, 5, 0))
    second = jnp.where(low5, pltpu.roll(v, 7, 0), one)
    third = jnp.where(low4, v, pltpu.roll(v, 4, 0))
    fourth = jnp.where(low4, pltpu.roll(v, 6, 0), one)
    return jnp.concatenate([first * v, first * second, third * fourth], axis=0)


def tile_sums(v, row, sources):
    products = pair_products(v, row)
    high = products.astype(BF16).astype(F32)
    left = jnp.concatenate([high, products - high], axis=0).astype(BF16)
    hits = (v[6:7, :].astype(BF16) == sources).astype(BF16)
    out = lax.dot_general(left, hits, (((1,), (1,)), ((), ())), preferred_element_type=F32)
    return out[:24] + out[24:]


def normals_kernel(pix_ref, in_ref, out_ref, acc_ref):
    zero = jnp.zeros((24, 128), F32)

    def clear(p, _):
        acc_ref[p] = zero
        return 0

    lax.fori_loop(0, 2 * (PIX + 1), clear, 0, unroll=6)
    row = lax.broadcasted_iota(jnp.int32, (8, 128), 0)
    sources = lax.broadcasted_iota(jnp.int32, (128, 128), 0).astype(F32).astype(BF16)

    def sender(b, _):
        count = pix_ref[b, 127]
        offset = lax.shift_right_logical(b, 5) * (PIX + 1)

        def group(g, _):
            sums = []
            for j in range(8):
                start = b * BLOCK_ROWS + (g * 8 + j) * FIELDS
                sums.append(tile_sums(in_ref[pl.ds(start, 8), :], row, sources))
            for j in range(8):
                p = offset + pix_ref[b, g * 8 + j]
                acc_ref[p] = acc_ref[p] + sums[j]
            return 0

        lax.fori_loop(0, lax.shift_right_logical(count + 7, 3), group, 0)
        return 0

    lax.fori_loop(0, SLOTS, sender, 0)

    for plan in range(2):
        def write(p, _):
            base = p * TERMS
            at = plan * (PIX + 1) + p
            out_ref[plan, pl.ds(base, 8), :] = acc_ref[at, 0:8]
            out_ref[plan, pl.ds(base + 6, 8), :] = acc_ref[at, 8:16]
            out_ref[plan, pl.ds(base + 13, 7), :] = acc_ref[at, 16:23]
            return 0

        lax.fori_loop(0, PIX, write, 0, unroll=4)


def normals_of(pix, arrived):
    return pl.pallas_call(
        normals_kernel,
        out_shape=jax.ShapeDtypeStruct((2, PIX * TERMS, 128), F32),
        in_specs=[SMEM, VMEM],
        out_specs=VMEM,
        scratch_shapes=[pltpu.VMEM((2 * (PIX + 1), 24, 128), F32)],
        compiler_params=params(),
        name="normals",
    )(pix, arrived)


def damped_solve(entries, target, order):
    factor = {}
    for column in range(order):
        pivot = entries[column, column] + 1.0
        for earlier in range(column):
            pivot = pivot - factor[column, earlier] * factor[column, earlier]
        pivot = jnp.sqrt(pivot)
        factor[column, column] = pivot
        for below in range(column + 1, order):
            current = entries[column, below]
            for earlier in range(column):
                current = current - factor[below, earlier] * factor[column, earlier]
            factor[below, column] = current / pivot
    forward = []
    for column in range(order):
        current = target[column]
        for earlier in range(column):
            current = current - factor[column, earlier] * forward[earlier]
        forward.append(current / factor[column, column])
    answer = [None] * order
    for column in reversed(range(order)):
        current = forward[column]
        for later in range(column + 1, order):
            current = current - factor[later, column] * answer[later]
        answer[column] = current / factor[column, column]
    return answer


def add_rows(out, base, refs, rows):
    def step(g, _):
        at = pl.multiple_of(g * 16, 16)
        total = None
        for ref, start in refs:
            value = ref[pl.ds(start + at, 16), :]
            total = value if total is None else total + value
        out[pl.ds(base + at, 16), :] = total
        return 0

    lax.fori_loop(0, rows // 16, step, 0)


def reduce_kernel(in_ref, table_ref, first_ref, sum_ref, other_ref, whole_ref, own_ref,
                  sent1, landed1, sent2, landed2, sent3, landed3):
    y, zh, x, zl, c = place_of()
    tm = y * 2 + zh
    diagonal = x == y
    greet([device_of((y + dy) % 4, (zh + dz) % 2, (x + dx) % 4, zl, c)
           for dx in range(4) for dy in range(4) for dz in range(2) if (dx, dy, dz) != (0, 0, 0)])
    copies = []
    for d in (2, 1, 3):
        for plan in range(2):
            far = ((x if plan else y) + d) % 4
            to = device_of(y, zh, far, zl, c) if plan else device_of(far, zh, x, zl, c)
            copies.append(send(in_ref.at[plan, pl.ds(far * QROWS, QROWS)], first_ref.at[plan, d - 1],
                               sent1.at[plan, d - 1], landed1.at[plan, d - 1], to))
    for copy in copies:
        copy.wait()
    for plan in range(2):
        near = (x if plan else y) * QROWS
        add_rows(sum_ref.at[plan], 0,
                 [(in_ref.at[plan], near)] + [(first_ref.at[plan, d], 0) for d in range(3)], QROWS)

    @pl.when(diagonal)
    def _():
        add_rows(sum_ref.at[0], 0, [(sum_ref.at[0], 0), (sum_ref.at[1], 0)], QROWS)

    across = send(sum_ref.at[0, pl.ds((1 - zh) * HROWS, HROWS)], other_ref.at[2], sent2.at[2], landed2.at[2],
                  device_of(y, 1 - zh, x, zl, c))

    @pl.when(diagonal)
    def _():
        def clear(g, _):
            other_ref[0, pl.ds(pl.multiple_of(g * 16, 16), 16), :] = jnp.zeros((16, 128), F32)
            other_ref[1, pl.ds(pl.multiple_of(g * 16, 16), 16), :] = jnp.zeros((16, 128), F32)
            return 0

        lax.fori_loop(0, HROWS // 16, clear, 0)

    @pl.when(jnp.logical_not(diagonal))
    def _():
        flips = [send(sum_ref.at[1, pl.ds(z * HROWS, HROWS)], other_ref.at[zh], sent2.at[z], landed2.at[zh],
                      device_of(x, z, y, zl, c)) for z in range(2)]
        for z, flip in enumerate(flips):
            flip.wait_send()
            pltpu.make_async_remote_copy(
                src_ref=sum_ref.at[1, pl.ds(z * HROWS, HROWS)], dst_ref=other_ref.at[z],
                send_sem=sent2.at[z], recv_sem=landed2.at[z], device_id=device_of(x, z, y, zl, c),
                device_id_type=pl.DeviceIdType.MESH).wait_recv()

    across.wait()
    add_rows(whole_ref, 0, [(sum_ref.at[0], zh * HROWS)] + [(other_ref.at[i], 0) for i in range(3)], HROWS)
    sums = [whole_ref[pl.ds(term, HALF, stride=TERMS), :] for term in range(TERMS)]
    entries = {key: sums[at] for key, at in TERM_ROW.items() if key[1] < 5}
    target = [sums[TERM_ROW[a, 5]] for a in range(5)]
    for a, value in enumerate(damped_solve(entries, target, 5)):
        own_ref[pl.ds(a, HALF, stride=5), :] = value
    part = pl.ds(tm * HALF * 5, HALF * 5)
    copies = []
    for d in (2, 1, 3, 0):
        for z in (1, 0):
            if (d, z) != (0, 0):
                copies.append(send(own_ref, table_ref.at[0, part], sent3.at[0, d * 2 + z], landed3.at[0, d * 2 + z],
                                   device_of((y + d) % 4, (zh + z) % 2, x, zl, c)))
    table_ref[0, part, :] = own_ref[...]

    def spread(d, z):
        return pltpu.make_async_remote_copy(
            src_ref=own_ref, dst_ref=table_ref.at[1, part], send_sem=sent3.at[1, d * 2 + z],
            recv_sem=landed3.at[1, tm], device_id=device_of(x, (zh + z) % 2, (x + d) % 4, zl, c),
            device_id_type=pl.DeviceIdType.MESH)

    for d in (2, 1, 3, 0):
        for z in (1, 0):
            if (d, z) != (0, 0):
                spread(d, z).start()

    @pl.when(jnp.logical_not(diagonal))
    def _():
        spread(0, 0).start()

    @pl.when(diagonal)
    def _():
        table_ref[1, part, :] = own_ref[...]

    for copy in copies:
        copy.wait()
    for d in range(4):
        for z in range(2):
            if (d, z) != (0, 0):
                spread(d, z).wait_send()

    @pl.when(jnp.logical_not(diagonal))
    def _():
        spread(0, 0).wait_send()

    for i in range(TIMES):
        arrival = pltpu.make_async_remote_copy(
            src_ref=own_ref, dst_ref=table_ref.at[1, pl.ds(i * HALF * 5, HALF * 5)], send_sem=sent3.at[1, 0],
            recv_sem=landed3.at[1, i], device_id=device_of(i // 2, i % 2, y, zl, c),
            device_id_type=pl.DeviceIdType.MESH)

        @pl.when(jnp.logical_or(jnp.logical_not(diagonal), tm != i))
        def _():
            arrival.wait_recv()


def reduce_and_solve(normals):
    return pl.pallas_call(
        reduce_kernel,
        out_shape=jax.ShapeDtypeStruct((2, PIX * 5, 128), F32),
        in_specs=[VMEM],
        out_specs=VMEM,
        scratch_shapes=[
            pltpu.VMEM((2, 3, QROWS, 128), F32),
            pltpu.VMEM((2, QROWS, 128), F32),
            pltpu.VMEM((3, HROWS, 128), F32),
            pltpu.VMEM((HROWS, 128), F32),
            pltpu.VMEM((HALF * 5, 128), F32),
            pltpu.SemaphoreType.DMA((2, 3)),
            pltpu.SemaphoreType.DMA((2, 3)),
            pltpu.SemaphoreType.DMA((3,)),
            pltpu.SemaphoreType.DMA((3,)),
            pltpu.SemaphoreType.DMA((2, 8)),
            pltpu.SemaphoreType.DMA((2, 8)),
        ],
        compiler_params=params(collective_id=2, has_side_effects=True),
        name="reduce",
    )(normals)


def pick_kernel(pix_ref, in_ref, table_ref, out_ref, update_ref, rows_ref):
    row = lax.broadcasted_iota(jnp.int32, (8, 128), 0)
    for plan in range(2):
        def spread(p, _):
            rows_ref[plan * PIX + p] = jnp.where(row < 5, table_ref[plan, pl.ds(p * 5, 8), :], -1.0)
            return 0

        lax.fori_loop(0, PIX - 1, spread, 0, unroll=4)
        rows_ref[plan * PIX + PIX - 1] = jnp.where(
            row < 5, pltpu.roll(table_ref[plan, pl.ds(PIX * 5 - 8, 8), :], 5, 0), -1.0)
    for p in range(PIX):
        update_ref[:, p * 128:(p + 1) * 128] = rows_ref[p, 0:5]

    def sender(b, _):
        count = pix_ref[b, 127]
        offset = lax.shift_right_logical(b, 5) * PIX

        def group(g, _):
            for j in range(8):
                start = b * BLOCK_ROWS + (g * 8 + j) * FIELDS
                v = in_ref[pl.ds(start, 8), :]
                table = rows_ref[offset + jnp.minimum(pix_ref[b, g * 8 + j], PIX - 1)]
                at = jnp.broadcast_to(jnp.clip(v[6:7, :].astype(jnp.int32), 0, 127), (8, 128))
                picked = jnp.take_along_axis(table, at, axis=1)
                terms = jnp.where(row < 6, v * picked, 0.0)
                out_ref[pl.ds(b * SEATS + g * 8 + j, 1), :] = -jnp.sum(terms, axis=0, keepdims=True)
            return 0

        lax.fori_loop(0, lax.shift_right_logical(count + 7, 3), group, 0)
        return 0

    lax.fori_loop(0, SLOTS, sender, 0)


def pick(pix, arrived, table):
    return pl.pallas_call(
        pick_kernel,
        out_shape=(
            jax.ShapeDtypeStruct((SLOTS * SEATS, 128), F32),
            jax.ShapeDtypeStruct((5, PIX * SRC), F32),
        ),
        in_specs=[SMEM, VMEM, VMEM],
        out_specs=(VMEM, VMEM),
        scratch_shapes=[pltpu.VMEM((2 * PIX, 8, 128), F32)],
        compiler_params=params(),
        name="pick",
    )(pix, arrived, table)


def knot_hits(knot_row, first):
    lane = lax.broadcasted_iota(jnp.int32, (SPAN, TILES), 0)
    return (lane == knot_row - first).astype(F32)


def split_dot(hits, value):
    high = value.astype(BF16)
    low = (value - high.astype(F32)).astype(BF16)
    return (jnp.dot(hits, high, preferred_element_type=F32)
            + jnp.dot(hits, low, preferred_element_type=F32))


def quad_kernel(knot_ref, first_ref, w_ref, att_ref, out_ref, hits_ref):
    hits = knot_hits(knot_ref[...], first_ref[0])
    flipped = hits.T
    hits_ref[...] = jnp.concatenate([flipped] * 3 + [jnp.zeros_like(flipped)], axis=1).astype(BF16)
    hits = hits.astype(BF16)
    lane = lax.broadcasted_iota(jnp.int32, (SPAN, 128), 1)
    total = jnp.zeros((SPAN, 128), F32)
    weight = w_ref[...]
    for m in range(4):
        for c in range(4):
            scaled = weight * att_ref[4 * m + c]
            for e in range(c, 4):
                sums = split_dot(hits, scaled * att_ref[4 * m + e])
                at = 14 * m + KNOT_PAIRS.index((c, e))
                total = total + jnp.where(lane == at, jnp.sum(sums, axis=1, keepdims=True), 0.0)
    out_ref[...] = total


def quads(knots, first, weight, attitude):
    return pl.pallas_call(
        quad_kernel,
        out_shape=(jax.ShapeDtypeStruct((SPAN, 128), F32), jax.ShapeDtypeStruct((TILES, 128), BF16)),
        in_specs=[VMEM, SMEM, VMEM, VMEM],
        out_specs=(VMEM, VMEM),
        compiler_params=params(),
        name="quads",
    )(knots, first, weight, attitude)


def finish_kernel(where_ref, knot_ref, first_ref, back_ref, w_ref, att_ref, quad_ref, hits_ref,
                  out_ref, attitude_ref, settled_ref, edge_ref, head_ref, next_ref, piece_ref, pieces_ref,
                  sent, landed):
    tm, sky = lax.axis_index("tm"), lax.axis_index("sky")
    block = tm * OWNERS + sky
    after = ((block + 1) // OWNERS % TIMES, (block + 1) % OWNERS)
    before = ((block + 127) // OWNERS % TIMES, (block + 127) % OWNERS)
    has_after, has_before = block < TIMES * OWNERS - 1, block > 0
    peers = [(tm, (sky + d) % OWNERS) for d in range(1, OWNERS)]
    barrier = pltpu.get_barrier_semaphore()
    edge_ref[1] = jnp.zeros((8, 128), F32)
    next_ref[...] = jnp.zeros((4, 8, 128), F32)
    for peer in peers + [after, before]:
        pl.semaphore_signal(barrier, inc=1, device_id=peer, device_id_type=pl.DeviceIdType.MESH)

    def fetch(g, _):
        for j in range(8):
            t = g * 8 + j
            settled_ref[pl.ds(t, 1), :] = back_ref[pl.ds(where_ref[t], 1), :]
        return 0

    lax.fori_loop(0, TILES // 8, fetch, 0)
    weight = w_ref[...]
    settled = settled_ref[...] / jnp.sqrt(weight)
    settled_ref[...] = settled
    hits = knot_hits(knot_ref[...], first_ref[0]).astype(BF16)
    lane = lax.broadcasted_iota(jnp.int32, (SPAN, 128), 1)
    total = quad_ref[...]
    scaled = weight * settled
    for m in range(4):
        for c in range(4):
            sums = split_dot(hits, scaled * att_ref[4 * m + c])
            at = 14 * m + 10 + c
            total = total + jnp.where(lane == at, jnp.sum(sums, axis=1, keepdims=True), 0.0)
    lane40 = lax.broadcasted_iota(jnp.int32, (SPAN + 8, 128), 1)
    padded = jnp.concatenate([total, jnp.zeros((8, 128), F32)], axis=0)
    moved = jnp.where(lane40 < 14, padded, 0.0)
    for m in range(1, 4):
        shifted = pltpu.roll(pltpu.roll(padded, m, 0), 128 - 14 * m, 1)
        moved = moved + jnp.where(lane40 < 14, shifted, 0.0)
    edge_ref[0] = moved[SPAN:]
    pl.semaphore_wait(barrier, OWNERS + 1)

    def onward(to):
        return pltpu.make_async_remote_copy(
            src_ref=edge_ref.at[0], dst_ref=edge_ref.at[1], send_sem=sent.at[0], recv_sem=landed.at[0],
            device_id=to, device_id_type=pl.DeviceIdType.MESH)

    def backward(to):
        return pltpu.make_async_remote_copy(
            src_ref=head_ref, dst_ref=next_ref, send_sem=sent.at[1], recv_sem=landed.at[1],
            device_id=to, device_id_type=pl.DeviceIdType.MESH)

    @pl.when(has_after)
    def _():
        onward(after).start()

    @pl.when(has_before)
    def _():
        onward(before).wait_recv()

    sums = jnp.concatenate([moved[:8] + edge_ref[1], moved[8:SPAN]], axis=0)

    def column(at):
        return jnp.broadcast_to(sums[:, at:at + 1], (SPAN, 128))

    entries = {pair: column(n) for n, pair in enumerate(KNOT_PAIRS)}
    answer = damped_solve(entries, [column(10 + c) for c in range(4)], 4)
    for c in range(4):
        head_ref[c] = answer[c][:8]

    @pl.when(has_before)
    def _():
        backward(before).start()

    row32 = lax.broadcasted_iota(jnp.int32, (SPAN, 128), 0)
    row8 = lax.broadcasted_iota(jnp.int32, (8, 128), 0)
    piece = jnp.zeros((8, 128), F32)
    for c in range(4):
        line = jnp.sum(jnp.where(lane == row32 + (sky % 4) * SPAN, answer[c], 0.0), axis=0, keepdims=True)
        piece = jnp.where(row8 == c, line, piece)
    piece_ref[...] = piece
    copies = [send(piece_ref, pieces_ref.at[sky], sent.at[1 + d], landed.at[1 + d], peers[d - 1])
              for d in range(1, OWNERS)]
    pieces_ref[sky] = piece

    @pl.when(has_after)
    def _():
        backward(after).wait_recv()

    fix = None
    for m in range(4):
        for c in range(4):
            both = jnp.concatenate([answer[c], next_ref[c]], axis=0)
            value = both[m:m + SPAN]
            high = value.astype(BF16)
            rest = value - high.astype(F32)
            middle = rest.astype(BF16)
            low = (rest - middle.astype(F32)).astype(BF16)
            table = jnp.concatenate([high, middle, low, jnp.zeros_like(high)], axis=0)
            term = att_ref[4 * m + c] * jnp.dot(hits_ref[...], table, preferred_element_type=F32)
            fix = term if fix is None else fix + term
    out_ref[...] = settled_ref[...] - fix
    for copy in copies:
        copy.wait()
    for j in range(4):
        total = pieces_ref[4 * j]
        for i in range(1, 4):
            total = total + pieces_ref[4 * j + i]
        attitude_ref[:, j * 128:(j + 1) * 128] = total[:4]

    @pl.when(has_after)
    def _():
        onward(after).wait_send()

    @pl.when(has_before)
    def _():
        backward(before).wait_send()


def finish(where, knots, first, back, weight, attitude, quad, hits):
    return pl.pallas_call(
        finish_kernel,
        out_shape=(
            jax.ShapeDtypeStruct((TILES, 128), F32),
            jax.ShapeDtypeStruct((4, SPAN * OWNERS), F32),
        ),
        in_specs=[SMEM, VMEM, SMEM, VMEM, VMEM, VMEM, VMEM, VMEM],
        out_specs=(VMEM, VMEM),
        scratch_shapes=[
            pltpu.VMEM((TILES, 128), F32),
            pltpu.VMEM((2, 8, 128), F32),
            pltpu.VMEM((4, 8, 128), F32),
            pltpu.VMEM((4, 8, 128), F32),
            pltpu.VMEM((8, 128), F32),
            pltpu.VMEM((OWNERS, 8, 128), F32),
            pltpu.SemaphoreType.DMA((OWNERS + 1,)),
            pltpu.SemaphoreType.DMA((OWNERS + 1,)),
        ],
        compiler_params=params(collective_id=4, has_side_effects=True),
        name="finish",
    )(where, knots, first, back, weight, attitude, quad, hits)


def body(residual, obs_weight, source_partials, attitude_partials, source_index,
         tile_pixel, tile_knot, pixel_slot):
    block = lax.axis_index("tm") * OWNERS + lax.axis_index("sky")
    first = (block * SPAN).reshape(1)
    knots = tile_knot.reshape(1, TILES)
    packed, where, pix = pack(tile_pixel, pixel_slot, residual, obs_weight, source_partials, source_index)
    arrived, pix = exchange((packed, pix), (BLOCK_ROWS, 1), 1)
    quad, hits = quads(knots, first, obs_weight, attitude_partials)
    normals = normals_of(pix, arrived)
    table = reduce_and_solve(normals)
    corrected, source_update = pick(pix, arrived, table)
    (back,) = exchange((corrected,), (SEATS,), 3)
    final, attitude_update = finish(
        where, knots, first, back, obs_weight, attitude_partials, quad, hits)
    return final, source_update, attitude_update


def solution(mesh):
    in_specs = (
        P(("tm", "sky"), None),
        P(("tm", "sky"), None),
        P(None, ("tm", "sky"), None),
        P(None, ("tm", "sky"), None),
        P(("tm", "sky"), None),
        P(("tm", "sky")),
        P(("tm", "sky")),
        P(),
    )
    out_specs = (P(("tm", "sky"), None), P(None, "sky"), P(None, "tm"))
    return jax.shard_map(body, mesh=mesh, in_specs=in_specs, out_specs=out_specs, check_vma=False)
```

time: 298 us -> 205 us (0.69)
  blocking collectives: 163 us -> 0 us
  Pallas kernels: 62.2 us -> 203 us
  starting transfers between devices: 53.2 us -> 0 us
  waiting for transfers between devices: 15.4 us -> 0 us
    pallas_call x7, Pallas kernels: 56.5 us -> 197 us  [the longest x2 62.9 us: exchange(): pl.pallas_call(lambda *refs: exchange_kernel(sizes, *refs), out_shape=tup...]
    all_to_all x3 -> x0, blocking collectives: 107 us -> none  [the longest x1 69.1 us: body(): lax.all_to_all(packed.reshape(OWNERS, BLOCK_ROWS, 128), 'sky', 0, 0, tile...]
    all_gather x2 -> x0, blocking collectives: 55.9 us -> none  [the longest x1 36 us: body(): table = lax.all_gather(solved, 'tm', axis=0, tiled=True)]
    all_to_all x1 -> x0, starting transfers between devices: 49.4 us -> none  [body(): lax.all_to_all(corrected, 'sky', 0, 0, tiled=True)]
    all_to_all x1 -> x0, waiting for transfers between devices: 7.99 us -> none  [body(): lax.all_to_all(corrected, 'sky', 0, 0, tiled=True)]
    ppermute x2 -> x0, waiting for transfers between devices: 7.43 us -> none  [the longest x1 7.43 us: body(): halo = lax.ppermute(halo, both, [(q, q + 1) for q in range(last)])]
    ppermute x2 -> x0, starting transfers between devices: 3.82 us -> none  [the longest x1 1.91 us: body(): following = lax.ppermute(head, both, [(q + 1, q) for q in range(last)])]
  transfers between devices with their start and end apart: 3 -> 0, of which waited for: 2 -> 0; matrix products, arithmetic and copies ran while one was open for 0% -> 0% of each run, Pallas kernels for 2% -> 0%
where the time goes in v2:
time: 205 us; the launch traced here: 206 us
  Pallas kernels  203 us (99%)
  local copies, waits for them, and re-layouts  2.96 us (1%)
    pallas_call x2, Pallas kernels, exchange(): pl.pallas_call(lambda *refs: exchange_kernel(sizes, *refs), out_shape=tup...  62.9 us
    pallas_call x1, Pallas kernels, reduce_and_solve(): pl.pallas_call(reduce_kernel, out_shape=jax.ShapeDtypeStruct((2, PIX * 5,...  54.2 us
    pallas_call x1, Pallas kernels, normals_of(): pl.pallas_call(normals_kernel, out_shape=jax.ShapeDtypeStruct((2, PIX * T...  39.8 us
    pallas_call x1, Pallas kernels, pick(): pl.pallas_call(pick_kernel, out_shape=(jax.ShapeDtypeStruct((SLOTS * SEAT...  16.7 us
    pallas_call x1, Pallas kernels, finish(): pl.pallas_call(finish_kernel, out_shape=(jax.ShapeDtypeStruct((TILES, 128...  12.8 us
    pallas_call x1, Pallas kernels, pack(): pl.pallas_call(pack_kernel, out_shape=(jax.ShapeDtypeStruct((ROWS_IN, 128...  10.5 us
    pallas_call x1, Pallas kernels, quads(): pl.pallas_call(quad_kernel, out_shape=(jax.ShapeDtypeStruct((SPAN, 128),...  5.62 us

profile of v2, /device:TPU:8, one launch (start us, length us, event | category | flops | bytes accessed | tf_op | source)
XLA Modules:
  0.0 206.3 jit_solution(13238693392446521383)
XLA Ops:
  0.6 10.5 %pack.1 = (f32[10760,128]{1,0:T(8,128)}, s32[512]{0:T(512)}, s32[64,128]{1,0:T(8,128)}) custom-call(s32[512]{0:T(512)} %pixel_ref.1, s32[2048]{0:T(1024)} %slot_ref.1, f32[512,128]{1,0:T(8,128)} %res_ref.1, f32[512,128]{1,0:T(8,128)} %w_ref.5, f32[5,512,128]{2,1,0:T(8,128)} %part_ref.1, s32[512,128]{1,0:T(8,128)} %idx_ref.1), custom_call_target="tpu_custom_call" | custom-call | tf_op jit(solution)/shard_map/pack/pallas_call | solution.py:91
  11.2 49.1 %exchange1.1 = (f32[10760,128]{1,0:T(8,128)}, s32[64,128]{1,0:T(8,128)}) custom-call(f32[10760,128]{1,0:T(8,128)} %get-tuple-element.15.refs_0_, s32[64,128]{1,0:T(8,128)} %get-tuple-element.16.refs_1_), custom_call_target="tpu_custom_call" | custom-call | tf_op jit(solution)/shard_map/exchange1/pallas_call | solution.py:175
  60.3 39.8 %normals.1.in_ref = f32[2,2560,128]{2,1,0:T(8,128)} custom-call(s32[64,128]{1,0:T(8,128)} %get-tuple-element.17.pix_ref, f32[10760,128]{1,0:T(8,128)} %get-tuple-element.18.in_ref), custom_call_target="tpu_custom_call" | custom-call | tf_op jit(solution)/shard_map/normals/pallas_call | solution.py:252
  100.1 54.2 %reduce.1.table_ref = f32[2,640,128]{2,1,0:T(8,128)} custom-call(f32[2,2560,128]{2,1,0:T(8,128)} %normals.1.in_ref), custom_call_target="tpu_custom_call" | custom-call | tf_op jit(solution)/shard_map/reduce/pallas_call | solution.py:410
  154.4 16.7 %pick.1 = (f32[1536,128]{1,0:T(8,128)}, f32[5,16384]{1,0:T(8,128)}) custom-call(s32[64,128]{1,0:T(8,128)} %get-tuple-element.17.pix_ref, f32[10760,128]{1,0:T(8,128)} %get-tuple-element.18.in_ref, f32[2,640,128]{2,1,0:T(8,128)} %reduce.1.table_ref), custom_call_target="tpu_custom_call" | custom-call | tf_op jit(solution)/shard_map/pick/pallas_call | solution.py:468
  171.1 13.8 %exchange3.1.back_ref = f32[1536,128]{1,0:T(8,128)} custom-call(f32[1536,128]{1,0:T(8,128)} %get-tuple-element.19.refs_0_), custom_call_target="tpu_custom_call" | custom-call | tf_op jit(solution)/shard_map/exchange3/pallas_call | solution.py:175
  184.9 5.6 %quads.1 = (f32[32,128]{1,0:T(8,128)}, bf16[512,128]{1,0:T(8,128)(2,1)}) custom-call(s32[1,512]{1,0:T(1,128)} %bitcast.2, s32[1]{0:T(128)} %bitcast.1.first_ref, f32[512,128]{1,0:T(8,128)} %w_ref.5, f32[16,512,128]{2,1,0:T(8,128)} %att_ref.3), custom_call_target="tpu_custom_call" | custom-call | tf_op jit(solution)/shard_map/quads/pallas_call | solution.py:513
  190.5 12.8 %finish.1 = (f32[512,128]{1,0:T(8,128)}, f32[4,512]{1,0:T(4,128)}) custom-call(s32[512]{0:T(512)} %get-tuple-element.14.where_ref, s32[1,512]{1,0:T(1,128)} %bitcast.3, s32[1]{0:T(128)} %bitcast.1.first_ref, f32[1536,128]{1,0:T(8,128)} %exchange3.1.back_ref, f32[512,128]{1,0:T(8,128)} %w_ref.5, f32[16,512,128]{2,1,0:T(8,128)} %att_ref.3, ...), custom_call_target="tpu_custom_call" | custom-call | tf_op jit(solution)/shard_map/finish/pallas_call | solution.py:644
  203.3 1.7 copy.13
  205.0 1.3 copy.14

commit v3 on v2

--- a/solution.py
+++ b/solution.py
@@ -40,15 +40,19 @@
 
 
 def pack_kernel(pixel_ref, slot_ref, res_ref, w_ref, part_ref, idx_ref,
-                out_ref, where_ref, pix_ref, count_ref, stage_ref):
-    def clear(i, _):
-        for b in range(SLOTS):
-            pix_ref[b, i] = PIX
-        return 0
-
-    lax.fori_loop(0, SEATS, clear, 0)
+                out_ref, where_ref, count_ref, stage_ref):
     for o in range(OWNERS):
         count_ref[o] = 0
+    nothing = jnp.zeros((SEATS, 128), F32)
+
+    def clear(b, _):
+        base = pl.multiple_of(b * BLOCK_ROWS, 8)
+        for i in range(FIELDS):
+            out_ref[pl.ds(base + i * SEATS, SEATS), :] = nothing
+        out_ref[pl.ds(base + 6, SEATS, stride=FIELDS), :] = nothing - 1.0
+        return 0
+
+    lax.fori_loop(0, SLOTS, clear, 0)
 
     def scale(g, _):
         rows = pl.ds(pl.multiple_of(g * 8, 8), 8)
@@ -73,18 +77,14 @@
             position = lax.shift_right_logical(rank, 2)
             block = plan * (2 * OWNERS) + owner * 2 + half
             where_ref[t] = block * SEATS + position
-            pix_ref[block, position] = lax.bitwise_and(seat, 127)
             base = block * BLOCK_ROWS + position * FIELDS
-            for f in range(FIELDS):
+            for f in range(6):
                 out_ref[pl.ds(base + f, 1), :] = stage_ref[f, pl.ds(t, 1), :]
+            first = (lax.bitwise_and(seat, 127) * SRC).astype(F32)
+            out_ref[pl.ds(base + 6, 1), :] = stage_ref[6, pl.ds(t, 1), :] + first
         return 0
 
     lax.fori_loop(0, TILES // 8, place, 0)
-    for o in range(OWNERS):
-        for plan in range(2):
-            for half in range(2):
-                left = count_ref[o] + (3 - plan - 2 * half)
-                pix_ref[plan * 2 * OWNERS + o * 2 + half, 127] = lax.shift_right_logical(left, 2)
 
 
 def pack(tile_pixel, pixel_slot, residual, weight, partials, index):
@@ -93,10 +93,9 @@
         out_shape=(
             jax.ShapeDtypeStruct((ROWS_IN, 128), F32),
             jax.ShapeDtypeStruct((TILES,), jnp.int32),
-            jax.ShapeDtypeStruct((SLOTS, 128), jnp.int32),
         ),
         in_specs=[SMEM, SMEM, VMEM, VMEM, VMEM, VMEM],
-        out_specs=(VMEM, SMEM, SMEM),
+        out_specs=(VMEM, SMEM),
         scratch_shapes=[pltpu.SMEM((OWNERS,), jnp.int32), pltpu.VMEM((FIELDS, TILES, 128), F32)],
         compiler_params=params(),
         name="pack",
@@ -127,64 +126,31 @@
     pl.semaphore_wait(barrier, len(devices))
 
 
-MOVES = [(plan, d, dz, dc, h) for d in (2, 1, 3, 0) for dz in (1, 0) for plan in range(2)
-         for dc in (1, 0) for h in range(2)]
-
-
-def exchange_kernel(sizes, *refs):
-    n = len(sizes)
-    srcs, dsts = refs[:n], refs[n:2 * n]
-    bounces = refs[2 * n:3 * n]
-    sent, landed, local = refs[3 * n:]
+MOVES = [(plan, d, dz, dc, h)
+         for d, dz in ((0, 0), (1, 0), (3, 0), (0, 1), (2, 0), (1, 1), (3, 1), (2, 1))
+         for plan in range(2) for dc in range(2) for h in range(2)]
+OWN = (0, 1, 4, 5)
+CHUNK = 4
+CHUNKS = SLOTS // CHUNK
+PITCH = 136
+ROOM = BLOCK_ROWS + 8
+HBM = pl.BlockSpec(memory_space=pltpu.HBM)
+
+
+def routes_of(back):
     y, zh, x, zl, c = place_of()
-    mine = (x * 4 + zl * 2 + c, y * 4 + zl * 2 + c)
+    sign = -1 if back else 1
     routes = []
     for plan, d, dz, dc, h in MOVES:
-        far = ((y if plan else x) + d) % 4
+        far = ((y if plan else x) + 4 + sign * d) % 4
         zl_to, c_to, zh_to = (zl + dz) % 2, (c + dc) % 2, (zh + dz * h) % 2
-        owner = far * 4 + zl_to * 2 + c_to
         to = device_of(far, zh_to, x, zl_to, c_to) if plan else device_of(y, zh_to, far, zl_to, c_to)
-        routes.append((plan * 32 + owner * 2 + h, plan * 32 + mine[plan] * 2 + h, to,
-                       d == 0 and dz == 0 and dc == 0))
-    greet([to for _, _, to, own in routes if not own])
-    copies = []
-    for k, (block, slot, to, own) in enumerate(routes):
-        if not own:
-            for i, size in enumerate(sizes):
-                copies.append(send(srcs[i].at[pl.ds(block * size, size)], dsts[i].at[pl.ds(slot * size, size)],
-                                   sent.at[i, k], landed.at[i, k], to))
-    kept = [(block, at) for at, (block, slot, to, own) in enumerate(r for r in routes if r[3])]
-    for way in range(2):
-        moves = []
-        for block, at in kept:
-            for i, size in enumerate(sizes):
-                ends = (srcs[i].at[pl.ds(block * size, size)], bounces[i].at[pl.ds(at * size, size)])
-                if way:
-                    ends = (ends[1], dsts[i].at[pl.ds(block * size, size)])
-                move = pltpu.make_async_copy(ends[0], ends[1], local.at[i, at])
-                move.start()
-                moves.append(move)
-        for move in moves:
-            move.wait()
-    for copy in copies:
-        copy.wait()
-
-
-def exchange(arrays, sizes, number):
-    n = len(arrays)
-    return pl.pallas_call(
-        lambda *refs: exchange_kernel(sizes, *refs),
-        out_shape=tuple(jax.ShapeDtypeStruct(a.shape, a.dtype) for a in arrays),
-        in_specs=[pl.BlockSpec(memory_space=pltpu.HBM)] * n,
-        out_specs=tuple(pl.BlockSpec(memory_space=pltpu.HBM) for _ in arrays),
-        scratch_shapes=[pltpu.VMEM((4 * size, 128), a.dtype) for a, size in zip(arrays, sizes)] + [
-            pltpu.SemaphoreType.DMA((n, len(MOVES))),
-            pltpu.SemaphoreType.DMA((n, len(MOVES))),
-            pltpu.SemaphoreType.DMA((n, 4)),
-        ],
-        compiler_params=params(collective_id=number, has_side_effects=True),
-        name="exchange" + str(number),
-    )(*arrays)
+        if back:
+            owner = (y if plan else x) * 4 + zl * 2 + c
+        else:
+            owner = far * 4 + zl_to * 2 + c_to
+        routes.append((plan * 2 * OWNERS + owner * 2 + h, to))
+    return routes
 
 
 def pair_products(v, row):
@@ -197,67 +163,201 @@
     return jnp.concatenate([first * v, first * second, third * fourth], axis=0)
 
 
-def tile_sums(v, row, sources):
+def left_side(v, row):
     products = pair_products(v, row)
     high = products.astype(BF16).astype(F32)
-    left = jnp.concatenate([high, products - high], axis=0).astype(BF16)
-    hits = (v[6:7, :].astype(BF16) == sources).astype(BF16)
-    out = lax.dot_general(left, hits, (((1,), (1,)), ((), ())), preferred_element_type=F32)
-    return out[:24] + out[24:]
-
-
-def normals_kernel(pix_ref, in_ref, out_ref, acc_ref):
-    zero = jnp.zeros((24, 128), F32)
-
-    def clear(p, _):
-        acc_ref[p] = zero
-        return 0
-
-    lax.fori_loop(0, 2 * (PIX + 1), clear, 0, unroll=6)
+    return jnp.concatenate([high, products - high], axis=0).astype(BF16)
+
+
+def landing(in_ref, arr_ref, sent, landed, k, to):
+    return pltpu.make_async_remote_copy(
+        src_ref=in_ref.at[pl.ds(k * BLOCK_ROWS, BLOCK_ROWS)],
+        dst_ref=arr_ref.at[pl.ds(k * ROOM, BLOCK_ROWS)], send_sem=sent.at[k], recv_sem=landed.at[k],
+        device_id=to, device_id_type=pl.DeviceIdType.MESH)
+
+
+def gather_kernel(in_ref, att_hbm, w_hbm, knot_ref, first_ref,
+                  keep_ref, sums_ref, pix_ref, quad_ref, hits_ref,
+                  arr_ref, att_ref, w_ref, spread_ref, sent, landed, local, stored):
+    routes = routes_of(False)
+    load_att = pltpu.make_async_copy(att_hbm, att_ref, local.at[4])
+    load_w = pltpu.make_async_copy(w_hbm, w_ref, local.at[5])
+    load_att.start()
+    load_w.start()
+    greet([to for k, (_, to) in enumerate(routes) if k not in OWN])
+    copies = []
+    for k, (block, to) in enumerate(routes):
+        if k not in OWN:
+            copies.append(send(in_ref.at[pl.ds(block * BLOCK_ROWS, BLOCK_ROWS)],
+                               arr_ref.at[pl.ds(k * ROOM, BLOCK_ROWS)], sent.at[k], landed.at[k], to))
+    kept = []
+    for i, k in enumerate(OWN):
+        kept.append(pltpu.make_async_copy(in_ref.at[pl.ds(routes[k][0] * BLOCK_ROWS, BLOCK_ROWS)],
+                                          arr_ref.at[pl.ds(k * ROOM, BLOCK_ROWS)], local.at[i]))
+        kept[-1].start()
+
+    def clear(g, _):
+        spread_ref[pl.ds(pl.multiple_of(g * 8, 8), 8), :] = jnp.zeros((8, 128), F32)
+        return 0
+
+    lax.fori_loop(0, 24 * PITCH // 8, clear, 0, unroll=4)
+
+    def clear_sums(g, _):
+        for plan in range(2):
+            sums_ref[plan, pl.ds(pl.multiple_of(g * 16, 16), 16), :] = jnp.zeros((16, 128), F32)
+        return 0
+
+    lax.fori_loop(0, PIX * TERMS // 16, clear_sums, 0, unroll=4)
+    load_att.wait()
+    load_w.wait()
+    quad_sums(knot_ref, first_ref, w_ref, att_ref, quad_ref, hits_ref)
+    for move in kept:
+        move.wait()
     row = lax.broadcasted_iota(jnp.int32, (8, 128), 0)
-    sources = lax.broadcasted_iota(jnp.int32, (128, 128), 0).astype(F32).astype(BF16)
-
-    def sender(b, _):
-        count = pix_ref[b, 127]
-        offset = lax.shift_right_logical(b, 5) * (PIX + 1)
+    sources = lax.broadcasted_iota(jnp.int32, (128, 128), 0).astype(F32)
+    pixels = lax.broadcasted_iota(jnp.int32, (SEATS, 128), 1)
+    seat_row = lax.broadcasted_iota(jnp.int32, (SEATS, 128), 0)
+    blank = jnp.zeros((48, 128), BF16)
+
+    def keep(k):
+        return pltpu.make_async_copy(arr_ref.at[pl.ds(k * ROOM, BLOCK_ROWS)],
+                                     keep_ref.at[pl.ds(k * BLOCK_ROWS, BLOCK_ROWS)], stored.at[k])
+
+    def chunk_step(chunk, _):
+        plan = chunk % 2
+        for i in range(CHUNK):
+            k = chunk * CHUNK + i
+            arrival = landing(in_ref, arr_ref, sent, landed, k, routes[2][1])
+            if i < 2:
+                @pl.when(chunk >= 2)
+                def _():
+                    arrival.wait_recv()
+            else:
+                arrival.wait_recv()
+            keep(k).start()
 
         def group(g, _):
-            sums = []
-            for j in range(8):
-                start = b * BLOCK_ROWS + (g * 8 + j) * FIELDS
-                sums.append(tile_sums(in_ref[pl.ds(start, 8), :], row, sources))
-            for j in range(8):
-                p = offset + pix_ref[b, g * 8 + j]
-                acc_ref[p] = acc_ref[p] + sums[j]
+            for j in range(0, 8, 2):
+                start = (chunk * CHUNK + g // 3) * ROOM + (g % 3 * 8 + j) * FIELDS
+                lefts, hits = [], []
+                for i in range(2):
+                    v = arr_ref[pl.ds(start + i * FIELDS, 8), :]
+                    within = v - jnp.floor(v * (1.0 / SRC)) * SRC
+                    lefts.append(left_side(v, row))
+                    hits.append((within[6:7, :] == sources).astype(F32).astype(BF16))
+                left = jnp.concatenate([jnp.concatenate([lefts[0], blank], axis=1),
+                                        jnp.concatenate([blank, lefts[1]], axis=1)], axis=0)
+                out = lax.dot_general(left, jnp.concatenate(hits, axis=1), (((1,), (1,)), ((), ())),
+                                      preferred_element_type=F32)
+                for i in range(2):
+                    both = out[48 * i:48 * i + 24] + out[48 * i + 24:48 * i + 48]
+                    for n in range(3):
+                        spread_ref[pl.ds(8 * n * PITCH + g * 8 + j + i, 8, stride=PITCH), :] = both[8 * n:8 * n + 8]
             return 0
 
-        lax.fori_loop(0, lax.shift_right_logical(count + 7, 3), group, 0)
-        return 0
-
-    lax.fori_loop(0, SLOTS, sender, 0)
-
-    for plan in range(2):
-        def write(p, _):
-            base = p * TERMS
-            at = plan * (PIX + 1) + p
-            out_ref[plan, pl.ds(base, 8), :] = acc_ref[at, 0:8]
-            out_ref[plan, pl.ds(base + 6, 8), :] = acc_ref[at, 8:16]
-            out_ref[plan, pl.ds(base + 13, 7), :] = acc_ref[at, 16:23]
-            return 0
-
-        lax.fori_loop(0, PIX, write, 0, unroll=4)
-
-
-def normals_of(pix, arrived):
+        lax.fori_loop(0, CHUNK * SEATS // 8, group, 0)
+        places = []
+        for i in range(CHUNK):
+            k = chunk * CHUNK + i
+            whole = arr_ref[pl.ds(k * ROOM + 6, SEATS, stride=FIELDS), :]
+            pixel = jnp.floor(whole * (1.0 / SRC)).astype(jnp.int32)
+            places.append((pixel == pixels).astype(F32))
+            line = jnp.sum(jnp.where(pixels == seat_row, pixel + plan * PIX, 0), axis=0, keepdims=True)
+            count = jnp.sum((pixel >= 0).astype(jnp.int32), axis=0, keepdims=True)
+            line = jnp.where(pixels[:1] == 127, count, jnp.where(pixels[:1] < SEATS, line, 0))
+            pix_ref[pl.ds(k, 1), :] = jnp.maximum(line, 0)
+        places.append(jnp.zeros((128 - CHUNK * SEATS, 128), F32))
+        place = jnp.concatenate(places, axis=0).T.astype(BF16)
+        place = jnp.concatenate([place, place], axis=1)
+        for n in range(TERMS):
+            at = n + (2 if n >= 6 else 0) + (1 if n >= 13 else 0)
+            value = spread_ref[pl.ds(at * PITCH, 128), :]
+            high = value.astype(BF16)
+            low = (value - high.astype(F32)).astype(BF16)
+            added = jnp.dot(place, jnp.concatenate([high, low], axis=0), preferred_element_type=F32)
+            for part in range(TIMES):
+                rows = pl.ds(part * HROWS + n * HALF, HALF)
+                sums_ref[plan, rows, :] = sums_ref[plan, rows, :] + added[part * HALF:(part + 1) * HALF]
+        return 0
+
+    lax.fori_loop(0, CHUNKS, chunk_step, 0)
+    for copy in copies:
+        copy.wait_send()
+
+    def kept_step(k, _):
+        keep(k).wait()
+        return 0
+
+    lax.fori_loop(0, SLOTS, kept_step, 0)
+
+
+def gather_tiles(packed, attitude, weight, knots, first):
     return pl.pallas_call(
-        normals_kernel,
-        out_shape=jax.ShapeDtypeStruct((2, PIX * TERMS, 128), F32),
-        in_specs=[SMEM, VMEM],
-        out_specs=VMEM,
-        scratch_shapes=[pltpu.VMEM((2 * (PIX + 1), 24, 128), F32)],
-        compiler_params=params(),
-        name="normals",
-    )(pix, arrived)
+        gather_kernel,
+        out_shape=(
+            jax.ShapeDtypeStruct((ROWS_IN, 128), F32),
+            jax.ShapeDtypeStruct((2, PIX * TERMS, 128), F32),
+            jax.ShapeDtypeStruct((SLOTS, 128), jnp.int32),
+            jax.ShapeDtypeStruct((SPAN, 128), F32),
+            jax.ShapeDtypeStruct((TILES, 128), BF16),
+        ),
+        in_specs=[HBM, HBM, HBM, VMEM, SMEM],
+        out_specs=(HBM, VMEM, VMEM, VMEM, VMEM),
+        scratch_shapes=[
+            pltpu.VMEM((SLOTS * ROOM, 128), F32),
+            pltpu.VMEM((16, TILES, 128), F32),
+            pltpu.VMEM((TILES, 128), F32),
+            pltpu.VMEM((24 * PITCH, 128), F32),
+            pltpu.SemaphoreType.DMA((SLOTS,)),
+            pltpu.SemaphoreType.DMA((SLOTS,)),
+            pltpu.SemaphoreType.DMA((6,)),
+            pltpu.SemaphoreType.DMA((SLOTS,)),
+        ],
+        compiler_params=params(collective_id=1, has_side_effects=True),
+        name="gather_tiles",
+    )(packed, attitude, weight, knots, first)
+
+
+def return_kernel(in_ref, out_ref, bounce_ref, sent, landed, local):
+    y, zh, x, zl, c = place_of()
+    routes = routes_of(True)
+    greet([to for k, (_, to) in enumerate(routes) if k not in OWN])
+    copies = []
+    for k, (block, to) in enumerate(routes):
+        if k not in OWN:
+            copies.append(send(in_ref.at[pl.ds(k * SEATS, SEATS)], out_ref.at[pl.ds(block * SEATS, SEATS)],
+                               sent.at[k], landed.at[k], to))
+    for way in range(2):
+        moves = []
+        for i, k in enumerate(OWN):
+            middle = bounce_ref.at[pl.ds(i * SEATS, SEATS)]
+            if way:
+                move = pltpu.make_async_copy(middle, out_ref.at[pl.ds(routes[k][0] * SEATS, SEATS)], local.at[i])
+            else:
+                move = pltpu.make_async_copy(in_ref.at[pl.ds(k * SEATS, SEATS)], middle, local.at[i])
+            move.start()
+            moves.append(move)
+        for move in moves:
+            move.wait()
+    for copy in copies:
+        copy.wait()
+
+
+def return_tiles(corrected):
+    return pl.pallas_call(
+        return_kernel,
+        out_shape=jax.ShapeDtypeStruct(corrected.shape, F32),
+        in_specs=[HBM],
+        out_specs=HBM,
+        scratch_shapes=[
+            pltpu.VMEM((4 * SEATS, 128), F32),
+            pltpu.SemaphoreType.DMA((SLOTS,)),
+            pltpu.SemaphoreType.DMA((SLOTS,)),
+            pltpu.SemaphoreType.DMA((4,)),
+        ],
+        compiler_params=params(collective_id=3, has_side_effects=True),
+        name="return_tiles",
+    )(corrected)
 
 
 def damped_solve(entries, target, order):
@@ -351,23 +451,23 @@
 
     across.wait()
     add_rows(whole_ref, 0, [(sum_ref.at[0], zh * HROWS)] + [(other_ref.at[i], 0) for i in range(3)], HROWS)
-    sums = [whole_ref[pl.ds(term, HALF, stride=TERMS), :] for term in range(TERMS)]
+    sums = [whole_ref[pl.ds(term * HALF, HALF), :] for term in range(TERMS)]
     entries = {key: sums[at] for key, at in TERM_ROW.items() if key[1] < 5}
     target = [sums[TERM_ROW[a, 5]] for a in range(5)]
     for a, value in enumerate(damped_solve(entries, target, 5)):
         own_ref[pl.ds(a, HALF, stride=5), :] = value
-    part = pl.ds(tm * HALF * 5, HALF * 5)
+    part = [pl.ds(plan * PIX * 5 + tm * HALF * 5, HALF * 5) for plan in range(2)]
     copies = []
     for d in (2, 1, 3, 0):
         for z in (1, 0):
             if (d, z) != (0, 0):
-                copies.append(send(own_ref, table_ref.at[0, part], sent3.at[0, d * 2 + z], landed3.at[0, d * 2 + z],
+                copies.append(send(own_ref, table_ref.at[part[0]], sent3.at[0, d * 2 + z], landed3.at[0, d * 2 + z],
                                    device_of((y + d) % 4, (zh + z) % 2, x, zl, c)))
-    table_ref[0, part, :] = own_ref[...]
+    table_ref[part[0], :] = own_ref[...]
 
     def spread(d, z):
         return pltpu.make_async_remote_copy(
-            src_ref=own_ref, dst_ref=table_ref.at[1, part], send_sem=sent3.at[1, d * 2 + z],
+            src_ref=own_ref, dst_ref=table_ref.at[part[1]], send_sem=sent3.at[1, d * 2 + z],
             recv_sem=landed3.at[1, tm], device_id=device_of(x, (zh + z) % 2, (x + d) % 4, zl, c),
             device_id_type=pl.DeviceIdType.MESH)
 
@@ -382,7 +482,7 @@
 
     @pl.when(diagonal)
     def _():
-        table_ref[1, part, :] = own_ref[...]
+        table_ref[part[1], :] = own_ref[...]
 
     for copy in copies:
         copy.wait()
@@ -397,7 +497,7 @@
 
     for i in range(TIMES):
         arrival = pltpu.make_async_remote_copy(
-            src_ref=own_ref, dst_ref=table_ref.at[1, pl.ds(i * HALF * 5, HALF * 5)], send_sem=sent3.at[1, 0],
+            src_ref=own_ref, dst_ref=table_ref.at[pl.ds(PIX * 5 + i * HALF * 5, HALF * 5)], send_sem=sent3.at[1, 0],
             recv_sem=landed3.at[1, i], device_id=device_of(i // 2, i % 2, y, zl, c),
             device_id_type=pl.DeviceIdType.MESH)
 
@@ -409,7 +509,7 @@
 def reduce_and_solve(normals):
     return pl.pallas_call(
         reduce_kernel,
-        out_shape=jax.ShapeDtypeStruct((2, PIX * 5, 128), F32),
+        out_shape=jax.ShapeDtypeStruct((2 * PIX * 5 + 8, 128), F32),
         in_specs=[VMEM],
         out_specs=VMEM,
         scratch_shapes=[
@@ -430,31 +530,23 @@
     )(normals)
 
 
-def pick_kernel(pix_ref, in_ref, table_ref, out_ref, update_ref, rows_ref):
+def pick_kernel(pix_ref, in_ref, table_ref, out_ref, update_ref):
     row = lax.broadcasted_iota(jnp.int32, (8, 128), 0)
-    for plan in range(2):
-        def spread(p, _):
-            rows_ref[plan * PIX + p] = jnp.where(row < 5, table_ref[plan, pl.ds(p * 5, 8), :], -1.0)
-            return 0
-
-        lax.fori_loop(0, PIX - 1, spread, 0, unroll=4)
-        rows_ref[plan * PIX + PIX - 1] = jnp.where(
-            row < 5, pltpu.roll(table_ref[plan, pl.ds(PIX * 5 - 8, 8), :], 5, 0), -1.0)
     for p in range(PIX):
-        update_ref[:, p * 128:(p + 1) * 128] = rows_ref[p, 0:5]
+        update_ref[:, p * 128:(p + 1) * 128] = table_ref[p * 5:p * 5 + 5, :]
 
     def sender(b, _):
         count = pix_ref[b, 127]
-        offset = lax.shift_right_logical(b, 5) * PIX
 
         def group(g, _):
             for j in range(8):
                 start = b * BLOCK_ROWS + (g * 8 + j) * FIELDS
                 v = in_ref[pl.ds(start, 8), :]
-                table = rows_ref[offset + jnp.minimum(pix_ref[b, g * 8 + j], PIX - 1)]
-                at = jnp.broadcast_to(jnp.clip(v[6:7, :].astype(jnp.int32), 0, 127), (8, 128))
+                table = table_ref[pl.ds(pix_ref[b, g * 8 + j] * 5, 8), :]
+                within = (v - jnp.floor(v * (1.0 / SRC)) * SRC).astype(jnp.int32)
+                at = jnp.broadcast_to(lax.bitwise_and(within[6:7, :], 127), (8, 128))
                 picked = jnp.take_along_axis(table, at, axis=1)
-                terms = jnp.where(row < 6, v * picked, 0.0)
+                terms = jnp.where(row < 5, v * picked, jnp.where(row == 5, -v, 0.0))
                 out_ref[pl.ds(b * SEATS + g * 8 + j, 1), :] = -jnp.sum(terms, axis=0, keepdims=True)
             return 0
 
@@ -473,7 +565,6 @@
         ),
         in_specs=[SMEM, VMEM, VMEM],
         out_specs=(VMEM, VMEM),
-        scratch_shapes=[pltpu.VMEM((2 * PIX, 8, 128), F32)],
         compiler_params=params(),
         name="pick",
     )(pix, arrived, table)
@@ -491,7 +582,7 @@
             + jnp.dot(hits, low, preferred_element_type=F32))
 
 
-def quad_kernel(knot_ref, first_ref, w_ref, att_ref, out_ref, hits_ref):
+def quad_sums(knot_ref, first_ref, w_ref, att_ref, out_ref, hits_ref):
     hits = knot_hits(knot_ref[...], first_ref[0])
     flipped = hits.T
     hits_ref[...] = jnp.concatenate([flipped] * 3 + [jnp.zeros_like(flipped)], axis=1).astype(BF16)
@@ -507,17 +598,6 @@
                 at = 14 * m + KNOT_PAIRS.index((c, e))
                 total = total + jnp.where(lane == at, jnp.sum(sums, axis=1, keepdims=True), 0.0)
     out_ref[...] = total
-
-
-def quads(knots, first, weight, attitude):
-    return pl.pallas_call(
-        quad_kernel,
-        out_shape=(jax.ShapeDtypeStruct((SPAN, 128), F32), jax.ShapeDtypeStruct((TILES, 128), BF16)),
-        in_specs=[VMEM, SMEM, VMEM, VMEM],
-        out_specs=(VMEM, VMEM),
-        compiler_params=params(),
-        name="quads",
-    )(knots, first, weight, attitude)
 
 
 def finish_kernel(where_ref, knot_ref, first_ref, back_ref, w_ref, att_ref, quad_ref, hits_ref,
@@ -669,13 +749,11 @@
     block = lax.axis_index("tm") * OWNERS + lax.axis_index("sky")
     first = (block * SPAN).reshape(1)
     knots = tile_knot.reshape(1, TILES)
-    packed, where, pix = pack(tile_pixel, pixel_slot, residual, obs_weight, source_partials, source_index)
-    arrived, pix = exchange((packed, pix), (BLOCK_ROWS, 1), 1)
-    quad, hits = quads(knots, first, obs_weight, attitude_partials)
-    normals = normals_of(pix, arrived)
+    packed, where = pack(tile_pixel, pixel_slot, residual, obs_weight, source_partials, source_index)
+    arrived, normals, pix, quad, hits = gather_tiles(packed, attitude_partials, obs_weight, knots, first)
     table = reduce_and_solve(normals)
     corrected, source_update = pick(pix, arrived, table)
-    (back,) = exchange((corrected,), (SEATS,), 3)
+    back = return_tiles(corrected)
     final, attitude_update = finish(
         where, knots, first, back, obs_weight, attitude_partials, quad, hits)
     return final, source_update, attitude_update

time: 205 us -> 178 us (0.87)
  Pallas kernels: 203 us -> 174 us
    pallas_call x5 -> x3, Pallas kernels: 163 us -> 140 us  [the longest x1 68.6 us: gather_tiles(): pl.pallas_call(gather_kernel, out_shape=(jax.ShapeDtypeStruct((ROWS_IN, 1...]
    pallas_call x1, Pallas kernels: 16.7 us -> 12.4 us  [pick(): pl.pallas_call(pick_kernel, out_shape=(jax.ShapeDtypeStruct((SLOTS * SEAT...]
where the time goes in v3:
time: 178 us
  Pallas kernels  174 us (98%)
  local copies, waits for them, and re-layouts  2.96 us (2%)
    pallas_call x1, Pallas kernels, gather_tiles(): pl.pallas_call(gather_kernel, out_shape=(jax.ShapeDtypeStruct((ROWS_IN, 1...  68.6 us
    pallas_call x1, Pallas kernels, reduce_and_solve(): pl.pallas_call(reduce_kernel, out_shape=jax.ShapeDtypeStruct((2 * PIX * 5...  50.7 us
    pallas_call x1, Pallas kernels, return_tiles(): pl.pallas_call(return_kernel, out_shape=jax.ShapeDtypeStruct(corrected.sh...  20.4 us
    pallas_call x1, Pallas kernels, finish(): pl.pallas_call(finish_kernel, out_shape=(jax.ShapeDtypeStruct((TILES, 128...  12.9 us
    pallas_call x1, Pallas kernels, pick(): pl.pallas_call(pick_kernel, out_shape=(jax.ShapeDtypeStruct((SLOTS * SEAT...  12.4 us
    pallas_call x1, Pallas kernels, pack(): pl.pallas_call(pack_kernel, out_shape=(jax.ShapeDtypeStruct((ROWS_IN, 128...  9.18 us

profile of v3, /device:TPU:8, one launch (start us, length us, event | category | flops | bytes accessed | tf_op | source)
XLA Modules:
  0.0 177.8 jit_solution(17556238491838481200)
XLA Ops:
  0.6 9.2 %pack.1 = (f32[10760,128]{1,0:T(8,128)}, s32[512]{0:T(512)}) custom-call(s32[512]{0:T(512)} %pixel_ref.1, s32[2048]{0:T(1024)} %slot_ref.1, f32[512,128]{1,0:T(8,128)} %res_ref.1, f32[512,128]{1,0:T(8,128)} %w_ref.3, f32[5,512,128]{2,1,0:T(8,128)} %part_ref.1, s32[512,128]{1,0:T(8,128)} %idx_ref.1), custom_call_target="tpu_custom_call" | custom-call | tf_op jit(solution)/shard_map/pack/pallas_call | solution.py:91
  9.8 68.6 %gather_tiles.1 = (f32[10760,128]{1,0:T(8,128)}, f32[2,2560,128]{2,1,0:T(8,128)}, s32[64,128]{1,0:T(8,128)}, f32[32,128]{1,0:T(8,128)}, bf16[512,128]{1,0:T(8,128)(2,1)}) custom-call(f32[10760,128]{1,0:T(8,128)} %get-tuple-element.15.in_ref, f32[16,512,128]{2,1,0:T(8,128)} %att_ref.1, f32[512,128]{1,0:T(8,128)} %w_ref.3, s32[1,512]{1,0:T(1,128)} %bitcast.2, ...), custom_call_target="tpu_custom_call" | custom-call | tf_op jit(solution)/shard_map/gather_tiles/pallas_call | solution.py:295
  78.5 50.7 %reduce.1.table_ref = f32[1288,128]{1,0:T(8,128)} custom-call(f32[2,2560,128]{2,1,0:T(8,128)} %get-tuple-element.18.in_ref), custom_call_target="tpu_custom_call" | custom-call | tf_op jit(solution)/shard_map/reduce/pallas_call | solution.py:510
  129.1 12.4 %pick.1 = (f32[1536,128]{1,0:T(8,128)}, f32[5,16384]{1,0:T(8,128)}) custom-call(s32[64,128]{1,0:T(8,128)} %get-tuple-element.16.pix_ref, f32[10760,128]{1,0:T(8,128)} %get-tuple-element.17.in_ref, f32[1288,128]{1,0:T(8,128)} %reduce.1.table_ref), custom_call_target="tpu_custom_call" | custom-call | tf_op jit(solution)/shard_map/pick/pallas_call | solution.py:560
  141.5 20.4 %return_tiles.1.back_ref = f32[1536,128]{1,0:T(8,128)} custom-call(f32[1536,128]{1,0:T(8,128)} %get-tuple-element.19.in_ref), custom_call_target="tpu_custom_call" | custom-call | tf_op jit(solution)/shard_map/return_tiles/pallas_call | solution.py:347
  162.0 12.9 %finish.1 = (f32[512,128]{1,0:T(8,128)}, f32[4,512]{1,0:T(4,128)}) custom-call(s32[512]{0:T(512)} %get-tuple-element.14.where_ref, s32[1,512]{1,0:T(1,128)} %bitcast.3, s32[1]{0:T(128)} %bitcast.1.first_ref, f32[1536,128]{1,0:T(8,128)} %return_tiles.1.back_ref, f32[512,128]{1,0:T(8,128)} %w_ref.3, f32[16,512,128]{2,1,0:T(8,128)} %att_ref.1, ...), custom_call_target="tpu_custom_call" | custom-call | tf_op jit(solution)/shard_map/finish/pallas_call | solution.py:724
  174.8 1.7 copy.13
  176.5 1.3 copy.14

commit v4 on v3

--- a/solution.py
+++ b/solution.py
@@ -126,9 +126,8 @@
     pl.semaphore_wait(barrier, len(devices))
 
 
-MOVES = [(plan, d, dz, dc, h)
-         for d, dz in ((0, 0), (1, 0), (3, 0), (0, 1), (2, 0), (1, 1), (3, 1), (2, 1))
-         for plan in range(2) for dc in range(2) for h in range(2)]
+MOVES = [(plan, m % 4, m // 4, dc, h)
+         for m in range(8) for plan in range(2) for dc in range(2) for h in range(2)]
 OWN = (0, 1, 4, 5)
 CHUNK = 4
 CHUNKS = SLOTS // CHUNK
@@ -137,18 +136,14 @@
 HBM = pl.BlockSpec(memory_space=pltpu.HBM)
 
 
-def routes_of(back):
+def routes_of():
     y, zh, x, zl, c = place_of()
-    sign = -1 if back else 1
     routes = []
     for plan, d, dz, dc, h in MOVES:
-        far = ((y if plan else x) + 4 + sign * d) % 4
+        far = ((y if plan else x) + d) % 4
         zl_to, c_to, zh_to = (zl + dz) % 2, (c + dc) % 2, (zh + dz * h) % 2
         to = device_of(far, zh_to, x, zl_to, c_to) if plan else device_of(y, zh_to, far, zl_to, c_to)
-        if back:
-            owner = (y if plan else x) * 4 + zl * 2 + c
-        else:
-            owner = far * 4 + zl_to * 2 + c_to
+        owner = far * 4 + zl_to * 2 + c_to
         routes.append((plan * 2 * OWNERS + owner * 2 + h, to))
     return routes
 
@@ -179,7 +174,7 @@
 def gather_kernel(in_ref, att_hbm, w_hbm, knot_ref, first_ref,
                   keep_ref, sums_ref, pix_ref, quad_ref, hits_ref,
                   arr_ref, att_ref, w_ref, spread_ref, sent, landed, local, stored):
-    routes = routes_of(False)
+    routes = routes_of()
     load_att = pltpu.make_async_copy(att_hbm, att_ref, local.at[4])
     load_w = pltpu.make_async_copy(w_hbm, w_ref, local.at[5])
     load_att.start()
@@ -221,7 +216,7 @@
 
     def keep(k):
         return pltpu.make_async_copy(arr_ref.at[pl.ds(k * ROOM, BLOCK_ROWS)],
-                                     keep_ref.at[pl.ds(k * BLOCK_ROWS, BLOCK_ROWS)], stored.at[k])
+                                     keep_ref.at[pl.ds(k * ROOM, BLOCK_ROWS)], stored.at[k])
 
     def chunk_step(chunk, _):
         plan = chunk % 2
@@ -237,8 +232,8 @@
             keep(k).start()
 
         def group(g, _):
-            for j in range(0, 8, 2):
-                start = (chunk * CHUNK + g // 3) * ROOM + (g % 3 * 8 + j) * FIELDS
+            for j in range(0, SEATS, 2):
+                start = (chunk * CHUNK + g) * ROOM + j * FIELDS
                 lefts, hits = [], []
                 for i in range(2):
                     v = arr_ref[pl.ds(start + i * FIELDS, 8), :]
@@ -252,10 +247,10 @@
                 for i in range(2):
                     both = out[48 * i:48 * i + 24] + out[48 * i + 24:48 * i + 48]
                     for n in range(3):
-                        spread_ref[pl.ds(8 * n * PITCH + g * 8 + j + i, 8, stride=PITCH), :] = both[8 * n:8 * n + 8]
+                        spread_ref[pl.ds(8 * n * PITCH + g * SEATS + j + i, 8, stride=PITCH), :] = both[8 * n:8 * n + 8]
             return 0
 
-        lax.fori_loop(0, CHUNK * SEATS // 8, group, 0)
+        lax.fori_loop(0, CHUNK, group, 0)
         places = []
         for i in range(CHUNK):
             k = chunk * CHUNK + i
@@ -295,7 +290,7 @@
     return pl.pallas_call(
         gather_kernel,
         out_shape=(
-            jax.ShapeDtypeStruct((ROWS_IN, 128), F32),
+            jax.ShapeDtypeStruct((SLOTS * ROOM, 128), F32),
             jax.ShapeDtypeStruct((2, PIX * TERMS, 128), F32),
             jax.ShapeDtypeStruct((SLOTS, 128), jnp.int32),
             jax.ShapeDtypeStruct((SPAN, 128), F32),
@@ -316,48 +311,6 @@
         compiler_params=params(collective_id=1, has_side_effects=True),
         name="gather_tiles",
     )(packed, attitude, weight, knots, first)
-
-
-def return_kernel(in_ref, out_ref, bounce_ref, sent, landed, local):
-    y, zh, x, zl, c = place_of()
-    routes = routes_of(True)
-    greet([to for k, (_, to) in enumerate(routes) if k not in OWN])
-    copies = []
-    for k, (block, to) in enumerate(routes):
-        if k not in OWN:
-            copies.append(send(in_ref.at[pl.ds(k * SEATS, SEATS)], out_ref.at[pl.ds(block * SEATS, SEATS)],
-                               sent.at[k], landed.at[k], to))
-    for way in range(2):
-        moves = []
-        for i, k in enumerate(OWN):
-            middle = bounce_ref.at[pl.ds(i * SEATS, SEATS)]
-            if way:
-                move = pltpu.make_async_copy(middle, out_ref.at[pl.ds(routes[k][0] * SEATS, SEATS)], local.at[i])
-            else:
-                move = pltpu.make_async_copy(in_ref.at[pl.ds(k * SEATS, SEATS)], middle, local.at[i])
-            move.start()
-            moves.append(move)
-        for move in moves:
-            move.wait()
-    for copy in copies:
-        copy.wait()
-
-
-def return_tiles(corrected):
-    return pl.pallas_call(
-        return_kernel,
-        out_shape=jax.ShapeDtypeStruct(corrected.shape, F32),
-        in_specs=[HBM],
-        out_specs=HBM,
-        scratch_shapes=[
-            pltpu.VMEM((4 * SEATS, 128), F32),
-            pltpu.SemaphoreType.DMA((SLOTS,)),
-            pltpu.SemaphoreType.DMA((SLOTS,)),
-            pltpu.SemaphoreType.DMA((4,)),
-        ],
-        compiler_params=params(collective_id=3, has_side_effects=True),
-        name="return_tiles",
-    )(corrected)
 
 
 def damped_solve(entries, target, order):
@@ -530,46 +483,6 @@
     )(normals)
 
 
-def pick_kernel(pix_ref, in_ref, table_ref, out_ref, update_ref):
-    row = lax.broadcasted_iota(jnp.int32, (8, 128), 0)
-    for p in range(PIX):
-        update_ref[:, p * 128:(p + 1) * 128] = table_ref[p * 5:p * 5 + 5, :]
-
-    def sender(b, _):
-        count = pix_ref[b, 127]
-
-        def group(g, _):
-            for j in range(8):
-                start = b * BLOCK_ROWS + (g * 8 + j) * FIELDS
-                v = in_ref[pl.ds(start, 8), :]
-                table = table_ref[pl.ds(pix_ref[b, g * 8 + j] * 5, 8), :]
-                within = (v - jnp.floor(v * (1.0 / SRC)) * SRC).astype(jnp.int32)
-                at = jnp.broadcast_to(lax.bitwise_and(within[6:7, :], 127), (8, 128))
-                picked = jnp.take_along_axis(table, at, axis=1)
-                terms = jnp.where(row < 5, v * picked, jnp.where(row == 5, -v, 0.0))
-                out_ref[pl.ds(b * SEATS + g * 8 + j, 1), :] = -jnp.sum(terms, axis=0, keepdims=True)
-            return 0
-
-        lax.fori_loop(0, lax.shift_right_logical(count + 7, 3), group, 0)
-        return 0
-
-    lax.fori_loop(0, SLOTS, sender, 0)
-
-
-def pick(pix, arrived, table):
-    return pl.pallas_call(
-        pick_kernel,
-        out_shape=(
-            jax.ShapeDtypeStruct((SLOTS * SEATS, 128), F32),
-            jax.ShapeDtypeStruct((5, PIX * SRC), F32),
-        ),
-        in_specs=[SMEM, VMEM, VMEM],
-        out_specs=(VMEM, VMEM),
-        compiler_params=params(),
-        name="pick",
-    )(pix, arrived, table)
-
-
 def knot_hits(knot_row, first):
     lane = lax.broadcasted_iota(jnp.int32, (SPAN, TILES), 0)
     return (lane == knot_row - first).astype(F32)
@@ -600,28 +513,99 @@
     out_ref[...] = total
 
 
-def finish_kernel(where_ref, knot_ref, first_ref, back_ref, w_ref, att_ref, quad_ref, hits_ref,
-                  out_ref, attitude_ref, settled_ref, edge_ref, head_ref, next_ref, piece_ref, pieces_ref,
-                  sent, landed):
+def apply_kernel(pix_ref, where_ref, first_ref, tiles_hbm, table_ref, knot_ref, w_ref, att_hbm, quad_ref, hits_ref,
+                 out_ref, attitude_ref, arr_ref, fixed_ref, back_ref, att_ref,
+                 settled_ref, edge_ref, head_ref, next_ref, piece_ref, pieces_ref,
+                 sent, landed, loaded, given, taken):
     tm, sky = lax.axis_index("tm"), lax.axis_index("sky")
+    y, zh, x, zl, c0 = place_of()
     block = tm * OWNERS + sky
     after = ((block + 1) // OWNERS % TIMES, (block + 1) % OWNERS)
     before = ((block + 127) // OWNERS % TIMES, (block + 127) % OWNERS)
     has_after, has_before = block < TIMES * OWNERS - 1, block > 0
     peers = [(tm, (sky + d) % OWNERS) for d in range(1, OWNERS)]
-    barrier = pltpu.get_barrier_semaphore()
+    parts = 8
+    size = SLOTS // parts * ROOM
+
+    def load(part):
+        rows = pl.ds(part * size, size)
+        return pltpu.make_async_copy(tiles_hbm.at[rows], arr_ref.at[rows], loaded.at[part])
+
+    for part in range(parts):
+        load(part).start()
+    load_att = pltpu.make_async_copy(att_hbm, att_ref, loaded.at[parts])
+    load_att.start()
     edge_ref[1] = jnp.zeros((8, 128), F32)
     next_ref[...] = jnp.zeros((4, 8, 128), F32)
-    for peer in peers + [after, before]:
-        pl.semaphore_signal(barrier, inc=1, device_id=peer, device_id_type=pl.DeviceIdType.MESH)
+    greet(peers + [after, before] + [to for k, (_, to) in enumerate(routes_of()) if k not in OWN])
+
+    def give(k):
+        m, plan, dc, h = k // 8, k // 4 % 2, k // 2 % 2, k % 2
+        d, dz = m % 4, m // 4
+        far = ((1 - plan) * x + plan * y + 4 - d) % 4
+        y_to, x_to = (1 - plan) * y + plan * far, (1 - plan) * far + plan * x
+        to = device_of(y_to, (zh + dz * h) % 2, x_to, (zl + dz) % 2, (c0 + dc) % 2)
+        seat = plan * 2 * OWNERS + (((1 - plan) * x + plan * y) * 4 + zl * 2 + c0) * 2 + h
+        return pltpu.make_async_remote_copy(
+            src_ref=fixed_ref.at[pl.ds(k * SEATS, SEATS)], dst_ref=back_ref.at[pl.ds(seat * SEATS, SEATS)],
+            send_sem=given.at[k], recv_sem=taken.at[k], device_id=to, device_id_type=pl.DeviceIdType.MESH), seat
+
+    def is_own(k):
+        return jnp.logical_and(k < 8, k // 2 % 2 == 0)
+
+    def pass_on(k):
+        copy, seat = give(k)
+
+        @pl.when(jnp.logical_not(is_own(k)))
+        def _():
+            copy.start()
+
+        @pl.when(is_own(k))
+        def _():
+            back_ref[pl.ds(seat * SEATS, SEATS), :] = fixed_ref[pl.ds(k * SEATS, SEATS), :]
+
+    row = lax.broadcasted_iota(jnp.int32, (8, 128), 0)
+
+    def pick(k, _):
+        @pl.when(k % (SLOTS // parts) == 0)
+        def _():
+            load(k // (SLOTS // parts)).wait()
+
+        for j in range(SEATS):
+            v = arr_ref[pl.ds(k * ROOM + j * FIELDS, 8), :]
+            table = table_ref[pl.ds(pix_ref[k, j] * 5, 8), :]
+            within = (v - jnp.floor(v * (1.0 / SRC)) * SRC).astype(jnp.int32)
+            at = jnp.broadcast_to(lax.bitwise_and(within[6:7, :], 127), (8, 128))
+            picked = jnp.take_along_axis(table, at, axis=1)
+            terms = jnp.where(row < 5, v * picked, jnp.where(row == 5, -v, 0.0))
+            fixed_ref[pl.ds(k * SEATS + j, 1), :] = -jnp.sum(terms, axis=0, keepdims=True)
+
+        @pl.when(k > 0)
+        def _():
+            pass_on(k - 1)
+
+        return 0
+
+    lax.fori_loop(0, SLOTS, pick, 0)
+    pass_on(SLOTS - 1)
+    load_att.wait()
+
+    def settle(k, _):
+        @pl.when(jnp.logical_not(is_own(k)))
+        def _():
+            give(k)[0].wait()
+
+        return 0
+
+    lax.fori_loop(0, SLOTS, settle, 0)
 
     def fetch(g, _):
-        for j in range(8):
-            t = g * 8 + j
+        for j in range(16):
+            t = g * 16 + j
             settled_ref[pl.ds(t, 1), :] = back_ref[pl.ds(where_ref[t], 1), :]
         return 0
 
-    lax.fori_loop(0, TILES // 8, fetch, 0)
+    lax.fori_loop(0, TILES // 16, fetch, 0)
     weight = w_ref[...]
     settled = settled_ref[...] / jnp.sqrt(weight)
     settled_ref[...] = settled
@@ -641,8 +625,6 @@
         shifted = pltpu.roll(pltpu.roll(padded, m, 0), 128 - 14 * m, 1)
         moved = moved + jnp.where(lane40 < 14, shifted, 0.0)
     edge_ref[0] = moved[SPAN:]
-    pl.semaphore_wait(barrier, OWNERS + 1)
-
     def onward(to):
         return pltpu.make_async_remote_copy(
             src_ref=edge_ref.at[0], dst_ref=edge_ref.at[1], send_sem=sent.at[0], recv_sem=landed.at[0],
@@ -720,16 +702,20 @@
         backward(before).wait_send()
 
 
-def finish(where, knots, first, back, weight, attitude, quad, hits):
+def apply_updates(pix, where, first, tiles, table, knots, weight, attitude, quad, hits):
     return pl.pallas_call(
-        finish_kernel,
+        apply_kernel,
         out_shape=(
             jax.ShapeDtypeStruct((TILES, 128), F32),
             jax.ShapeDtypeStruct((4, SPAN * OWNERS), F32),
         ),
-        in_specs=[SMEM, VMEM, SMEM, VMEM, VMEM, VMEM, VMEM, VMEM],
+        in_specs=[SMEM, SMEM, SMEM, HBM, VMEM, VMEM, VMEM, HBM, VMEM, VMEM],
         out_specs=(VMEM, VMEM),
         scratch_shapes=[
+            pltpu.VMEM((SLOTS * ROOM, 128), F32),
+            pltpu.VMEM((SLOTS * SEATS, 128), F32),
+            pltpu.VMEM((SLOTS * SEATS, 128), F32),
+            pltpu.VMEM((16, TILES, 128), F32),
             pltpu.VMEM((TILES, 128), F32),
             pltpu.VMEM((2, 8, 128), F32),
             pltpu.VMEM((4, 8, 128), F32),
@@ -738,10 +724,35 @@
             pltpu.VMEM((OWNERS, 8, 128), F32),
             pltpu.SemaphoreType.DMA((OWNERS + 1,)),
             pltpu.SemaphoreType.DMA((OWNERS + 1,)),
+            pltpu.SemaphoreType.DMA((9,)),
+            pltpu.SemaphoreType.DMA((SLOTS,)),
+            pltpu.SemaphoreType.DMA((SLOTS,)),
         ],
         compiler_params=params(collective_id=4, has_side_effects=True),
-        name="finish",
-    )(where, knots, first, back, weight, attitude, quad, hits)
+        name="apply_updates",
+    )(pix, where, first, tiles, table, knots, weight, attitude, quad, hits)
+
+
+def emit_kernel(final_ref, attitude_ref, table_ref, final_out, attitude_out, update_out):
+    final_out[...] = final_ref[...]
+    attitude_out[...] = attitude_ref[...]
+    for p in range(PIX):
+        update_out[:, p * 128:(p + 1) * 128] = table_ref[p * 5:p * 5 + 5, :]
+
+
+def emit(final, attitude, table):
+    return pl.pallas_call(
+        emit_kernel,
+        out_shape=(
+            jax.ShapeDtypeStruct((TILES, 128), F32),
+            jax.ShapeDtypeStruct((4, SPAN * OWNERS), F32),
+            jax.ShapeDtypeStruct((5, PIX * SRC), F32),
+        ),
+        in_specs=[VMEM, VMEM, VMEM],
+        out_specs=(VMEM, VMEM, VMEM),
+        compiler_params=params(),
+        name="emit",
+    )(final, attitude, table)
 
 
 def body(residual, obs_weight, source_partials, attitude_partials, source_index,
@@ -752,10 +763,9 @@
     packed, where = pack(tile_pixel, pixel_slot, residual, obs_weight, source_partials, source_index)
     arrived, normals, pix, quad, hits = gather_tiles(packed, attitude_partials, obs_weight, knots, first)
     table = reduce_and_solve(normals)
-    corrected, source_update = pick(pix, arrived, table)
-    back = return_tiles(corrected)
-    final, attitude_update = finish(
-        where, knots, first, back, obs_weight, attitude_partials, quad, hits)
+    final, attitude_update = apply_updates(
+        pix, where, first, arrived, table, knots, obs_weight, attitude_partials, quad, hits)
+    final, attitude_update, source_update = emit(final, attitude_update, table)
     return final, source_update, attitude_update
 
 

time: 178 us -> 165 us (0.927); the launches traced: 178 us -> 163 us
  Pallas kernels: 174 us -> 162 us
  local copies, waits for them, and re-layouts: 2.96 us -> 0 us
    pallas_call x4 -> x3, Pallas kernels: 114 us -> 97.9 us  [the longest x1 62 us: gather_tiles(): pl.pallas_call(gather_kernel, out_shape=(jax.ShapeDtypeStruct((SLOTS * RO...]
    pallas_call x1, Pallas kernels: 50.7 us -> 54.9 us  [reduce_and_solve(): pl.pallas_call(reduce_kernel, out_shape=jax.ShapeDtypeStruct((2 * PIX * 5...]
    unnamed x2 -> x0, local copies, waits for them, and re-layouts: 2.96 us -> none
where the time goes in v4:
time: 165 us; the launch traced here: 163 us
  Pallas kernels  162 us (98%)
    pallas_call x1, Pallas kernels, gather_tiles(): pl.pallas_call(gather_kernel, out_shape=(jax.ShapeDtypeStruct((SLOTS * RO...  62 us
    pallas_call x1, Pallas kernels, reduce_and_solve(): pl.pallas_call(reduce_kernel, out_shape=jax.ShapeDtypeStruct((2 * PIX * 5...  54.9 us
    pallas_call x1, Pallas kernels, apply_updates(): pl.pallas_call(apply_kernel, out_shape=(jax.ShapeDtypeStruct((TILES, 128)...  33.8 us
    pallas_call x1, Pallas kernels, pack(): pl.pallas_call(pack_kernel, out_shape=(jax.ShapeDtypeStruct((ROWS_IN, 128...  9.15 us

profile of v4, /device:TPU:8, one launch (start us, length us, event | category | flops | bytes accessed | tf_op | source)
XLA Modules:
  0.0 162.6 jit_solution(6396249204440447745)
XLA Ops:
  0.6 9.1 %pack.1 = (f32[10760,128]{1,0:T(8,128)}, s32[512]{0:T(512)}) custom-call(s32[512]{0:T(512)} %pixel_ref.1, s32[2048]{0:T(1024)} %slot_ref.1, f32[512,128]{1,0:T(8,128)} %res_ref.1, f32[512,128]{1,0:T(8,128)} %w_ref.3, f32[5,512,128]{2,1,0:T(8,128)} %part_ref.1, s32[512,128]{1,0:T(8,128)} %idx_ref.1), custom_call_target="tpu_custom_call" | custom-call | tf_op jit(solution)/shard_map/pack/pallas_call | solution.py:91
  9.8 62.0 %gather_tiles.1 = (f32[11264,128]{1,0:T(8,128)}, f32[2,2560,128]{2,1,0:T(8,128)}, s32[64,128]{1,0:T(8,128)}, f32[32,128]{1,0:T(8,128)}, bf16[512,128]{1,0:T(8,128)(2,1)}) custom-call(f32[10760,128]{1,0:T(8,128)} %get-tuple-element.15.in_ref, f32[16,512,128]{2,1,0:T(8,128)} %att_hbm.3, f32[512,128]{1,0:T(8,128)} %w_ref.3, s32[1,512]{1,0:T(1,128)} %bitcast.2, ...), custom_call_target="tpu_custom_call" | custom-call | tf_op jit(solution)/shard_map/gather_tiles/pallas_call | solution.py:290
  71.8 54.9 %reduce.1.table_ref = f32[1288,128]{1,0:T(8,128)} custom-call(f32[2,2560,128]{2,1,0:T(8,128)} %get-tuple-element.19.in_ref), custom_call_target="tpu_custom_call" | custom-call | tf_op jit(solution)/shard_map/reduce/pallas_call | solution.py:463
  126.7 33.8 %apply_updates.1 = (f32[512,128]{1,0:T(8,128)}, f32[4,512]{1,0:T(4,128)}) custom-call(s32[64,128]{1,0:T(8,128)} %get-tuple-element.16.pix_ref, s32[512]{0:T(512)} %get-tuple-element.17.where_ref, s32[1]{0:T(128)} %bitcast.1.first_ref, f32[11264,128]{1,0:T(8,128)} %get-tuple-element.18.tiles_hbm, f32[1288,128]{1,0:T(8,128)} %reduce.1.table_ref, ...), custom_call_target="tpu_custom_call" | custom-call | tf_op jit(solution)/shard_map/apply_updates/pallas_call | solution.py:706
  160.5 2.1 %emit.1 = (f32[512,128]{1,0:T(8,128)}, f32[4,512]{1,0:T(4,128)}, f32[5,16384]{1,0:T(8,128)}) custom-call(f32[512,128]{1,0:T(8,128)} %get-tuple-element.22.final_ref, f32[4,512]{1,0:T(4,128)} %get-tuple-element.23.attitude_ref, f32[1288,128]{1,0:T(8,128)} %reduce.1.table_ref), custom_call_target="tpu_custom_call" | custom-call | tf_op jit(solution)/shard_map/emit/pallas_call | solution.py:744

commit v5 on v4

--- a/solution.py
+++ b/solution.py
@@ -12,16 +12,14 @@
 PIX = 128
 SRC = 128
 FIELDS = 7
-CLASSES = 4
+CLASSES = 2
 SEATS = CAP // CLASSES
 SLOTS = OWNERS * CLASSES
 BLOCK_ROWS = SEATS * FIELDS
 ROWS_IN = SLOTS * BLOCK_ROWS + 8
 SPAN = 32
 TERMS = 20
-QUARTER = PIX // 4
 HALF = PIX // TIMES
-QROWS = QUARTER * TERMS
 HROWS = HALF * TERMS
 KNOT_PAIRS = tuple((c, e) for c in range(4) for e in range(c, 4))
 TERM_ROW = {
@@ -72,10 +70,8 @@
             owner = lax.shift_right_logical(seat, 7)
             rank = count_ref[owner]
             count_ref[owner] = rank + 1
-            plan = lax.bitwise_and(rank, 1)
-            half = lax.bitwise_and(lax.shift_right_logical(rank, 1), 1)
-            position = lax.shift_right_logical(rank, 2)
-            block = plan * (2 * OWNERS) + owner * 2 + half
+            block = owner * CLASSES + lax.bitwise_and(rank, 1)
+            position = lax.shift_right_logical(rank, 1)
             where_ref[t] = block * SEATS + position
             base = block * BLOCK_ROWS + position * FIELDS
             for f in range(6):
@@ -126,11 +122,11 @@
     pl.semaphore_wait(barrier, len(devices))
 
 
-MOVES = [(plan, m % 4, m // 4, dc, h)
-         for m in range(8) for plan in range(2) for dc in range(2) for h in range(2)]
-OWN = (0, 1, 4, 5)
-CHUNK = 4
+MOVES = [(m % 4, m // 4, dc, h) for m in range(8) for dc in range(2) for h in range(2)]
+OWN = (0, 1)
+CHUNK = 2
 CHUNKS = SLOTS // CHUNK
+STEP = 24
 PITCH = 136
 ROOM = BLOCK_ROWS + 8
 HBM = pl.BlockSpec(memory_space=pltpu.HBM)
@@ -139,12 +135,10 @@
 def routes_of():
     y, zh, x, zl, c = place_of()
     routes = []
-    for plan, d, dz, dc, h in MOVES:
-        far = ((y if plan else x) + d) % 4
-        zl_to, c_to, zh_to = (zl + dz) % 2, (c + dc) % 2, (zh + dz * h) % 2
-        to = device_of(far, zh_to, x, zl_to, c_to) if plan else device_of(y, zh_to, far, zl_to, c_to)
+    for d, dz, dc, h in MOVES:
+        far, zl_to, c_to = (x + d) % 4, (zl + dz) % 2, (c + dc) % 2
         owner = far * 4 + zl_to * 2 + c_to
-        routes.append((plan * 2 * OWNERS + owner * 2 + h, to))
+        routes.append((owner * CLASSES + h, device_of(y, (zh + dz * h) % 2, far, zl_to, c_to)))
     return routes
 
 
@@ -198,8 +192,7 @@
     lax.fori_loop(0, 24 * PITCH // 8, clear, 0, unroll=4)
 
     def clear_sums(g, _):
-        for plan in range(2):
-            sums_ref[plan, pl.ds(pl.multiple_of(g * 16, 16), 16), :] = jnp.zeros((16, 128), F32)
+        sums_ref[pl.ds(pl.multiple_of(g * 16, 16), 16), :] = jnp.zeros((16, 128), F32)
         return 0
 
     lax.fori_loop(0, PIX * TERMS // 16, clear_sums, 0, unroll=4)
@@ -219,21 +212,19 @@
                                      keep_ref.at[pl.ds(k * ROOM, BLOCK_ROWS)], stored.at[k])
 
     def chunk_step(chunk, _):
-        plan = chunk % 2
         for i in range(CHUNK):
             k = chunk * CHUNK + i
             arrival = landing(in_ref, arr_ref, sent, landed, k, routes[2][1])
-            if i < 2:
-                @pl.when(chunk >= 2)
-                def _():
-                    arrival.wait_recv()
-            else:
+
+            @pl.when(chunk >= 1)
+            def _():
                 arrival.wait_recv()
+
             keep(k).start()
 
         def group(g, _):
-            for j in range(0, SEATS, 2):
-                start = (chunk * CHUNK + g) * ROOM + j * FIELDS
+            for j in range(0, STEP, 2):
+                start = (chunk * CHUNK + g // 2) * ROOM + (g % 2 * STEP + j) * FIELDS
                 lefts, hits = [], []
                 for i in range(2):
                     v = arr_ref[pl.ds(start + i * FIELDS, 8), :]
@@ -247,19 +238,17 @@
                 for i in range(2):
                     both = out[48 * i:48 * i + 24] + out[48 * i + 24:48 * i + 48]
                     for n in range(3):
-                        spread_ref[pl.ds(8 * n * PITCH + g * SEATS + j + i, 8, stride=PITCH), :] = both[8 * n:8 * n + 8]
+                        spread_ref[pl.ds(8 * n * PITCH + g * STEP + j + i, 8, stride=PITCH), :] = both[8 * n:8 * n + 8]
             return 0
 
-        lax.fori_loop(0, CHUNK, group, 0)
+        lax.fori_loop(0, CHUNK * SEATS // STEP, group, 0)
         places = []
         for i in range(CHUNK):
             k = chunk * CHUNK + i
             whole = arr_ref[pl.ds(k * ROOM + 6, SEATS, stride=FIELDS), :]
             pixel = jnp.floor(whole * (1.0 / SRC)).astype(jnp.int32)
             places.append((pixel == pixels).astype(F32))
-            line = jnp.sum(jnp.where(pixels == seat_row, pixel + plan * PIX, 0), axis=0, keepdims=True)
-            count = jnp.sum((pixel >= 0).astype(jnp.int32), axis=0, keepdims=True)
-            line = jnp.where(pixels[:1] == 127, count, jnp.where(pixels[:1] < SEATS, line, 0))
+            line = jnp.sum(jnp.where(pixels == seat_row, pixel, 0), axis=0, keepdims=True)
             pix_ref[pl.ds(k, 1), :] = jnp.maximum(line, 0)
         places.append(jnp.zeros((128 - CHUNK * SEATS, 128), F32))
         place = jnp.concatenate(places, axis=0).T.astype(BF16)
@@ -272,7 +261,7 @@
             added = jnp.dot(place, jnp.concatenate([high, low], axis=0), preferred_element_type=F32)
             for part in range(TIMES):
                 rows = pl.ds(part * HROWS + n * HALF, HALF)
-                sums_ref[plan, rows, :] = sums_ref[plan, rows, :] + added[part * HALF:(part + 1) * HALF]
+                sums_ref[rows, :] = sums_ref[rows, :] + added[part * HALF:(part + 1) * HALF]
         return 0
 
     lax.fori_loop(0, CHUNKS, chunk_step, 0)
@@ -291,7 +280,7 @@
         gather_kernel,
         out_shape=(
             jax.ShapeDtypeStruct((SLOTS * ROOM, 128), F32),
-            jax.ShapeDtypeStruct((2, PIX * TERMS, 128), F32),
+            jax.ShapeDtypeStruct((PIX * TERMS, 128), F32),
             jax.ShapeDtypeStruct((SLOTS, 128), jnp.int32),
             jax.ShapeDtypeStruct((SPAN, 128), F32),
             jax.ShapeDtypeStruct((TILES, 128), BF16),
@@ -341,142 +330,55 @@
     return answer
 
 
-def add_rows(out, base, refs, rows):
-    def step(g, _):
-        at = pl.multiple_of(g * 16, 16)
-        total = None
-        for ref, start in refs:
-            value = ref[pl.ds(start + at, 16), :]
-            total = value if total is None else total + value
-        out[pl.ds(base + at, 16), :] = total
-        return 0
-
-    lax.fori_loop(0, rows // 16, step, 0)
-
-
-def reduce_kernel(in_ref, table_ref, first_ref, sum_ref, other_ref, whole_ref, own_ref,
-                  sent1, landed1, sent2, landed2, sent3, landed3):
+def reduce_kernel(in_ref, table_ref, parts_ref, whole_ref, own_ref, sent1, landed1, sent2, landed2):
     y, zh, x, zl, c = place_of()
     tm = y * 2 + zh
-    diagonal = x == y
-    greet([device_of((y + dy) % 4, (zh + dz) % 2, (x + dx) % 4, zl, c)
-           for dx in range(4) for dy in range(4) for dz in range(2) if (dx, dy, dz) != (0, 0, 0)])
+    peers = [((y + d) % 4, (zh + z) % 2) for d, z in ((2, 1), (2, 0), (1, 1), (3, 1), (1, 0), (3, 0), (0, 1))]
+    devices = [device_of(to_y, to_zh, x, zl, c) for to_y, to_zh in peers]
+    greet(devices)
     copies = []
-    for d in (2, 1, 3):
-        for plan in range(2):
-            far = ((x if plan else y) + d) % 4
-            to = device_of(y, zh, far, zl, c) if plan else device_of(far, zh, x, zl, c)
-            copies.append(send(in_ref.at[plan, pl.ds(far * QROWS, QROWS)], first_ref.at[plan, d - 1],
-                               sent1.at[plan, d - 1], landed1.at[plan, d - 1], to))
+    for i, (to_y, to_zh) in enumerate(peers):
+        copies.append(send(in_ref.at[pl.ds((to_y * 2 + to_zh) * HROWS, HROWS)], parts_ref.at[i],
+                           sent1.at[i], landed1.at[i], devices[i]))
     for copy in copies:
         copy.wait()
-    for plan in range(2):
-        near = (x if plan else y) * QROWS
-        add_rows(sum_ref.at[plan], 0,
-                 [(in_ref.at[plan], near)] + [(first_ref.at[plan, d], 0) for d in range(3)], QROWS)
-
-    @pl.when(diagonal)
-    def _():
-        add_rows(sum_ref.at[0], 0, [(sum_ref.at[0], 0), (sum_ref.at[1], 0)], QROWS)
-
-    across = send(sum_ref.at[0, pl.ds((1 - zh) * HROWS, HROWS)], other_ref.at[2], sent2.at[2], landed2.at[2],
-                  device_of(y, 1 - zh, x, zl, c))
-
-    @pl.when(diagonal)
-    def _():
-        def clear(g, _):
-            other_ref[0, pl.ds(pl.multiple_of(g * 16, 16), 16), :] = jnp.zeros((16, 128), F32)
-            other_ref[1, pl.ds(pl.multiple_of(g * 16, 16), 16), :] = jnp.zeros((16, 128), F32)
-            return 0
-
-        lax.fori_loop(0, HROWS // 16, clear, 0)
-
-    @pl.when(jnp.logical_not(diagonal))
-    def _():
-        flips = [send(sum_ref.at[1, pl.ds(z * HROWS, HROWS)], other_ref.at[zh], sent2.at[z], landed2.at[zh],
-                      device_of(x, z, y, zl, c)) for z in range(2)]
-        for z, flip in enumerate(flips):
-            flip.wait_send()
-            pltpu.make_async_remote_copy(
-                src_ref=sum_ref.at[1, pl.ds(z * HROWS, HROWS)], dst_ref=other_ref.at[z],
-                send_sem=sent2.at[z], recv_sem=landed2.at[z], device_id=device_of(x, z, y, zl, c),
-                device_id_type=pl.DeviceIdType.MESH).wait_recv()
-
-    across.wait()
-    add_rows(whole_ref, 0, [(sum_ref.at[0], zh * HROWS)] + [(other_ref.at[i], 0) for i in range(3)], HROWS)
+
+    def add(g, _):
+        rows = pl.ds(pl.multiple_of(g * 16, 16), 16)
+        total = in_ref[pl.ds(tm * HROWS + pl.multiple_of(g * 16, 16), 16), :]
+        for i in range(TIMES - 1):
+            total = total + parts_ref[i, rows, :]
+        whole_ref[rows, :] = total
+        return 0
+
+    lax.fori_loop(0, TERMS, add, 0, unroll=4)
     sums = [whole_ref[pl.ds(term * HALF, HALF), :] for term in range(TERMS)]
     entries = {key: sums[at] for key, at in TERM_ROW.items() if key[1] < 5}
     target = [sums[TERM_ROW[a, 5]] for a in range(5)]
     for a, value in enumerate(damped_solve(entries, target, 5)):
         own_ref[pl.ds(a, HALF, stride=5), :] = value
-    part = [pl.ds(plan * PIX * 5 + tm * HALF * 5, HALF * 5) for plan in range(2)]
-    copies = []
-    for d in (2, 1, 3, 0):
-        for z in (1, 0):
-            if (d, z) != (0, 0):
-                copies.append(send(own_ref, table_ref.at[part[0]], sent3.at[0, d * 2 + z], landed3.at[0, d * 2 + z],
-                                   device_of((y + d) % 4, (zh + z) % 2, x, zl, c)))
-    table_ref[part[0], :] = own_ref[...]
-
-    def spread(d, z):
-        return pltpu.make_async_remote_copy(
-            src_ref=own_ref, dst_ref=table_ref.at[part[1]], send_sem=sent3.at[1, d * 2 + z],
-            recv_sem=landed3.at[1, tm], device_id=device_of(x, (zh + z) % 2, (x + d) % 4, zl, c),
-            device_id_type=pl.DeviceIdType.MESH)
-
-    for d in (2, 1, 3, 0):
-        for z in (1, 0):
-            if (d, z) != (0, 0):
-                spread(d, z).start()
-
-    @pl.when(jnp.logical_not(diagonal))
-    def _():
-        spread(0, 0).start()
-
-    @pl.when(diagonal)
-    def _():
-        table_ref[part[1], :] = own_ref[...]
-
+    part = pl.ds(tm * HALF * 5, HALF * 5)
+    table_ref[part, :] = own_ref[...]
+    copies = [send(own_ref, table_ref.at[part], sent2.at[i], landed2.at[i], device)
+              for i, device in enumerate(devices)]
     for copy in copies:
         copy.wait()
-    for d in range(4):
-        for z in range(2):
-            if (d, z) != (0, 0):
-                spread(d, z).wait_send()
-
-    @pl.when(jnp.logical_not(diagonal))
-    def _():
-        spread(0, 0).wait_send()
-
-    for i in range(TIMES):
-        arrival = pltpu.make_async_remote_copy(
-            src_ref=own_ref, dst_ref=table_ref.at[pl.ds(PIX * 5 + i * HALF * 5, HALF * 5)], send_sem=sent3.at[1, 0],
-            recv_sem=landed3.at[1, i], device_id=device_of(i // 2, i % 2, y, zl, c),
-            device_id_type=pl.DeviceIdType.MESH)
-
-        @pl.when(jnp.logical_or(jnp.logical_not(diagonal), tm != i))
-        def _():
-            arrival.wait_recv()
 
 
 def reduce_and_solve(normals):
     return pl.pallas_call(
         reduce_kernel,
-        out_shape=jax.ShapeDtypeStruct((2 * PIX * 5 + 8, 128), F32),
+        out_shape=jax.ShapeDtypeStruct((PIX * 5 + 8, 128), F32),
         in_specs=[VMEM],
         out_specs=VMEM,
         scratch_shapes=[
-            pltpu.VMEM((2, 3, QROWS, 128), F32),
-            pltpu.VMEM((2, QROWS, 128), F32),
-            pltpu.VMEM((3, HROWS, 128), F32),
+            pltpu.VMEM((TIMES - 1, HROWS, 128), F32),
             pltpu.VMEM((HROWS, 128), F32),
             pltpu.VMEM((HALF * 5, 128), F32),
-            pltpu.SemaphoreType.DMA((2, 3)),
-            pltpu.SemaphoreType.DMA((2, 3)),
-            pltpu.SemaphoreType.DMA((3,)),
-            pltpu.SemaphoreType.DMA((3,)),
-            pltpu.SemaphoreType.DMA((2, 8)),
-            pltpu.SemaphoreType.DMA((2, 8)),
+            pltpu.SemaphoreType.DMA((TIMES - 1,)),
+            pltpu.SemaphoreType.DMA((TIMES - 1,)),
+            pltpu.SemaphoreType.DMA((TIMES - 1,)),
+            pltpu.SemaphoreType.DMA((TIMES - 1,)),
         ],
         compiler_params=params(collective_id=2, has_side_effects=True),
         name="reduce",
@@ -540,18 +442,16 @@
     greet(peers + [after, before] + [to for k, (_, to) in enumerate(routes_of()) if k not in OWN])
 
     def give(k):
-        m, plan, dc, h = k // 8, k // 4 % 2, k // 2 % 2, k % 2
-        d, dz = m % 4, m // 4
-        far = ((1 - plan) * x + plan * y + 4 - d) % 4
-        y_to, x_to = (1 - plan) * y + plan * far, (1 - plan) * far + plan * x
-        to = device_of(y_to, (zh + dz * h) % 2, x_to, (zl + dz) % 2, (c0 + dc) % 2)
-        seat = plan * 2 * OWNERS + (((1 - plan) * x + plan * y) * 4 + zl * 2 + c0) * 2 + h
+        m, dc, h = k // 4, k // 2 % 2, k % 2
+        dz = m // 4
+        to = device_of(y, (zh + dz * h) % 2, (x + 4 - m % 4) % 4, (zl + dz) % 2, (c0 + dc) % 2)
+        seat = sky * CLASSES + h
         return pltpu.make_async_remote_copy(
             src_ref=fixed_ref.at[pl.ds(k * SEATS, SEATS)], dst_ref=back_ref.at[pl.ds(seat * SEATS, SEATS)],
             send_sem=given.at[k], recv_sem=taken.at[k], device_id=to, device_id_type=pl.DeviceIdType.MESH), seat
 
     def is_own(k):
-        return jnp.logical_and(k < 8, k // 2 % 2 == 0)
+        return k < 2
 
     def pass_on(k):
         copy, seat = give(k)
@@ -566,27 +466,29 @@
 
     row = lax.broadcasted_iota(jnp.int32, (8, 128), 0)
 
-    def pick(k, _):
-        @pl.when(k % (SLOTS // parts) == 0)
+    def pick(step, _):
+        k, first = step // 2, step % 2 * STEP
+
+        @pl.when(step % (2 * SLOTS // parts) == 0)
         def _():
-            load(k // (SLOTS // parts)).wait()
-
-        for j in range(SEATS):
-            v = arr_ref[pl.ds(k * ROOM + j * FIELDS, 8), :]
-            table = table_ref[pl.ds(pix_ref[k, j] * 5, 8), :]
+            load(step // (2 * SLOTS // parts)).wait()
+
+        for j in range(STEP):
+            v = arr_ref[pl.ds(k * ROOM + (first + j) * FIELDS, 8), :]
+            table = table_ref[pl.ds(pix_ref[k, first + j] * 5, 8), :]
             within = (v - jnp.floor(v * (1.0 / SRC)) * SRC).astype(jnp.int32)
             at = jnp.broadcast_to(lax.bitwise_and(within[6:7, :], 127), (8, 128))
             picked = jnp.take_along_axis(table, at, axis=1)
             terms = jnp.where(row < 5, v * picked, jnp.where(row == 5, -v, 0.0))
-            fixed_ref[pl.ds(k * SEATS + j, 1), :] = -jnp.sum(terms, axis=0, keepdims=True)
-
-        @pl.when(k > 0)
+            fixed_ref[pl.ds(k * SEATS + first + j, 1), :] = -jnp.sum(terms, axis=0, keepdims=True)
+
+        @pl.when(jnp.logical_and(first == 0, k > 0))
         def _():
             pass_on(k - 1)
 
         return 0
 
-    lax.fori_loop(0, SLOTS, pick, 0)
+    lax.fori_loop(0, 2 * SLOTS, pick, 0)
     pass_on(SLOTS - 1)
     load_att.wait()
 

time: 165 us -> 162 us (0.982)
  Pallas kernels: 162 us -> 159 us
    pallas_call x1, Pallas kernels: 54.9 us -> 29.7 us  [reduce_and_solve(): pl.pallas_call(reduce_kernel, out_shape=jax.ShapeDtypeStruct((PIX * 5 + 8...]
    pallas_call x1, Pallas kernels: 62 us -> 83.5 us  [gather_tiles(): pl.pallas_call(gather_kernel, out_shape=(jax.ShapeDtypeStruct((SLOTS * RO...]
    pallas_call x1, Pallas kernels: 33.8 us -> 35.5 us  [apply_updates(): pl.pallas_call(apply_kernel, out_shape=(jax.ShapeDtypeStruct((TILES, 128)...]
where the time goes in v5:
time: 162 us; the launch traced here: 160 us
  Pallas kernels  159 us (98%)
    pallas_call x1, Pallas kernels, gather_tiles(): pl.pallas_call(gather_kernel, out_shape=(jax.ShapeDtypeStruct((SLOTS * RO...  83.5 us
    pallas_call x1, Pallas kernels, apply_updates(): pl.pallas_call(apply_kernel, out_shape=(jax.ShapeDtypeStruct((TILES, 128)...  35.5 us
    pallas_call x1, Pallas kernels, reduce_and_solve(): pl.pallas_call(reduce_kernel, out_shape=jax.ShapeDtypeStruct((PIX * 5 + 8...  29.7 us
    pallas_call x1, Pallas kernels, pack(): pl.pallas_call(pack_kernel, out_shape=(jax.ShapeDtypeStruct((ROWS_IN, 128...  8.58 us

profile of v5, /device:TPU:8, one launch (start us, length us, event | category | flops | bytes accessed | tf_op | source)
XLA Modules:
  0.0 160.0 jit_solution(161454076432748023)
XLA Ops:
  0.6 8.6 %pack.1 = (f32[10760,128]{1,0:T(8,128)}, s32[512]{0:T(512)}) custom-call(s32[512]{0:T(512)} %pixel_ref.1, s32[2048]{0:T(1024)} %slot_ref.1, f32[512,128]{1,0:T(8,128)} %res_ref.1, f32[512,128]{1,0:T(8,128)} %w_ref.3, f32[5,512,128]{2,1,0:T(8,128)} %part_ref.1, s32[512,128]{1,0:T(8,128)} %idx_ref.1), custom_call_target="tpu_custom_call" | custom-call | tf_op jit(solution)/shard_map/pack/pallas_call | solution.py:87
  9.2 83.5 %gather_tiles.1 = (f32[11008,128]{1,0:T(8,128)}, f32[2560,128]{1,0:T(8,128)}, s32[32,128]{1,0:T(8,128)}, f32[32,128]{1,0:T(8,128)}, bf16[512,128]{1,0:T(8,128)(2,1)}) custom-call(f32[10760,128]{1,0:T(8,128)} %get-tuple-element.15.in_ref, f32[16,512,128]{2,1,0:T(8,128)} %att_hbm.3, f32[512,128]{1,0:T(8,128)} %w_ref.3, s32[1,512]{1,0:T(1,128)} %bitcast.2, ...), custom_call_target="tpu_custom_call" | custom-call | tf_op jit(solution)/shard_map/gather_tiles/pallas_call | solution.py:279
  92.7 29.7 %reduce.1.table_ref = f32[648,128]{1,0:T(8,128)} custom-call(f32[2560,128]{1,0:T(8,128)} %get-tuple-element.19.in_ref), custom_call_target="tpu_custom_call" | custom-call | tf_op jit(solution)/shard_map/reduce/pallas_call | solution.py:369
  122.4 35.5 %apply_updates.1 = (f32[512,128]{1,0:T(8,128)}, f32[4,512]{1,0:T(4,128)}) custom-call(s32[32,128]{1,0:T(8,128)} %get-tuple-element.16.pix_ref, s32[512]{0:T(512)} %get-tuple-element.17.where_ref, s32[1]{0:T(128)} %bitcast.1.first_ref, f32[11008,128]{1,0:T(8,128)} %get-tuple-element.18.tiles_hbm, f32[648,128]{1,0:T(8,128)} %reduce.1.table_ref, ...), custom_call_target="tpu_custom_call" | custom-call | tf_op jit(solution)/shard_map/apply_updates/pallas_call | solution.py:608
  157.9 2.0 %emit.1 = (f32[512,128]{1,0:T(8,128)}, f32[4,512]{1,0:T(4,128)}, f32[5,16384]{1,0:T(8,128)}) custom-call(f32[512,128]{1,0:T(8,128)} %get-tuple-element.22.final_ref, f32[4,512]{1,0:T(4,128)} %get-tuple-element.23.attitude_ref, f32[648,128]{1,0:T(8,128)} %reduce.1.table_ref), custom_call_target="tpu_custom_call" | custom-call | tf_op jit(solution)/shard_map/emit/pallas_call | solution.py:646

commit v6 on v5

--- a/solution.py
+++ b/solution.py
@@ -122,7 +122,17 @@
     pl.semaphore_wait(barrier, len(devices))
 
 
-MOVES = [(m % 4, m // 4, dc, h) for m in range(8) for dc in range(2) for h in range(2)]
+def move_of(k):
+    far, step, turn = (k // 8 + 2) // 3, (k + 4) % 6, (k + 4) // 6 - 2
+    u = step // 2
+    d = far * (2 - u + 3 * (u // 2))
+    dz = far * (1 - step % 2) + (1 - far) * (k // 4)
+    dc = far * (turn // 2) + (1 - far) * (k // 2 % 2)
+    h = far * (turn % 2) + (1 - far) * (k % 2)
+    return d, dz, dc, h
+
+
+MOVES = [move_of(k) for k in range(SLOTS)]
 OWN = (0, 1)
 CHUNK = 2
 CHUNKS = SLOTS // CHUNK
@@ -330,12 +340,8 @@
     return answer
 
 
-def reduce_kernel(in_ref, table_ref, parts_ref, whole_ref, own_ref, sent1, landed1, sent2, landed2):
-    y, zh, x, zl, c = place_of()
-    tm = y * 2 + zh
-    peers = [((y + d) % 4, (zh + z) % 2) for d, z in ((2, 1), (2, 0), (1, 1), (3, 1), (1, 0), (3, 0), (0, 1))]
-    devices = [device_of(to_y, to_zh, x, zl, c) for to_y, to_zh in peers]
-    greet(devices)
+def reduce_and_solve(in_ref, table_ref, parts_ref, whole_ref, own_ref, peers, devices, tm,
+                     sent1, landed1, sent2, landed2):
     copies = []
     for i, (to_y, to_zh) in enumerate(peers):
         copies.append(send(in_ref.at[pl.ds((to_y * 2 + to_zh) * HROWS, HROWS)], parts_ref.at[i],
@@ -363,26 +369,6 @@
               for i, device in enumerate(devices)]
     for copy in copies:
         copy.wait()
-
-
-def reduce_and_solve(normals):
-    return pl.pallas_call(
-        reduce_kernel,
-        out_shape=jax.ShapeDtypeStruct((PIX * 5 + 8, 128), F32),
-        in_specs=[VMEM],
-        out_specs=VMEM,
-        scratch_shapes=[
-            pltpu.VMEM((TIMES - 1, HROWS, 128), F32),
-            pltpu.VMEM((HROWS, 128), F32),
-            pltpu.VMEM((HALF * 5, 128), F32),
-            pltpu.SemaphoreType.DMA((TIMES - 1,)),
-            pltpu.SemaphoreType.DMA((TIMES - 1,)),
-            pltpu.SemaphoreType.DMA((TIMES - 1,)),
-            pltpu.SemaphoreType.DMA((TIMES - 1,)),
-        ],
-        compiler_params=params(collective_id=2, has_side_effects=True),
-        name="reduce",
-    )(normals)
 
 
 def knot_hits(knot_row, first):
@@ -415,10 +401,10 @@
     out_ref[...] = total
 
 
-def apply_kernel(pix_ref, where_ref, first_ref, tiles_hbm, table_ref, knot_ref, w_ref, att_hbm, quad_ref, hits_ref,
-                 out_ref, attitude_ref, arr_ref, fixed_ref, back_ref, att_ref,
+def apply_kernel(pix_ref, where_ref, first_ref, normals_ref, tiles_hbm, knot_ref, w_ref, att_hbm, quad_ref, hits_ref,
+                 out_ref, attitude_ref, table_ref, parts_ref, whole_ref, own_ref, arr_ref, fixed_ref, back_ref, att_ref,
                  settled_ref, edge_ref, head_ref, next_ref, piece_ref, pieces_ref,
-                 sent, landed, loaded, given, taken):
+                 sent, landed, loaded, given, taken, sent1, landed1, sent2, landed2):
     tm, sky = lax.axis_index("tm"), lax.axis_index("sky")
     y, zh, x, zl, c0 = place_of()
     block = tm * OWNERS + sky
@@ -439,12 +425,15 @@
     load_att.start()
     edge_ref[1] = jnp.zeros((8, 128), F32)
     next_ref[...] = jnp.zeros((4, 8, 128), F32)
-    greet(peers + [after, before] + [to for k, (_, to) in enumerate(routes_of()) if k not in OWN])
+    times = [((y + d) % 4, (zh + z) % 2) for d, z in ((2, 1), (2, 0), (1, 1), (3, 1), (1, 0), (3, 0), (0, 1))]
+    shards = [device_of(to_y, to_zh, x, zl, c0) for to_y, to_zh in times]
+    greet(shards + peers + [after, before] + [to for k, (_, to) in enumerate(routes_of()) if k not in OWN])
+    reduce_and_solve(normals_ref, table_ref, parts_ref, whole_ref, own_ref, times, shards, tm,
+                     sent1, landed1, sent2, landed2)
 
     def give(k):
-        m, dc, h = k // 4, k // 2 % 2, k % 2
-        dz = m // 4
-        to = device_of(y, (zh + dz * h) % 2, (x + 4 - m % 4) % 4, (zl + dz) % 2, (c0 + dc) % 2)
+        d, dz, dc, h = move_of(k)
+        to = device_of(y, (zh + dz * h) % 2, (x + 4 - d) % 4, (zl + dz) % 2, (c0 + dc) % 2)
         seat = sky * CLASSES + h
         return pltpu.make_async_remote_copy(
             src_ref=fixed_ref.at[pl.ds(k * SEATS, SEATS)], dst_ref=back_ref.at[pl.ds(seat * SEATS, SEATS)],
@@ -604,16 +593,20 @@
         backward(before).wait_send()
 
 
-def apply_updates(pix, where, first, tiles, table, knots, weight, attitude, quad, hits):
+def apply_updates(pix, where, first, normals, tiles, knots, weight, attitude, quad, hits):
     return pl.pallas_call(
         apply_kernel,
         out_shape=(
             jax.ShapeDtypeStruct((TILES, 128), F32),
             jax.ShapeDtypeStruct((4, SPAN * OWNERS), F32),
+            jax.ShapeDtypeStruct((PIX * 5 + 8, 128), F32),
         ),
-        in_specs=[SMEM, SMEM, SMEM, HBM, VMEM, VMEM, VMEM, HBM, VMEM, VMEM],
-        out_specs=(VMEM, VMEM),
+        in_specs=[SMEM, SMEM, SMEM, VMEM, HBM, VMEM, VMEM, HBM, VMEM, VMEM],
+        out_specs=(VMEM, VMEM, VMEM),
         scratch_shapes=[
+            pltpu.VMEM((TIMES - 1, HROWS, 128), F32),
+            pltpu.VMEM((HROWS, 128), F32),
+            pltpu.VMEM((HALF * 5, 128), F32),
             pltpu.VMEM((SLOTS * ROOM, 128), F32),
             pltpu.VMEM((SLOTS * SEATS, 128), F32),
             pltpu.VMEM((SLOTS * SEATS, 128), F32),
@@ -629,10 +622,14 @@
             pltpu.SemaphoreType.DMA((9,)),
             pltpu.SemaphoreType.DMA((SLOTS,)),
             pltpu.SemaphoreType.DMA((SLOTS,)),
+            pltpu.SemaphoreType.DMA((TIMES - 1,)),
+            pltpu.SemaphoreType.DMA((TIMES - 1,)),
+            pltpu.SemaphoreType.DMA((TIMES - 1,)),
+            pltpu.SemaphoreType.DMA((TIMES - 1,)),
         ],
         compiler_params=params(collective_id=4, has_side_effects=True),
         name="apply_updates",
-    )(pix, where, first, tiles, table, knots, weight, attitude, quad, hits)
+    )(pix, where, first, normals, tiles, knots, weight, attitude, quad, hits)
 
 
 def emit_kernel(final_ref, attitude_ref, table_ref, final_out, attitude_out, update_out):
@@ -664,9 +661,8 @@
     knots = tile_knot.reshape(1, TILES)
     packed, where = pack(tile_pixel, pixel_slot, residual, obs_weight, source_partials, source_index)
     arrived, normals, pix, quad, hits = gather_tiles(packed, attitude_partials, obs_weight, knots, first)
-    table = reduce_and_solve(normals)
-    final, attitude_update = apply_updates(
-        pix, where, first, arrived, table, knots, obs_weight, attitude_partials, quad, hits)
+    final, attitude_update, table = apply_updates(
+        pix, where, first, normals, arrived, knots, obs_weight, attitude_partials, quad, hits)
     final, attitude_update, source_update = emit(final, attitude_update, table)
     return final, source_update, attitude_update
 

time: 162 us -> 146 us (0.901)
  Pallas kernels: 159 us -> 143 us
    pallas_call x1 -> x0, Pallas kernels: 29.7 us -> none  [reduce_and_solve(): pl.pallas_call(reduce_kernel, out_shape=jax.ShapeDtypeStruct((PIX * 5 + 8...]
    pallas_call x1, Pallas kernels: 35.5 us -> 55.3 us  [apply_updates(): pl.pallas_call(apply_kernel, out_shape=(jax.ShapeDtypeStruct((TILES, 128)...]
    pallas_call x1, Pallas kernels: 83.5 us -> 77.4 us  [gather_tiles(): pl.pallas_call(gather_kernel, out_shape=(jax.ShapeDtypeStruct((SLOTS * RO...]
where the time goes in v6:
time: 146 us; the launch traced here: 144 us
  Pallas kernels  143 us (98%)
    pallas_call x1, Pallas kernels, gather_tiles(): pl.pallas_call(gather_kernel, out_shape=(jax.ShapeDtypeStruct((SLOTS * RO...  77.4 us
    pallas_call x1, Pallas kernels, apply_updates(): pl.pallas_call(apply_kernel, out_shape=(jax.ShapeDtypeStruct((TILES, 128)...  55.3 us
    pallas_call x1, Pallas kernels, pack(): pl.pallas_call(pack_kernel, out_shape=(jax.ShapeDtypeStruct((ROWS_IN, 128...  8.47 us

profile of v6, /device:TPU:8, one launch (start us, length us, event | category | flops | bytes accessed | tf_op | source)
XLA Modules:
  0.0 143.9 jit_solution(12714925524624142116)
XLA Ops:
  0.6 8.5 %pack.1 = (f32[10760,128]{1,0:T(8,128)}, s32[512]{0:T(512)}) custom-call(s32[512]{0:T(512)} %pixel_ref.1, s32[2048]{0:T(1024)} %slot_ref.1, f32[512,128]{1,0:T(8,128)} %res_ref.1, f32[512,128]{1,0:T(8,128)} %w_ref.3, f32[5,512,128]{2,1,0:T(8,128)} %part_ref.1, s32[512,128]{1,0:T(8,128)} %idx_ref.1), custom_call_target="tpu_custom_call" | custom-call | tf_op jit(solution)/shard_map/pack/pallas_call | solution.py:87
  9.1 77.4 %gather_tiles.1 = (f32[11008,128]{1,0:T(8,128)}, f32[2560,128]{1,0:T(8,128)}, s32[32,128]{1,0:T(8,128)}, f32[32,128]{1,0:T(8,128)}, bf16[512,128]{1,0:T(8,128)(2,1)}) custom-call(f32[10760,128]{1,0:T(8,128)} %get-tuple-element.16.in_ref, f32[16,512,128]{2,1,0:T(8,128)} %att_hbm.3, f32[512,128]{1,0:T(8,128)} %w_ref.3, s32[1,512]{1,0:T(1,128)} %bitcast.2, ...), custom_call_target="tpu_custom_call" | custom-call | tf_op jit(solution)/shard_map/gather_tiles/pallas_call | solution.py:289
  86.5 55.3 %apply_updates.1 = (f32[512,128]{1,0:T(8,128)}, f32[4,512]{1,0:T(4,128)}, f32[648,128]{1,0:T(8,128)}) custom-call(s32[32,128]{1,0:T(8,128)} %get-tuple-element.17.pix_ref, s32[512]{0:T(512)} %get-tuple-element.18.where_ref, s32[1]{0:T(128)} %bitcast.1.first_ref, f32[2560,128]{1,0:T(8,128)} %get-tuple-element.19.normals_ref, ...), custom_call_target="tpu_custom_call" | custom-call | tf_op jit(solution)/shard_map/apply_updates/pallas_call | solution.py:597
  141.8 2.0 %emit.1 = (f32[512,128]{1,0:T(8,128)}, f32[4,512]{1,0:T(4,128)}, f32[5,16384]{1,0:T(8,128)}) custom-call(f32[512,128]{1,0:T(8,128)} %get-tuple-element.23.final_ref, f32[4,512]{1,0:T(4,128)} %get-tuple-element.24.attitude_ref, f32[648,128]{1,0:T(8,128)} %get-tuple-element.25.table_ref), custom_call_target="tpu_custom_call" | custom-call | tf_op jit(solution)/shard_map/emit/pallas_call | solution.py:643

commit v7 on v6

--- a/solution.py
+++ b/solution.py
@@ -123,17 +123,16 @@
 
 
 def move_of(k):
-    far, step, turn = (k // 8 + 2) // 3, (k + 4) % 6, (k + 4) // 6 - 2
-    u = step // 2
-    d = far * (2 - u + 3 * (u // 2))
-    dz = far * (1 - step % 2) + (1 - far) * (k // 4)
-    dc = far * (turn // 2) + (1 - far) * (k // 2 % 2)
-    h = far * (turn % 2) + (1 - far) * (k % 2)
-    return d, dz, dc, h
+    rest, near = k // 16, (k // 8 + 1) % 2 * (1 - k // 16)
+    d = rest * (1 + k % 2 * 2)
+    dz = rest * (1 - k // 2 % 2) + (1 - rest) * (k // 4 % 2)
+    dc = rest * (k // 8 % 2) + (1 - rest) * (k // 2 % 2)
+    h = rest * (k // 4 % 2) + (1 - rest) * (k % 2)
+    return d, dz, dc, h, near
 
 
 MOVES = [move_of(k) for k in range(SLOTS)]
-OWN = (0, 1)
+OWN = (0, 1, 8, 9)
 CHUNK = 2
 CHUNKS = SLOTS // CHUNK
 STEP = 24
@@ -145,11 +144,15 @@
 def routes_of():
     y, zh, x, zl, c = place_of()
     routes = []
-    for d, dz, dc, h in MOVES:
+    for d, dz, dc, h, pair in MOVES:
         far, zl_to, c_to = (x + d) % 4, (zl + dz) % 2, (c + dc) % 2
-        owner = far * 4 + zl_to * 2 + c_to
+        owner = (far + 2 * pair) % 4 * 4 + zl_to * 2 + c_to
         routes.append((owner * CLASSES + h, device_of(y, (zh + dz * h) % 2, far, zl_to, c_to)))
     return routes
+
+
+def times_of(y, zh):
+    return [((y + d) % 4, (zh + z) % 2) for d, z in ((2, 1), (2, 0), (1, 1), (3, 1), (1, 0), (3, 0), (0, 1))]
 
 
 def pair_products(v, row):
@@ -177,13 +180,19 @@
 
 def gather_kernel(in_ref, att_hbm, w_hbm, knot_ref, first_ref,
                   keep_ref, sums_ref, pix_ref, quad_ref, hits_ref,
-                  arr_ref, att_ref, w_ref, spread_ref, sent, landed, local, stored):
+                  arr_ref, att_ref, w_ref, spread_ref, parts_ref, pair_ref, across_ref,
+                  sent, landed, local, stored, sent1, landed1, sent2, landed2):
     routes = routes_of()
     load_att = pltpu.make_async_copy(att_hbm, att_ref, local.at[4])
     load_w = pltpu.make_async_copy(w_hbm, w_ref, local.at[5])
     load_att.start()
     load_w.start()
-    greet([to for k, (_, to) in enumerate(routes) if k not in OWN])
+    y, zh, x, zl, c = place_of()
+    tm = y * 2 + zh
+    times = times_of(y, zh)
+    partner = device_of(y, zh, (x + 2) % 4, zl, c)
+    shards = [device_of(to_y, to_zh, x, zl, c) for to_y, to_zh in times]
+    greet([to for k, (_, to) in enumerate(routes) if k not in OWN] + shards + [partner])
     copies = []
     for k, (block, to) in enumerate(routes):
         if k not in OWN:
@@ -205,7 +214,7 @@
         sums_ref[pl.ds(pl.multiple_of(g * 16, 16), 16), :] = jnp.zeros((16, 128), F32)
         return 0
 
-    lax.fori_loop(0, PIX * TERMS // 16, clear_sums, 0, unroll=4)
+    lax.fori_loop(0, 2 * PIX * TERMS // 16, clear_sums, 0, unroll=4)
     load_att.wait()
     load_w.wait()
     quad_sums(knot_ref, first_ref, w_ref, att_ref, quad_ref, hits_ref)
@@ -221,12 +230,49 @@
         return pltpu.make_async_copy(arr_ref.at[pl.ds(k * ROOM, BLOCK_ROWS)],
                                      keep_ref.at[pl.ds(k * ROOM, BLOCK_ROWS)], stored.at[k])
 
+    def part_copy(i):
+        to_y, to_zh = times[i]
+        return pltpu.make_async_remote_copy(
+            src_ref=sums_ref.at[pl.ds(PIX * TERMS + (to_y * 2 + to_zh) * HROWS, HROWS)], dst_ref=parts_ref.at[i],
+            send_sem=sent1.at[i], recv_sem=landed1.at[i], device_id=shards[i], device_id_type=pl.DeviceIdType.MESH)
+
+    def cross():
+        return pltpu.make_async_remote_copy(
+            src_ref=pair_ref, dst_ref=across_ref, send_sem=sent2.at[0], recv_sem=landed2.at[0],
+            device_id=partner, device_id_type=pl.DeviceIdType.MESH)
+
     def chunk_step(chunk, _):
+        pair = 1 - (chunk // 4 + 3) // 4
+
+        @pl.when(chunk == 5)
+        def _():
+            for i in range(TIMES - 1):
+                part_copy(i).start()
+
+        @pl.when(chunk == 12)
+        def _():
+            for i in range(TIMES - 1):
+                part_copy(i).wait()
+
+            def add(g, _):
+                at = pl.multiple_of(g * 16, 16)
+                total = sums_ref[pl.ds(PIX * TERMS + tm * HROWS + at, 16), :]
+                for i in range(TIMES - 1):
+                    total = total + parts_ref[i, pl.ds(at, 16), :]
+                pair_ref[pl.ds(at, 16), :] = total
+                return 0
+
+            lax.fori_loop(0, TERMS, add, 0)
+
+        @pl.when(chunk == 13)
+        def _():
+            cross().start()
+
         for i in range(CHUNK):
             k = chunk * CHUNK + i
             arrival = landing(in_ref, arr_ref, sent, landed, k, routes[2][1])
 
-            @pl.when(chunk >= 1)
+            @pl.when(jnp.logical_and(chunk != 0, chunk != 4))
             def _():
                 arrival.wait_recv()
 
@@ -259,7 +305,7 @@
             pixel = jnp.floor(whole * (1.0 / SRC)).astype(jnp.int32)
             places.append((pixel == pixels).astype(F32))
             line = jnp.sum(jnp.where(pixels == seat_row, pixel, 0), axis=0, keepdims=True)
-            pix_ref[pl.ds(k, 1), :] = jnp.maximum(line, 0)
+            pix_ref[pl.ds(k, 1), :] = jnp.maximum(line, 0) + pair * PIX
         places.append(jnp.zeros((128 - CHUNK * SEATS, 128), F32))
         place = jnp.concatenate(places, axis=0).T.astype(BF16)
         place = jnp.concatenate([place, place], axis=1)
@@ -270,11 +316,20 @@
             low = (value - high.astype(F32)).astype(BF16)
             added = jnp.dot(place, jnp.concatenate([high, low], axis=0), preferred_element_type=F32)
             for part in range(TIMES):
-                rows = pl.ds(part * HROWS + n * HALF, HALF)
+                rows = pl.ds(pair * (PIX * TERMS) + part * HROWS + n * HALF, HALF)
                 sums_ref[rows, :] = sums_ref[rows, :] + added[part * HALF:(part + 1) * HALF]
         return 0
 
     lax.fori_loop(0, CHUNKS, chunk_step, 0)
+    cross().wait()
+
+    def take(g, _):
+        at = pl.multiple_of(g * 16, 16)
+        rows = pl.ds(tm * HROWS + at, 16)
+        sums_ref[rows, :] = sums_ref[rows, :] + across_ref[pl.ds(at, 16), :]
+        return 0
+
+    lax.fori_loop(0, TERMS, take, 0)
     for copy in copies:
         copy.wait_send()
 
@@ -290,7 +345,7 @@
         gather_kernel,
         out_shape=(
             jax.ShapeDtypeStruct((SLOTS * ROOM, 128), F32),
-            jax.ShapeDtypeStruct((PIX * TERMS, 128), F32),
+            jax.ShapeDtypeStruct((2 * PIX * TERMS, 128), F32),
             jax.ShapeDtypeStruct((SLOTS, 128), jnp.int32),
             jax.ShapeDtypeStruct((SPAN, 128), F32),
             jax.ShapeDtypeStruct((TILES, 128), BF16),
@@ -302,10 +357,17 @@
             pltpu.VMEM((16, TILES, 128), F32),
             pltpu.VMEM((TILES, 128), F32),
             pltpu.VMEM((24 * PITCH, 128), F32),
+            pltpu.VMEM((TIMES - 1, HROWS, 128), F32),
+            pltpu.VMEM((HROWS, 128), F32),
+            pltpu.VMEM((HROWS, 128), F32),
             pltpu.SemaphoreType.DMA((SLOTS,)),
             pltpu.SemaphoreType.DMA((SLOTS,)),
             pltpu.SemaphoreType.DMA((6,)),
             pltpu.SemaphoreType.DMA((SLOTS,)),
+            pltpu.SemaphoreType.DMA((TIMES - 1,)),
+            pltpu.SemaphoreType.DMA((TIMES - 1,)),
+            pltpu.SemaphoreType.DMA((1,)),
+            pltpu.SemaphoreType.DMA((1,)),
         ],
         compiler_params=params(collective_id=1, has_side_effects=True),
         name="gather_tiles",
@@ -340,7 +402,7 @@
     return answer
 
 
-def reduce_and_solve(in_ref, table_ref, parts_ref, whole_ref, own_ref, peers, devices, tm,
+def reduce_and_solve(in_ref, table_ref, parts_ref, whole_ref, own_ref, peers, devices, opposite, tm,
                      sent1, landed1, sent2, landed2):
     copies = []
     for i, (to_y, to_zh) in enumerate(peers):
@@ -365,8 +427,12 @@
         own_ref[pl.ds(a, HALF, stride=5), :] = value
     part = pl.ds(tm * HALF * 5, HALF * 5)
     table_ref[part, :] = own_ref[...]
-    copies = [send(own_ref, table_ref.at[part], sent2.at[i], landed2.at[i], device)
-              for i, device in enumerate(devices)]
+    pair = pl.ds(PIX * 5 + tm * HALF * 5, HALF * 5)
+    copies = []
+    for i, device in enumerate(opposite):
+        copies.append(send(own_ref, table_ref.at[pair], sent2.at[TIMES + i], landed2.at[TIMES + i], device))
+        if i < TIMES - 1:
+            copies.append(send(own_ref, table_ref.at[part], sent2.at[i], landed2.at[i], devices[i]))
     for copy in copies:
         copy.wait()
 
@@ -401,8 +467,8 @@
     out_ref[...] = total
 
 
-def apply_kernel(pix_ref, where_ref, first_ref, normals_ref, tiles_hbm, knot_ref, w_ref, att_hbm, quad_ref, hits_ref,
-                 out_ref, attitude_ref, table_ref, parts_ref, whole_ref, own_ref, arr_ref, fixed_ref, back_ref, att_ref,
+def apply_kernel(pix_ref, where_ref, first_ref, normals_hbm, tiles_hbm, knot_ref, w_ref, att_hbm, quad_ref, hits_ref,
+                 out_ref, attitude_ref, table_ref, normals_ref, parts_ref, whole_ref, own_ref, arr_ref, fixed_ref, back_ref, att_ref,
                  settled_ref, edge_ref, head_ref, next_ref, piece_ref, pieces_ref,
                  sent, landed, loaded, given, taken, sent1, landed1, sent2, landed2):
     tm, sky = lax.axis_index("tm"), lax.axis_index("sky")
@@ -419,28 +485,33 @@
         rows = pl.ds(part * size, size)
         return pltpu.make_async_copy(tiles_hbm.at[rows], arr_ref.at[rows], loaded.at[part])
 
+    load_sums = pltpu.make_async_copy(normals_hbm.at[pl.ds(0, PIX * TERMS)], normals_ref, loaded.at[parts + 1])
+    load_sums.start()
     for part in range(parts):
         load(part).start()
     load_att = pltpu.make_async_copy(att_hbm, att_ref, loaded.at[parts])
     load_att.start()
     edge_ref[1] = jnp.zeros((8, 128), F32)
     next_ref[...] = jnp.zeros((4, 8, 128), F32)
-    times = [((y + d) % 4, (zh + z) % 2) for d, z in ((2, 1), (2, 0), (1, 1), (3, 1), (1, 0), (3, 0), (0, 1))]
+    times = times_of(y, zh)
+    others = times + [(y, zh)]
+    opposite = [device_of(to_y, to_zh, (x + 2) % 4, zl, c0) for to_y, to_zh in others]
     shards = [device_of(to_y, to_zh, x, zl, c0) for to_y, to_zh in times]
-    greet(shards + peers + [after, before] + [to for k, (_, to) in enumerate(routes_of()) if k not in OWN])
-    reduce_and_solve(normals_ref, table_ref, parts_ref, whole_ref, own_ref, times, shards, tm,
+    greet(shards + opposite + peers + [after, before] + [to for k, (_, to) in enumerate(routes_of()) if k not in OWN])
+    load_sums.wait()
+    reduce_and_solve(normals_ref, table_ref, parts_ref, whole_ref, own_ref, times, shards, opposite, tm,
                      sent1, landed1, sent2, landed2)
 
     def give(k):
-        d, dz, dc, h = move_of(k)
+        d, dz, dc, h, pair = move_of(k)
         to = device_of(y, (zh + dz * h) % 2, (x + 4 - d) % 4, (zl + dz) % 2, (c0 + dc) % 2)
-        seat = sky * CLASSES + h
+        seat = ((x + 2 * pair) % 4 * 4 + zl * 2 + c0) * CLASSES + h
         return pltpu.make_async_remote_copy(
             src_ref=fixed_ref.at[pl.ds(k * SEATS, SEATS)], dst_ref=back_ref.at[pl.ds(seat * SEATS, SEATS)],
             send_sem=given.at[k], recv_sem=taken.at[k], device_id=to, device_id_type=pl.DeviceIdType.MESH), seat
 
     def is_own(k):
-        return k < 2
+        return jnp.logical_and(k < 16, k % 8 < 2)
 
     def pass_on(k):
         copy, seat = give(k)
@@ -599,11 +670,12 @@
         out_shape=(
             jax.ShapeDtypeStruct((TILES, 128), F32),
             jax.ShapeDtypeStruct((4, SPAN * OWNERS), F32),
-            jax.ShapeDtypeStruct((PIX * 5 + 8, 128), F32),
+            jax.ShapeDtypeStruct((2 * PIX * 5 + 8, 128), F32),
         ),
-        in_specs=[SMEM, SMEM, SMEM, VMEM, HBM, VMEM, VMEM, HBM, VMEM, VMEM],
+        in_specs=[SMEM, SMEM, SMEM, HBM, HBM, VMEM, VMEM, HBM, VMEM, VMEM],
         out_specs=(VMEM, VMEM, VMEM),
         scratch_shapes=[
+            pltpu.VMEM((PIX * TERMS, 128), F32),
             pltpu.VMEM((TIMES - 1, HROWS, 128), F32),
             pltpu.VMEM((HROWS, 128), F32),
             pltpu.VMEM((HALF * 5, 128), F32),
@@ -619,13 +691,13 @@
             pltpu.VMEM((OWNERS, 8, 128), F32),
             pltpu.SemaphoreType.DMA((OWNERS + 1,)),
             pltpu.SemaphoreType.DMA((OWNERS + 1,)),
-            pltpu.SemaphoreType.DMA((9,)),
+            pltpu.SemaphoreType.DMA((10,)),
             pltpu.SemaphoreType.DMA((SLOTS,)),
             pltpu.SemaphoreType.DMA((SLOTS,)),
             pltpu.SemaphoreType.DMA((TIMES - 1,)),
             pltpu.SemaphoreType.DMA((TIMES - 1,)),
-            pltpu.SemaphoreType.DMA((TIMES - 1,)),
-            pltpu.SemaphoreType.DMA((TIMES - 1,)),
+            pltpu.SemaphoreType.DMA((2 * TIMES,)),
+            pltpu.SemaphoreType.DMA((2 * TIMES,)),
         ],
         compiler_params=params(collective_id=4, has_side_effects=True),
         name="apply_updates",

time: 146 us -> 146 us (level)
    pallas_call x1, Pallas kernels: 55.3 us -> 62.4 us  [apply_updates(): pl.pallas_call(apply_kernel, out_shape=(jax.ShapeDtypeStruct((TILES, 128)...]
    pallas_call x1, Pallas kernels: 77.4 us -> 70.6 us  [gather_tiles(): pl.pallas_call(gather_kernel, out_shape=(jax.ShapeDtypeStruct((SLOTS * RO...]
where the time goes in v7:
time: 146 us; the launch traced here: 144 us
  Pallas kernels  144 us (99%)
    pallas_call x1, Pallas kernels, gather_tiles(): pl.pallas_call(gather_kernel, out_shape=(jax.ShapeDtypeStruct((SLOTS * RO...  70.6 us
    pallas_call x1, Pallas kernels, apply_updates(): pl.pallas_call(apply_kernel, out_shape=(jax.ShapeDtypeStruct((TILES, 128)...  62.4 us
    pallas_call x1, Pallas kernels, pack(): pl.pallas_call(pack_kernel, out_shape=(jax.ShapeDtypeStruct((ROWS_IN, 128...  8.61 us

profile of v7, /device:TPU:8, one launch (start us, length us, event | category | flops | bytes accessed | tf_op | source)
XLA Modules:
  0.0 144.4 jit_solution(16087344825994809193)
XLA Ops:
  0.6 8.6 %pack.1 = (f32[10760,128]{1,0:T(8,128)}, s32[512]{0:T(512)}) custom-call(s32[512]{0:T(512)} %pixel_ref.1, s32[2048]{0:T(1024)} %slot_ref.1, f32[512,128]{1,0:T(8,128)} %res_ref.1, f32[512,128]{1,0:T(8,128)} %w_ref.3, f32[5,512,128]{2,1,0:T(8,128)} %part_ref.1, s32[512,128]{1,0:T(8,128)} %idx_ref.1), custom_call_target="tpu_custom_call" | custom-call | tf_op jit(solution)/shard_map/pack/pallas_call | solution.py:87
  9.3 70.6 %gather_tiles.1 = (f32[11008,128]{1,0:T(8,128)}, f32[5120,128]{1,0:T(8,128)}, s32[32,128]{1,0:T(8,128)}, f32[32,128]{1,0:T(8,128)}, bf16[512,128]{1,0:T(8,128)(2,1)}) custom-call(f32[10760,128]{1,0:T(8,128)} %get-tuple-element.16.in_ref, f32[16,512,128]{2,1,0:T(8,128)} %att_hbm.3, f32[512,128]{1,0:T(8,128)} %w_ref.3, s32[1,512]{1,0:T(1,128)} %bitcast.2, ...), custom_call_target="tpu_custom_call" | custom-call | tf_op jit(solution)/shard_map/gather_tiles/pallas_call | solution.py:344
  79.8 62.4 %apply_updates.1 = (f32[512,128]{1,0:T(8,128)}, f32[4,512]{1,0:T(4,128)}, f32[1288,128]{1,0:T(8,128)}) custom-call(s32[32,128]{1,0:T(8,128)} %get-tuple-element.17.pix_ref, s32[512]{0:T(512)} %get-tuple-element.18.where_ref, s32[1]{0:T(128)} %bitcast.1.first_ref, f32[5120,128]{1,0:T(8,128)} %get-tuple-element.19.normals_hbm, ...), custom_call_target="tpu_custom_call" | custom-call | tf_op jit(solution)/shard_map/apply_updates/pallas_call | solution.py:668
  142.3 2.1 %emit.1 = (f32[512,128]{1,0:T(8,128)}, f32[4,512]{1,0:T(4,128)}, f32[5,16384]{1,0:T(8,128)}) custom-call(f32[512,128]{1,0:T(8,128)} %get-tuple-element.23.final_ref, f32[4,512]{1,0:T(4,128)} %get-tuple-element.24.attitude_ref, f32[1288,128]{1,0:T(8,128)} %get-tuple-element.25.table_ref), custom_call_target="tpu_custom_call" | custom-call | tf_op jit(solution)/shard_map/emit/pallas_call | solution.py:715

commit v8 on v7

--- a/solution.py
+++ b/solution.py
@@ -1,3 +1,5 @@
+import functools
+
 import jax
 import jax.numpy as jnp
 from jax import lax
@@ -188,10 +190,9 @@
     load_att.start()
     load_w.start()
     y, zh, x, zl, c = place_of()
-    tm = y * 2 + zh
-    times = times_of(y, zh)
+    rows_y = [(y + d) % 4 for d in (2, 1, 3)]
     partner = device_of(y, zh, (x + 2) % 4, zl, c)
-    shards = [device_of(to_y, to_zh, x, zl, c) for to_y, to_zh in times]
+    shards = [device_of(to_y, zh, x, zl, c) for to_y in rows_y]
     greet([to for k, (_, to) in enumerate(routes) if k not in OWN] + shards + [partner])
     copies = []
     for k, (block, to) in enumerate(routes):
@@ -231,9 +232,8 @@
                                      keep_ref.at[pl.ds(k * ROOM, BLOCK_ROWS)], stored.at[k])
 
     def part_copy(i):
-        to_y, to_zh = times[i]
         return pltpu.make_async_remote_copy(
-            src_ref=sums_ref.at[pl.ds(PIX * TERMS + (to_y * 2 + to_zh) * HROWS, HROWS)], dst_ref=parts_ref.at[i],
+            src_ref=sums_ref.at[pl.ds(PIX * TERMS + rows_y[i] * 2 * HROWS, 2 * HROWS)], dst_ref=parts_ref.at[i],
             send_sem=sent1.at[i], recv_sem=landed1.at[i], device_id=shards[i], device_id_type=pl.DeviceIdType.MESH)
 
     def cross():
@@ -246,25 +246,25 @@
 
         @pl.when(chunk == 5)
         def _():
-            for i in range(TIMES - 1):
+            for i in range(3):
                 part_copy(i).start()
 
-        @pl.when(chunk == 12)
+        @pl.when(chunk == 11)
         def _():
-            for i in range(TIMES - 1):
+            for i in range(3):
                 part_copy(i).wait()
 
             def add(g, _):
                 at = pl.multiple_of(g * 16, 16)
-                total = sums_ref[pl.ds(PIX * TERMS + tm * HROWS + at, 16), :]
-                for i in range(TIMES - 1):
+                total = sums_ref[pl.ds(PIX * TERMS + y * 2 * HROWS + at, 16), :]
+                for i in range(3):
                     total = total + parts_ref[i, pl.ds(at, 16), :]
                 pair_ref[pl.ds(at, 16), :] = total
                 return 0
 
-            lax.fori_loop(0, TERMS, add, 0)
-
-        @pl.when(chunk == 13)
+            lax.fori_loop(0, 2 * TERMS, add, 0)
+
+        @pl.when(chunk == 12)
         def _():
             cross().start()
 
@@ -305,7 +305,7 @@
             pixel = jnp.floor(whole * (1.0 / SRC)).astype(jnp.int32)
             places.append((pixel == pixels).astype(F32))
             line = jnp.sum(jnp.where(pixels == seat_row, pixel, 0), axis=0, keepdims=True)
-            pix_ref[pl.ds(k, 1), :] = jnp.maximum(line, 0) + pair * PIX
+            pix_ref[pl.ds(k, 1), :] = jnp.maximum(line, 0)
         places.append(jnp.zeros((128 - CHUNK * SEATS, 128), F32))
         place = jnp.concatenate(places, axis=0).T.astype(BF16)
         place = jnp.concatenate([place, place], axis=1)
@@ -325,11 +325,11 @@
 
     def take(g, _):
         at = pl.multiple_of(g * 16, 16)
-        rows = pl.ds(tm * HROWS + at, 16)
+        rows = pl.ds(y * 2 * HROWS + at, 16)
         sums_ref[rows, :] = sums_ref[rows, :] + across_ref[pl.ds(at, 16), :]
         return 0
 
-    lax.fori_loop(0, TERMS, take, 0)
+    lax.fori_loop(0, 2 * TERMS, take, 0)
     for copy in copies:
         copy.wait_send()
 
@@ -357,15 +357,15 @@
             pltpu.VMEM((16, TILES, 128), F32),
             pltpu.VMEM((TILES, 128), F32),
             pltpu.VMEM((24 * PITCH, 128), F32),
-            pltpu.VMEM((TIMES - 1, HROWS, 128), F32),
-            pltpu.VMEM((HROWS, 128), F32),
-            pltpu.VMEM((HROWS, 128), F32),
+            pltpu.VMEM((3, 2 * HROWS, 128), F32),
+            pltpu.VMEM((2 * HROWS, 128), F32),
+            pltpu.VMEM((2 * HROWS, 128), F32),
             pltpu.SemaphoreType.DMA((SLOTS,)),
             pltpu.SemaphoreType.DMA((SLOTS,)),
             pltpu.SemaphoreType.DMA((6,)),
             pltpu.SemaphoreType.DMA((SLOTS,)),
-            pltpu.SemaphoreType.DMA((TIMES - 1,)),
-            pltpu.SemaphoreType.DMA((TIMES - 1,)),
+            pltpu.SemaphoreType.DMA((3,)),
+            pltpu.SemaphoreType.DMA((3,)),
             pltpu.SemaphoreType.DMA((1,)),
             pltpu.SemaphoreType.DMA((1,)),
         ],
@@ -402,7 +402,7 @@
     return answer
 
 
-def reduce_and_solve(in_ref, table_ref, parts_ref, whole_ref, own_ref, peers, devices, opposite, tm,
+def reduce_and_solve(in_ref, table_ref, second_ref, parts_ref, whole_ref, own_ref, peers, devices, opposite, tm,
                      sent1, landed1, sent2, landed2):
     copies = []
     for i, (to_y, to_zh) in enumerate(peers):
@@ -427,14 +427,19 @@
         own_ref[pl.ds(a, HALF, stride=5), :] = value
     part = pl.ds(tm * HALF * 5, HALF * 5)
     table_ref[part, :] = own_ref[...]
-    pair = pl.ds(PIX * 5 + tm * HALF * 5, HALF * 5)
-    copies = []
-    for i, device in enumerate(opposite):
-        copies.append(send(own_ref, table_ref.at[pair], sent2.at[TIMES + i], landed2.at[TIMES + i], device))
-        if i < TIMES - 1:
-            copies.append(send(own_ref, table_ref.at[part], sent2.at[i], landed2.at[i], devices[i]))
+    copies = [send(own_ref, table_ref.at[part], sent2.at[i], landed2.at[i], device)
+              for i, device in enumerate(devices)]
+
+    def spread(i):
+        return pltpu.make_async_remote_copy(
+            src_ref=own_ref, dst_ref=second_ref.at[part], send_sem=sent2.at[TIMES + i], recv_sem=landed2.at[TIMES + i],
+            device_id=opposite[i], device_id_type=pl.DeviceIdType.MESH)
+
+    for i in range(TIMES):
+        spread(i).start()
     for copy in copies:
         copy.wait()
+    return spread
 
 
 def knot_hits(knot_row, first):
@@ -468,7 +473,7 @@
 
 
 def apply_kernel(pix_ref, where_ref, first_ref, normals_hbm, tiles_hbm, knot_ref, w_ref, att_hbm, quad_ref, hits_ref,
-                 out_ref, attitude_ref, table_ref, normals_ref, parts_ref, whole_ref, own_ref, arr_ref, fixed_ref, back_ref, att_ref,
+                 out_ref, attitude_ref, table_ref, second_ref, normals_ref, parts_ref, whole_ref, own_ref, arr_ref, fixed_ref, back_ref, att_ref,
                  settled_ref, edge_ref, head_ref, next_ref, piece_ref, pieces_ref,
                  sent, landed, loaded, given, taken, sent1, landed1, sent2, landed2):
     tm, sky = lax.axis_index("tm"), lax.axis_index("sky")
@@ -488,7 +493,7 @@
     load_sums = pltpu.make_async_copy(normals_hbm.at[pl.ds(0, PIX * TERMS)], normals_ref, loaded.at[parts + 1])
     load_sums.start()
     for part in range(parts):
-        load(part).start()
+        load((part + 2) % parts).start()
     load_att = pltpu.make_async_copy(att_hbm, att_ref, loaded.at[parts])
     load_att.start()
     edge_ref[1] = jnp.zeros((8, 128), F32)
@@ -499,8 +504,8 @@
     shards = [device_of(to_y, to_zh, x, zl, c0) for to_y, to_zh in times]
     greet(shards + opposite + peers + [after, before] + [to for k, (_, to) in enumerate(routes_of()) if k not in OWN])
     load_sums.wait()
-    reduce_and_solve(normals_ref, table_ref, parts_ref, whole_ref, own_ref, times, shards, opposite, tm,
-                     sent1, landed1, sent2, landed2)
+    spread = reduce_and_solve(normals_ref, table_ref, second_ref, parts_ref, whole_ref, own_ref, times, shards, opposite, tm,
+                              sent1, landed1, sent2, landed2)
 
     def give(k):
         d, dz, dc, h, pair = move_of(k)
@@ -526,30 +531,33 @@
 
     row = lax.broadcasted_iota(jnp.int32, (8, 128), 0)
 
-    def pick(step, _):
-        k, first = step // 2, step % 2 * STEP
+    def pick(rows_ref, step, _):
+        k, first = (step // 2 + 8) % SLOTS, step % 2 * STEP
 
         @pl.when(step % (2 * SLOTS // parts) == 0)
         def _():
-            load(step // (2 * SLOTS // parts)).wait()
+            load(k // (SLOTS // parts)).wait()
 
         for j in range(STEP):
             v = arr_ref[pl.ds(k * ROOM + (first + j) * FIELDS, 8), :]
-            table = table_ref[pl.ds(pix_ref[k, first + j] * 5, 8), :]
+            table = rows_ref[pl.ds(pix_ref[k, first + j] * 5, 8), :]
             within = (v - jnp.floor(v * (1.0 / SRC)) * SRC).astype(jnp.int32)
             at = jnp.broadcast_to(lax.bitwise_and(within[6:7, :], 127), (8, 128))
             picked = jnp.take_along_axis(table, at, axis=1)
             terms = jnp.where(row < 5, v * picked, jnp.where(row == 5, -v, 0.0))
             fixed_ref[pl.ds(k * SEATS + first + j, 1), :] = -jnp.sum(terms, axis=0, keepdims=True)
 
-        @pl.when(jnp.logical_and(first == 0, k > 0))
+        @pl.when(jnp.logical_and(first == 0, step > 0))
         def _():
-            pass_on(k - 1)
-
-        return 0
-
-    lax.fori_loop(0, 2 * SLOTS, pick, 0)
-    pass_on(SLOTS - 1)
+            pass_on((k + SLOTS - 1) % SLOTS)
+
+        return 0
+
+    lax.fori_loop(0, 2 * (SLOTS - 8), functools.partial(pick, table_ref), 0)
+    for i in range(TIMES):
+        spread(i).wait()
+    lax.fori_loop(2 * (SLOTS - 8), 2 * SLOTS, functools.partial(pick, second_ref), 0)
+    pass_on(7)
     load_att.wait()
 
     def settle(k, _):
@@ -670,11 +678,12 @@
         out_shape=(
             jax.ShapeDtypeStruct((TILES, 128), F32),
             jax.ShapeDtypeStruct((4, SPAN * OWNERS), F32),
-            jax.ShapeDtypeStruct((2 * PIX * 5 + 8, 128), F32),
+            jax.ShapeDtypeStruct((PIX * 5 + 8, 128), F32),
         ),
         in_specs=[SMEM, SMEM, SMEM, HBM, HBM, VMEM, VMEM, HBM, VMEM, VMEM],
         out_specs=(VMEM, VMEM, VMEM),
         scratch_shapes=[
+            pltpu.VMEM((PIX * 5 + 8, 128), F32),
             pltpu.VMEM((PIX * TERMS, 128), F32),
             pltpu.VMEM((TIMES - 1, HROWS, 128), F32),
             pltpu.VMEM((HROWS, 128), F32),

time: 146 us -> 134 us (0.918)
  Pallas kernels: 144 us -> 132 us
    pallas_call x1, Pallas kernels: 70.6 us -> 61.4 us  [gather_tiles(): pl.pallas_call(gather_kernel, out_shape=(jax.ShapeDtypeStruct((SLOTS * RO...]
    pallas_call x1, Pallas kernels: 62.4 us -> 60.1 us  [apply_updates(): pl.pallas_call(apply_kernel, out_shape=(jax.ShapeDtypeStruct((TILES, 128)...]
where the time goes in v8:
time: 134 us; the launch traced here: 133 us
  Pallas kernels  132 us (99%)
    pallas_call x1, Pallas kernels, gather_tiles(): pl.pallas_call(gather_kernel, out_shape=(jax.ShapeDtypeStruct((SLOTS * RO...  61.4 us
    pallas_call x1, Pallas kernels, apply_updates(): pl.pallas_call(apply_kernel, out_shape=(jax.ShapeDtypeStruct((TILES, 128)...  60.1 us
    pallas_call x1, Pallas kernels, pack(): pl.pallas_call(pack_kernel, out_shape=(jax.ShapeDtypeStruct((ROWS_IN, 128...  8.61 us

profile of v8, /device:TPU:8, one launch (start us, length us, event | category | flops | bytes accessed | tf_op | source)
XLA Modules:
  0.0 132.7 jit_solution(14786570133566533596)
XLA Ops:
  0.6 8.6 %pack.1 = (f32[10760,128]{1,0:T(8,128)}, s32[512]{0:T(512)}) custom-call(s32[512]{0:T(512)} %pixel_ref.1, s32[2048]{0:T(1024)} %slot_ref.1, f32[512,128]{1,0:T(8,128)} %res_ref.1, f32[512,128]{1,0:T(8,128)} %w_ref.3, f32[5,512,128]{2,1,0:T(8,128)} %part_ref.1, s32[512,128]{1,0:T(8,128)} %idx_ref.1), custom_call_target="tpu_custom_call" | custom-call | tf_op jit(solution)/shard_map/pack/pallas_call | solution.py:89
  9.3 61.4 %gather_tiles.1 = (f32[11008,128]{1,0:T(8,128)}, f32[5120,128]{1,0:T(8,128)}, s32[32,128]{1,0:T(8,128)}, f32[32,128]{1,0:T(8,128)}, bf16[512,128]{1,0:T(8,128)(2,1)}) custom-call(f32[10760,128]{1,0:T(8,128)} %get-tuple-element.16.in_ref, f32[16,512,128]{2,1,0:T(8,128)} %att_hbm.3, f32[512,128]{1,0:T(8,128)} %w_ref.3, s32[1,512]{1,0:T(1,128)} %bitcast.2, ...), custom_call_target="tpu_custom_call" | custom-call | tf_op jit(solution)/shard_map/gather_tiles/pallas_call | solution.py:344
  70.6 60.1 %apply_updates.1 = (f32[512,128]{1,0:T(8,128)}, f32[4,512]{1,0:T(4,128)}, f32[648,128]{1,0:T(8,128)}) custom-call(s32[32,128]{1,0:T(8,128)} %get-tuple-element.17.pix_ref, s32[512]{0:T(512)} %get-tuple-element.18.where_ref, s32[1]{0:T(128)} %bitcast.1.first_ref, f32[5120,128]{1,0:T(8,128)} %get-tuple-element.19.normals_hbm, ...), custom_call_target="tpu_custom_call" | custom-call | tf_op jit(solution)/shard_map/apply_updates/pallas_call | solution.py:676
  130.7 2.0 %emit.1 = (f32[512,128]{1,0:T(8,128)}, f32[4,512]{1,0:T(4,128)}, f32[5,16384]{1,0:T(8,128)}) custom-call(f32[512,128]{1,0:T(8,128)} %get-tuple-element.23.final_ref, f32[4,512]{1,0:T(4,128)} %get-tuple-element.24.attitude_ref, f32[648,128]{1,0:T(8,128)} %get-tuple-element.25.table_ref), custom_call_target="tpu_custom_call" | custom-call | tf_op jit(solution)/shard_map/emit/pallas_call | solution.py:724

commit v9 on v8

--- a/solution.py
+++ b/solution.py
@@ -66,8 +66,8 @@
     lax.fori_loop(0, TILES // 8, scale, 0, unroll=4)
 
     def place(g, _):
-        for j in range(8):
-            t = g * 8 + j
+        for j in range(16):
+            t = g * 16 + j
             seat = slot_ref[pixel_ref[t]]
             owner = lax.shift_right_logical(seat, 7)
             rank = count_ref[owner]
@@ -82,7 +82,7 @@
             out_ref[pl.ds(base + 6, 1), :] = stage_ref[6, pl.ds(t, 1), :] + first
         return 0
 
-    lax.fori_loop(0, TILES // 8, place, 0)
+    lax.fori_loop(0, TILES // 16, place, 0)
 
 
 def pack(tile_pixel, pixel_slot, residual, weight, partials, index):
@@ -137,7 +137,8 @@
 OWN = (0, 1, 8, 9)
 CHUNK = 2
 CHUNKS = SLOTS // CHUNK
-STEP = 24
+STEP = 48
+PER = SEATS // STEP
 PITCH = 136
 ROOM = BLOCK_ROWS + 8
 HBM = pl.BlockSpec(memory_space=pltpu.HBM)
@@ -280,7 +281,7 @@
 
         def group(g, _):
             for j in range(0, STEP, 2):
-                start = (chunk * CHUNK + g // 2) * ROOM + (g % 2 * STEP + j) * FIELDS
+                start = (chunk * CHUNK + g // PER) * ROOM + (g % PER * STEP + j) * FIELDS
                 lefts, hits = [], []
                 for i in range(2):
                     v = arr_ref[pl.ds(start + i * FIELDS, 8), :]
@@ -532,9 +533,9 @@
     row = lax.broadcasted_iota(jnp.int32, (8, 128), 0)
 
     def pick(rows_ref, step, _):
-        k, first = (step // 2 + 8) % SLOTS, step % 2 * STEP
-
-        @pl.when(step % (2 * SLOTS // parts) == 0)
+        k, first = (step // PER + 8) % SLOTS, step % PER * STEP
+
+        @pl.when(step % (PER * SLOTS // parts) == 0)
         def _():
             load(k // (SLOTS // parts)).wait()
 
@@ -553,10 +554,10 @@
 
         return 0
 
-    lax.fori_loop(0, 2 * (SLOTS - 8), functools.partial(pick, table_ref), 0)
+    lax.fori_loop(0, PER * (SLOTS - 8), functools.partial(pick, table_ref), 0)
     for i in range(TIMES):
         spread(i).wait()
-    lax.fori_loop(2 * (SLOTS - 8), 2 * SLOTS, functools.partial(pick, second_ref), 0)
+    lax.fori_loop(PER * (SLOTS - 8), PER * SLOTS, functools.partial(pick, second_ref), 0)
     pass_on(7)
     load_att.wait()
 

time: 134 us -> 129 us (0.963)
  Pallas kernels: 132 us -> 127 us
    pallas_call x1, Pallas kernels: 60.1 us -> 56.6 us  [apply_updates(): pl.pallas_call(apply_kernel, out_shape=(jax.ShapeDtypeStruct((TILES, 128)...]
    pallas_call x1, Pallas kernels: 61.4 us -> 59.8 us  [gather_tiles(): pl.pallas_call(gather_kernel, out_shape=(jax.ShapeDtypeStruct((SLOTS * RO...]
where the time goes in v9:
time: 129 us; the launch traced here: 128 us
  Pallas kernels  127 us (98%)
    pallas_call x1, Pallas kernels, gather_tiles(): pl.pallas_call(gather_kernel, out_shape=(jax.ShapeDtypeStruct((SLOTS * RO...  59.8 us
    pallas_call x1, Pallas kernels, apply_updates(): pl.pallas_call(apply_kernel, out_shape=(jax.ShapeDtypeStruct((TILES, 128)...  56.6 us
    pallas_call x1, Pallas kernels, pack(): pl.pallas_call(pack_kernel, out_shape=(jax.ShapeDtypeStruct((ROWS_IN, 128...  8.52 us

profile of v9, /device:TPU:8, one launch (start us, length us, event | category | flops | bytes accessed | tf_op | source)
XLA Modules:
  0.0 127.6 jit_solution(14720528804728293341)
XLA Ops:
  0.6 8.5 %pack.1 = (f32[10760,128]{1,0:T(8,128)}, s32[512]{0:T(512)}) custom-call(s32[512]{0:T(512)} %pixel_ref.1, s32[2048]{0:T(1024)} %slot_ref.1, f32[512,128]{1,0:T(8,128)} %res_ref.1, f32[512,128]{1,0:T(8,128)} %w_ref.3, f32[5,512,128]{2,1,0:T(8,128)} %part_ref.1, s32[512,128]{1,0:T(8,128)} %idx_ref.1), custom_call_target="tpu_custom_call" | custom-call | tf_op jit(solution)/shard_map/pack/pallas_call | solution.py:89
  9.2 59.8 %gather_tiles.1 = (f32[11008,128]{1,0:T(8,128)}, f32[5120,128]{1,0:T(8,128)}, s32[32,128]{1,0:T(8,128)}, f32[32,128]{1,0:T(8,128)}, bf16[512,128]{1,0:T(8,128)(2,1)}) custom-call(f32[10760,128]{1,0:T(8,128)} %get-tuple-element.16.in_ref, f32[16,512,128]{2,1,0:T(8,128)} %att_hbm.3, f32[512,128]{1,0:T(8,128)} %w_ref.3, s32[1,512]{1,0:T(1,128)} %bitcast.2, ...), custom_call_target="tpu_custom_call" | custom-call | tf_op jit(solution)/shard_map/gather_tiles/pallas_call | solution.py:345
  69.0 56.6 %apply_updates.1 = (f32[512,128]{1,0:T(8,128)}, f32[4,512]{1,0:T(4,128)}, f32[648,128]{1,0:T(8,128)}) custom-call(s32[32,128]{1,0:T(8,128)} %get-tuple-element.17.pix_ref, s32[512]{0:T(512)} %get-tuple-element.18.where_ref, s32[1]{0:T(128)} %bitcast.1.first_ref, f32[5120,128]{1,0:T(8,128)} %get-tuple-element.19.normals_hbm, ...), custom_call_target="tpu_custom_call" | custom-call | tf_op jit(solution)/shard_map/apply_updates/pallas_call | solution.py:677
  125.6 2.0 %emit.1 = (f32[512,128]{1,0:T(8,128)}, f32[4,512]{1,0:T(4,128)}, f32[5,16384]{1,0:T(8,128)}) custom-call(f32[512,128]{1,0:T(8,128)} %get-tuple-element.23.final_ref, f32[4,512]{1,0:T(4,128)} %get-tuple-element.24.attitude_ref, f32[648,128]{1,0:T(8,128)} %get-tuple-element.25.table_ref), custom_call_target="tpu_custom_call" | custom-call | tf_op jit(solution)/shard_map/emit/pallas_call | solution.py:725

commit v10 on v9

--- a/solution.py
+++ b/solution.py
@@ -298,7 +298,8 @@
                         spread_ref[pl.ds(8 * n * PITCH + g * STEP + j + i, 8, stride=PITCH), :] = both[8 * n:8 * n + 8]
             return 0
 
-        lax.fori_loop(0, CHUNK * SEATS // STEP, group, 0)
+        for g in range(CHUNK * SEATS // STEP):
+            group(g, 0)
         places = []
         for i in range(CHUNK):
             k = chunk * CHUNK + i
@@ -571,12 +572,12 @@
     lax.fori_loop(0, SLOTS, settle, 0)
 
     def fetch(g, _):
-        for j in range(16):
-            t = g * 16 + j
+        for j in range(32):
+            t = g * 32 + j
             settled_ref[pl.ds(t, 1), :] = back_ref[pl.ds(where_ref[t], 1), :]
         return 0
 
-    lax.fori_loop(0, TILES // 16, fetch, 0)
+    lax.fori_loop(0, TILES // 32, fetch, 0)
     weight = w_ref[...]
     settled = settled_ref[...] / jnp.sqrt(weight)
     settled_ref[...] = settled

time: 129 us -> 128 us (level)
  no operation moved by 1% of the time
where the time goes in v10:
time: 128 us; the launch traced here: 126 us
  Pallas kernels  126 us (98%)
    pallas_call x1, Pallas kernels, gather_tiles(): pl.pallas_call(gather_kernel, out_shape=(jax.ShapeDtypeStruct((SLOTS * RO...  58.8 us
    pallas_call x1, Pallas kernels, apply_updates(): pl.pallas_call(apply_kernel, out_shape=(jax.ShapeDtypeStruct((TILES, 128)...  56.5 us
    pallas_call x1, Pallas kernels, pack(): pl.pallas_call(pack_kernel, out_shape=(jax.ShapeDtypeStruct((ROWS_IN, 128...  8.52 us

profile of v10, /device:TPU:8, one launch (start us, length us, event | category | flops | bytes accessed | tf_op | source)
XLA Modules:
  0.0 126.5 jit_solution(16867286123493336749)
XLA Ops:
  0.6 8.5 %pack.1 = (f32[10760,128]{1,0:T(8,128)}, s32[512]{0:T(512)}) custom-call(s32[512]{0:T(512)} %pixel_ref.1, s32[2048]{0:T(1024)} %slot_ref.1, f32[512,128]{1,0:T(8,128)} %res_ref.1, f32[512,128]{1,0:T(8,128)} %w_ref.3, f32[5,512,128]{2,1,0:T(8,128)} %part_ref.1, s32[512,128]{1,0:T(8,128)} %idx_ref.1), custom_call_target="tpu_custom_call" | custom-call | tf_op jit(solution)/shard_map/pack/pallas_call | solution.py:89
  9.2 58.8 %gather_tiles.1 = (f32[11008,128]{1,0:T(8,128)}, f32[5120,128]{1,0:T(8,128)}, s32[32,128]{1,0:T(8,128)}, f32[32,128]{1,0:T(8,128)}, bf16[512,128]{1,0:T(8,128)(2,1)}) custom-call(f32[10760,128]{1,0:T(8,128)} %get-tuple-element.16.in_ref, f32[16,512,128]{2,1,0:T(8,128)} %att_hbm.3, f32[512,128]{1,0:T(8,128)} %w_ref.3, s32[1,512]{1,0:T(1,128)} %bitcast.2, ...), custom_call_target="tpu_custom_call" | custom-call | tf_op jit(solution)/shard_map/gather_tiles/pallas_call | solution.py:346
  68.0 56.5 %apply_updates.1 = (f32[512,128]{1,0:T(8,128)}, f32[4,512]{1,0:T(4,128)}, f32[648,128]{1,0:T(8,128)}) custom-call(s32[32,128]{1,0:T(8,128)} %get-tuple-element.17.pix_ref, s32[512]{0:T(512)} %get-tuple-element.18.where_ref, s32[1]{0:T(128)} %bitcast.1.first_ref, f32[5120,128]{1,0:T(8,128)} %get-tuple-element.19.normals_hbm, ...), custom_call_target="tpu_custom_call" | custom-call | tf_op jit(solution)/shard_map/apply_updates/pallas_call | solution.py:678
  124.5 2.0 %emit.1 = (f32[512,128]{1,0:T(8,128)}, f32[4,512]{1,0:T(4,128)}, f32[5,16384]{1,0:T(8,128)}) custom-call(f32[512,128]{1,0:T(8,128)} %get-tuple-element.23.final_ref, f32[4,512]{1,0:T(4,128)} %get-tuple-element.24.attitude_ref, f32[648,128]{1,0:T(8,128)} %get-tuple-element.25.table_ref), custom_call_target="tpu_custom_call" | custom-call | tf_op jit(solution)/shard_map/emit/pallas_call | solution.py:726
